TPU v7x, 32 devices: a whole 2x2x4 slice. The times are simulated.
32 devices in a mesh: dp: 4 (over y, x), expert: 8 (over z, core).
Axes of the slice: x: 2, y: 2, z: 4, core: 2. Of those that a mesh axis runs over, the one named last changes fastest.
Arguments:
- master: float32 [2, 32, 64, 2880], P(None, 'expert', 'dp'), may hold values from -6 to 6
- moment_one: float32 [2, 32, 64, 2880], P(None, 'expert', 'dp'), may hold values from -1.2 to 1.2
- moment_two: float32 [2, 32, 64, 2880], P(None, 'expert', 'dp'), may hold values from 0.0005 to 0.5
- gradient: bfloat16 [2, 32, 64, 2880], P(None, 'expert', 'dp'), may hold values from -150000 to 150000
- old_slot: int32 [2, 32], replicated, may hold values from 0 to 31, as said below
- new_slot: int32 [2, 32], replicated, may hold values from 0 to 31, as said below
Outputs:
- new_master: float32 [2, 32, 64, 2880], P(None, 'expert', 'dp')
- new_moment_one: float32 [2, 32, 64, 2880], P(None, 'expert', 'dp')
- new_moment_two: float32 [2, 32, 64, 2880], P(None, 'expert', 'dp')
Inputs may be any that keep to these rules, and one draw needn't show every extreme that they name: `old_slot`: for each layer a permutation of 0 to 31; global slot s is held by index s // 4 of expert. `new_slot`: for each layer a permutation of 0 to 31; in each layer exactly 1 slot of each index of expert receives another expert than it held, and exactly 1 of the experts held by each index leaves its slot; all other experts keep their slot.
All inputs are finite; a program needn't handle non-finite values.
Results may differ from a plain program's by a relative error of at most 0.001.
Values sent between devices are 32-bit elements; how exact they have to be, the bound alone decides.
No kernel may reach another device: no remote copies, remote signals or barrier semaphores. Data moves between devices by JAX's collectives and lax.ppermute only.
A program may use at most 64 MiB of HBM per device.

v0:
```python
import functools
import math

import jax
import jax.numpy as jnp
from jax import lax
from jax.experimental import pallas as pl
from jax.experimental.pallas import tpu as pltpu
from jax.sharding import PartitionSpec as P


BETA_ONE = 0.9
BETA_TWO = 0.95
LEARN_RATE = 0.05
DECAY_RATE = 0.1
ADAM_EPS = 1e-08
CLIP_RMS = 2.0
FIRST_FIX = 1.0 - 0.9**10
SECOND_FIX = 1.0 - 0.95**10

LANES = 128
CORES = 2
EARLY = 0.5

ANY = pl.BlockSpec(memory_space=pl.ANY)
SMEM = pl.BlockSpec(memory_space=pltpu.SMEM)
VMEM = pl.BlockSpec(memory_space=pltpu.VMEM)


def out(*shape, dtype=jnp.float32):
    return pltpu.VMEM(shape, dtype)


def near(arrays):
    return [pltpu.with_memory_space_constraint(a, pltpu.VMEM) for a in arrays]


def up(n):
    return -(-n // LANES) * LANES


def moments(moment_one, moment_two, gradient, clip_scale):
    scaled = gradient * clip_scale
    first = BETA_ONE * moment_one + (1.0 - BETA_ONE) * scaled
    second = BETA_TWO * moment_two + (1.0 - BETA_TWO) * scaled * scaled
    return first, second


def new_weights(master, first, second):
    step_dir = first / FIRST_FIX / (jnp.sqrt(second / SECOND_FIX) + ADAM_EPS)
    return master - LEARN_RATE * (step_dir + DECAY_RATE * master)


class Sizes:
    def __init__(self, shape, group, dp):
        self.layers, self.slots, self.rows, self.cols = shape
        self.group = group
        self.devices = group * dp
        self.chips = group // CORES
        self.piece = self.layers * self.rows // self.chips
        self.per_layer = self.rows // self.piece
        early = up(int(self.cols * EARLY)) - LANES
        self.early = early
        self.late = self.cols - early
        self.lat = up(self.late)
        self.full = up(self.cols)
        self.w_one = self.full + 3 * early
        self.w_two = self.full + 2 * early
        self.w_late = 2 * self.lat


def peer(i, x, n):
    return i ^ x if n & (n - 1) == 0 else (i + x) % n


def dyn_peer(i, x, n):
    return i ^ x if n & (n - 1) == 0 else lax.rem(i + x, n)


def prep_kernel(sz, me_ref, old_ref, new_ref, master, mone, mtwo, grad, *rest):
    c = sz.chips
    pieces = rest[:c]
    late_raw, plan = rest[c : c + 2]
    mv, m1v, m2v, gv, st, sem = rest[c + 2 :]
    me = me_ref[0]
    chip = lax.div(me, CORES)
    n_slots = sz.layers * sz.group

    for i in range(sz.layers):
        def note(e, carry):
            o = old_ref[i, e]
            n = new_ref[i, e]
            place = jnp.where(o != n, i * sz.group + lax.div(n, sz.slots), n_slots)
            plan[0, place] = lax.div(o, sz.slots)
            plan[1, place] = lax.rem(n, sz.slots)
            return carry

        lax.fori_loop(0, old_ref.shape[1], note, 0, unroll=8)
        slot = plan[1, i * sz.group + me]
        for a, (src, dst) in enumerate(((master, mv), (mone, m1v), (mtwo, m2v), (grad, gv))):
            pltpu.make_async_copy(src.at[i, slot], dst.at[i], sem.at[i, a]).start()
    for i in range(sz.layers):
        for a, (src, dst) in enumerate(((master, mv), (mone, m1v), (mtwo, m2v), (grad, gv))):
            pltpu.make_async_copy(src.at[i, 0], dst.at[i], sem.at[i, a]).wait()
        g = gv[i].astype(jnp.float32)
        for q in range(sz.per_layer):
            k = i * sz.per_layer + q
            r = slice(q * sz.piece, (q + 1) * sz.piece)
            st[0, k] = mv[i, r, :]
            st[1, k] = m1v[i, r, :]
            st[2, k] = m2v[i, r, :]
            st[3, k] = g[r, :]
    for x in range(c):
        k = dyn_peer(chip, x, c)
        pieces[x][:, : sz.cols] = st[0, k]
        for a in range(3):
            lo = sz.full + a * sz.early
            pieces[x][:, lo : lo + sz.early] = st[a + 1, k, :, : sz.early]
            late_raw[a, x] = st[a + 1, k, :, sz.early :]


def prep(sz, me, old_slot, new_slot, master, mone, mtwo, grad):
    f32 = jnp.float32
    slot = (sz.layers, sz.rows, sz.cols)
    outs = [out(sz.piece, sz.w_one)] * sz.chips + [
        out(3, sz.chips, sz.piece, sz.late),
        jax.ShapeDtypeStruct((2, sz.layers * sz.group + 1), jnp.int32),
    ]
    return pl.pallas_call(
        functools.partial(prep_kernel, sz),
        in_specs=[SMEM, SMEM, SMEM, ANY, ANY, ANY, ANY],
        out_specs=[VMEM] * (sz.chips + 1) + [SMEM],
        out_shape=outs,
        scratch_shapes=[
            pltpu.VMEM(slot, f32),
            pltpu.VMEM(slot, f32),
            pltpu.VMEM(slot, f32),
            pltpu.VMEM(slot, grad.dtype),
            pltpu.VMEM((4, sz.chips, sz.piece, sz.cols), f32),
            pltpu.SemaphoreType.DMA((sz.layers, 4)),
        ],
        name="prep",
    )(me, old_slot, new_slot, master, mone, mtwo, grad)


def square_kernel(sz, grad, total, gv, sem):
    copies = [pltpu.make_async_copy(grad.at[i], gv.at[i], sem.at[i]) for i in range(sz.layers)]
    for cp in copies:
        cp.start()
    acc = jnp.zeros((sz.rows, sz.cols), jnp.float32)
    for i in range(sz.layers):
        copies[i].wait()
        for s in range(sz.slots):
            x = gv[i, s].astype(jnp.float32)
            acc = acc + x * x
    total[...] = jnp.broadcast_to(jnp.sum(acc), total.shape)


def squares(sz, grad):
    return pl.pallas_call(
        functools.partial(square_kernel, sz),
        in_specs=[ANY],
        out_specs=VMEM,
        out_shape=out(sz.devices, LANES),
        scratch_shapes=[
            pltpu.VMEM(grad.shape, grad.dtype),
            pltpu.SemaphoreType.DMA((sz.layers,)),
        ],
        name="squares",
    )(grad)


def scale_kernel(sz, total, raw, clip, *late):
    entries = sz.layers * sz.slots * sz.rows * sz.cols * sz.devices
    square_sum = jnp.sum(total[:, 0:1])
    root = jnp.sqrt(jnp.full((1, LANES), square_sum, jnp.float32))
    scale = jnp.minimum(1.0, CLIP_RMS * math.sqrt(entries) / (root + 1e-06))
    clip[...] = scale
    for x in range(sz.chips):
        first, second = moments(raw[0, x], raw[1, x], raw[2, x], scale[:, 0:1])
        late[x][:, : sz.late] = first
        late[x][:, sz.lat : sz.lat + sz.late] = second


def scale_and_late(sz, total, raw):
    return pl.pallas_call(
        functools.partial(scale_kernel, sz),
        in_specs=[VMEM, VMEM],
        out_specs=[VMEM] * (sz.chips + 1),
        out_shape=[out(1, LANES)] + [out(sz.piece, sz.w_late)] * sz.chips,
        name="scale_late",
    )(*near((total, raw)))


def pick_kernel(sz, early, me_ref, plan, *rest):
    c = sz.chips
    if early:
        clip, rest = rest[0], rest[1:]
    refs = rest[: 2 * c]
    outs = rest[2 * c : 3 * c]
    me = me_ref[0]
    chip = lax.div(me, CORES)
    core = lax.rem(me, CORES)
    layer = lax.div(chip, sz.per_layer)
    for x in range(c):
        target = dyn_peer(chip, x, c) * CORES + core
        sender = plan[0, layer * sz.group + target]
        from_chip = lax.div(sender, CORES)
        shift = from_chip ^ chip if c & (c - 1) == 0 else lax.rem(chip - from_chip + c, c)
        choice = shift + jnp.where(lax.rem(sender, CORES) == core, 0, c)
        for q in range(2 * c):
            @pl.when(choice == q)
            def _():
                if not early:
                    outs[x][...] = refs[q][...]
                    return
                at = [sz.full + a * sz.early for a in range(3)]
                parts = [refs[q][:, lo : lo + sz.early] for lo in at]
                first, second = moments(*parts, clip[:, 0:1])
                outs[x][:, : sz.full] = refs[q][:, : sz.full]
                outs[x][:, at[0] : at[0] + sz.early] = first
                outs[x][:, at[1] : at[1] + sz.early] = second


def pick(sz, early, me, plan, clip, own, other):
    c = sz.chips
    width = sz.w_two if early else sz.w_late
    vectors = ([clip] if early else []) + own + other
    return pl.pallas_call(
        functools.partial(pick_kernel, sz, early),
        in_specs=[SMEM, SMEM] + [VMEM] * len(vectors),
        out_specs=[VMEM] * c,
        out_shape=[out(sz.piece, width)] * c,
        name="pick_early" if early else "pick_late",
    )(me, plan, *vectors)


def land_kernel(sz, me_ref, plan, *rest):
    c = sz.chips
    early, late = rest[:c], rest[c : 2 * c]
    outs = rest[2 * c + 3 : 2 * c + 6]
    st, full, sem = rest[2 * c + 6 :]
    me = me_ref[0]
    chip = lax.div(me, CORES)
    e, f = sz.early, sz.full
    for x in range(c):
        k = dyn_peer(chip, x, c) if c & (c - 1) == 0 else lax.rem(chip - x + c, c)
        a, b = early[x], late[x]
        first, second = a[:, f : f + e], a[:, f + e : f + 2 * e]
        st[0, k, :, :e] = new_weights(a[:, :e], first, second)
        st[1, k, :, :e] = first
        st[2, k, :, :e] = second
        first, second = b[:, : sz.late], b[:, sz.lat : sz.lat + sz.late]
        st[0, k, :, e:] = new_weights(a[:, e : sz.cols], first, second)
        st[1, k, :, e:] = first
        st[2, k, :, e:] = second
    copies = []
    for i in range(sz.layers):
        slot = plan[1, i * sz.group + me]
        for a in range(3):
            for q in range(sz.per_layer):
                r = slice(q * sz.piece, (q + 1) * sz.piece)
                full[a, i, r, :] = st[a, i * sz.per_layer + q]
            cp = pltpu.make_async_copy(full.at[a, i], outs[a].at[i, slot], sem.at[a, i])
            cp.start()
            copies.append(cp)
    for cp in copies:
        cp.wait()


def land(sz, me, plan, early, late, outs):
    f32 = jnp.float32
    c = sz.chips
    return pl.pallas_call(
        functools.partial(land_kernel, sz),
        in_specs=[SMEM, SMEM] + [VMEM] * (2 * c) + [ANY] * 3,
        out_specs=[ANY] * 3,
        out_shape=[jax.ShapeDtypeStruct(o.shape, o.dtype) for o in outs],
        scratch_shapes=[
            pltpu.VMEM((3, c, sz.piece, sz.cols), f32),
            pltpu.VMEM((3, sz.layers, sz.rows, sz.cols), f32),
            pltpu.SemaphoreType.DMA((3, sz.layers)),
        ],
        input_output_aliases={2 + 2 * c + a: a for a in range(3)},
        name="land",
    )(me, plan, *early, *late, *outs)


def spread(sz, arrays):
    c = sz.chips
    got = [arrays[0]]
    for x in range(1, c):
        pairs = [
            (i * CORES + k, peer(i, x, c) * CORES + k) for i in range(c) for k in range(CORES)
        ]
        got.append(lax.ppermute(arrays[x], "expert", pairs))
    return got[:1] + near(got[1:])


def swap(sz, arrays):
    pairs = [(i, i ^ 1) for i in range(sz.group)]
    return near([lax.ppermute(a, "expert", pairs) for a in arrays])


def shards(master, moment_one, moment_two, gradient, old_slot, new_slot):
    sz = Sizes(master.shape, lax.axis_size("expert"), lax.axis_size("dp"))
    me = lax.axis_index("expert").reshape(1)
    c = sz.chips
    got = prep(sz, me, old_slot, new_slot, master, moment_one, moment_two, gradient)
    pieces, raw, plan = list(got[:c]), got[c], got[c + 1]
    held = spread(sz, pieces)
    partial = squares(sz, gradient)
    sums = lax.all_to_all(partial, ("dp", "expert"), 0, 0, tiled=True)
    clip, *late = scale_and_late(sz, sums, raw)
    late_held = spread(sz, late)
    other = swap(sz, held)
    early_out = pick(sz, True, me, plan, clip, held, other)
    early_in = spread(sz, list(early_out))
    late_other = swap(sz, late_held)
    late_out = pick(sz, False, me, plan, None, late_held, late_other)
    late_in = spread(sz, list(late_out))
    scale = clip[0, 0]
    wide = gradient.astype(jnp.float32)
    first, second = moments(moment_one, moment_two, wide, scale)
    weights = new_weights(master, first, second)
    return tuple(land(sz, me, plan, early_in, late_in, (weights, first, second)))


def solution(mesh):
    spec = P(None, "expert", "dp", None)
    return jax.shard_map(
        shards,
        mesh=mesh,
        in_specs=(spec, spec, spec, spec, P(), P()),
        out_specs=(spec, spec, spec),
        check_vma=False,
    )
```

profile of v0, /device:TPU:12, one launch (start us, length us, event | category | flops | bytes accessed | tf_op | source)
XLA Modules:
  0.0 83.4 jit_solution(10657131986976533040)
XLA Ops:
  0.6 1.9 %squares.1 = f32[32,128]{1,0:T(8,128)} custom-call(bf16[2,4,16,2880]{3,2,1,0:T(8,128)(2,1)} %grad.3), custom_call_target="tpu_custom_call" | custom-call | tf_op jit(solution)/shard_map/squares/pallas_call | solution.py:160
  2.6 6.0 %all-to-all-start = ((f32[32,1,128]{2,1,0:T(1,128)}), f32[32,1,128]{2,1,0:T(1,128)S(1)}, u32[]{:S(2)}, u32[]{:S(2)}) async-start(f32[32,1,128]{2,1,0:T(1,128)} %bitcast.2), calls=%async_computation | async-start | bytes 32768 | tf_op jit(solution)/shard_map/all_to_all | solution.py:313
  8.6 3.4 %prep.1 = (f32[8,7168]{1,0:T(8,128)S(1)}, f32[8,7168]{1,0:T(8,128)}, f32[8,7168]{1,0:T(8,128)}, f32[8,7168]{1,0:T(8,128)S(1)}, f32[3,4,8,1472]{3,2,1,0:T(8,128)S(1)}, /*index=5*/s32[2,17]{1,0:T(2,128)}) custom-call(s32[1]{0:T(128)} %bitcast.me_ref, s32[2,32]{1,0:T(2,128)} %old_ref.1, s32[2,32]{1,0:T(2,128)} %new_ref.1, f32[2,4,16,2880]{3,2,1,0:T(8,128)} %master.1, ...), custom_call_target="tpu_custom_call" | custom-call | tf_op jit(solution)/shard_map/prep/pallas_call | solution.py:129
  12.0 1.7 %all-to-all-done = f32[32,1,128]{2,1,0:T(1,128)S(1)} async-done(((f32[32,1,128]{2,1,0:T(1,128)}), f32[32,1,128]{2,1,0:T(1,128)S(1)}, u32[]{:S(2)}, u32[]{:S(2)}) %all-to-all-start) | async-done | bytes 16416 | tf_op jit(solution)/shard_map/all_to_all | solution.py:313
  13.8 1.6 %collective-permute-start.10 = (f32[8,3072]{1,0:T(8,128)S(1)}, f32[8,3072]{1,0:T(8,128)S(1)}, u32[]{:S(2)}, u32[]{:S(2)}) collective-permute-start(f32[8,3072]{1,0:T(8,128)S(1)} %get-tuple-element.34), channel_id=1, source_target_pairs={{0,2},{1,3},{2,0},{3,1},{4,6},{5,7},{6,4},{7,5},{8,10},{9,11},{10,... | collective-permute-start | bytes 294920 | tf_op jit(solution)/shard_map/ppermute | solution.py:296
  15.9 0.8 collective-permute-start
  16.7 2.1 %collective-permute-start.1 = (f32[8,7168]{1,0:T(8,128)}, f32[8,7168]{1,0:T(8,128)S(1)}, u32[]{:S(2)}, u32[]{:S(2)}) collective-permute-start(f32[8,7168]{1,0:T(8,128)} %get-tuple-element.27), channel_id=1, source_target_pairs={{0,4},{1,5},{2,6},{3,7},{4,0},{5,1},{6,2},{7,3},{8,12},{9,13},{10,... | collective-permute-start | bytes 688136 | tf_op jit(solution)/shard_map/ppermute | solution.py:296
  20.9 1.1 %collective-permute-done.11.rest_2_ = f32[8,3072]{1,0:T(8,128)S(1)} collective-permute-done((f32[8,3072]{1,0:T(8,128)S(1)}, f32[8,3072]{1,0:T(8,128)S(1)}, u32[]{:S(2)}, u32[]{:S(2)}) %collective-permute-start.11) | collective-permute-done | bytes 98336 | tf_op jit(solution)/shard_map/ppermute | solution.py:296
  22.0 23.7 %collective-permute-done.12.rest_3_ = f32[8,3072]{1,0:T(8,128)S(1)} collective-permute-done((f32[8,3072]{1,0:T(8,128)S(1)}, f32[8,3072]{1,0:T(8,128)S(1)}, u32[]{:S(2)}, u32[]{:S(2)}) %collective-permute-start.12) | collective-permute-done | bytes 98336 | tf_op jit(solution)/shard_map/ppermute | solution.py:296
  48.2 1.4 %collective-permute-done.16.rest_7_ = f32[8,3072]{1,0:T(8,128)S(1)} collective-permute-done((f32[8,3072]{1,0:T(8,128)S(1)}, f32[8,3072]{1,0:T(8,128)S(1)}, u32[]{:S(2)}, u32[]{:S(2)}) %collective-permute-start.16) | collective-permute-done | bytes 98336 | tf_op jit(solution)/shard_map/ppermute | solution.py:302
  49.6 1.8 %pick_late.1 = (f32[8,3072]{1,0:T(8,128)S(1)}, f32[8,3072]{1,0:T(8,128)}, f32[8,3072]{1,0:T(8,128)}, f32[8,3072]{1,0:T(8,128)}) custom-call(s32[1]{0:T(128)} %bitcast.me_ref, s32[2,17]{1,0:T(2,128)} %get-tuple-element.22.plan, f32[8,3072]{1,0:T(8,128)} %copy-done.8, f32[8,3072]{1,0:T(8,128)S(1)} %collective-permute-done.10.rest_1_, ...), custom_call_target="tpu_custom_call" | custom-call | tf_op jit(solution)/shard_map/pick_late/pallas_call | solution.py:229
  52.0 2.0 %collective-permute-start.18 = (f32[8,3072]{1,0:T(8,128)}, f32[8,3072]{1,0:T(8,128)}, u32[]{:S(2)}, u32[]{:S(2)}) collective-permute-start(f32[8,3072]{1,0:T(8,128)} %get-tuple-element.39), channel_id=1, source_target_pairs={{0,4},{1,5},{2,6},{3,7},{4,0},{5,1},{6,2},{7,3},{8,12},{9,13},{10,... | collective-permute-start | bytes 294920 | tf_op jit(solution)/shard_map/ppermute | solution.py:296
  54.7 1.5 %collective-permute-start.19 = (f32[8,3072]{1,0:T(8,128)}, f32[8,3072]{1,0:T(8,128)S(1)}, u32[]{:S(2)}, u32[]{:S(2)}) collective-permute-start(f32[8,3072]{1,0:T(8,128)} %get-tuple-element.40), channel_id=1, source_target_pairs={{0,6},{1,7},{2,4},{3,5},{4,2},{5,3},{6,0},{7,1},{8,14},{9,15},{10,... | collective-permute-start | bytes 294920 | tf_op jit(solution)/shard_map/ppermute | solution.py:296
  57.6 0.9 %copy-done.2 = f32[8,7168]{1,0:T(8,128)S(1)} copy-done((f32[8,7168]{1,0:T(8,128)S(1)}, f32[8,7168]{1,0:T(8,128)}, u32[]{:S(2)}) %copy-start.2) | copy-done | bytes 229400
  58.5 0.9 %copy-done.4 = f32[8,7168]{1,0:T(8,128)S(1)} copy-done((f32[8,7168]{1,0:T(8,128)S(1)}, f32[8,7168]{1,0:T(8,128)}, u32[]{:S(2)}) %copy-start.4) | copy-done | bytes 229400
  59.5 0.9 %copy-done.6 = f32[8,7168]{1,0:T(8,128)S(1)} copy-done((f32[8,7168]{1,0:T(8,128)S(1)}, f32[8,7168]{1,0:T(8,128)}, u32[]{:S(2)}) %copy-start.6) | copy-done | bytes 229400
  60.4 1.5 %pick_early.1 = (f32[8,5760]{1,0:T(8,128)S(1)}, f32[8,5760]{1,0:T(8,128)S(1)}, f32[8,5760]{1,0:T(8,128)S(1)}, f32[8,5760]{1,0:T(8,128)S(1)}) custom-call(s32[1]{0:T(128)} %bitcast.me_ref, s32[2,17]{1,0:T(2,128)} %get-tuple-element.22.plan, f32[1,128]{1,0:T(1,128)} %copy-done.10, f32[8,7168]{1,0:T(8,128)} %copy-done, ...), custom_call_target="tpu_custom_call" | custom-call | tf_op jit(solution)/shard_map/pick_early/pallas_call | solution.py:229
  61.9 1.0 %collective-permute-start.7 = (f32[8,5760]{1,0:T(8,128)S(1)}, f32[8,5760]{1,0:T(8,128)S(1)}, u32[]{:S(2)}, u32[]{:S(2)}) collective-permute-start(f32[8,5760]{1,0:T(8,128)S(1)} %get-tuple-element.30), channel_id=1, source_target_pairs={{0,2},{1,3},{2,0},{3,1},{4,6},{5,7},{6,4},{7,5},{8,10},{9,11},{10,... | collective-permute-start | bytes 552968 | tf_op jit(solution)/shard_map/ppermute | solution.py:296
  62.9 1.1 %collective-permute-start.8 = (f32[8,5760]{1,0:T(8,128)S(1)}, f32[8,5760]{1,0:T(8,128)S(1)}, u32[]{:S(2)}, u32[]{:S(2)}) collective-permute-start(f32[8,5760]{1,0:T(8,128)S(1)} %get-tuple-element.31), channel_id=1, source_target_pairs={{0,4},{1,5},{2,6},{3,7},{4,0},{5,1},{6,2},{7,3},{8,12},{9,13},{10,... | collective-permute-start | bytes 552968 | tf_op jit(solution)/shard_map/ppermute | solution.py:296
  64.0 1.5 %collective-permute-start.9 = (f32[8,5760]{1,0:T(8,128)S(1)}, f32[8,5760]{1,0:T(8,128)S(1)}, u32[]{:S(2)}, u32[]{:S(2)}) collective-permute-start(f32[8,5760]{1,0:T(8,128)S(1)} %get-tuple-element.32), channel_id=1, source_target_pairs={{0,6},{1,7},{2,4},{3,5},{4,2},{5,3},{6,0},{7,1},{8,14},{9,15},{10,... | collective-permute-start | bytes 552968 | tf_op jit(solution)/shard_map/ppermute | solution.py:296
  65.5 5.2 %multiply_subtract_fusion = (f32[2,4,16,2880]{3,2,1,0:T(8,128)}, f32[2,4,16,2880]{3,2,1,0:T(8,128)}, f32[2,4,16,2880]{3,2,1,0:T(8,128)}) fusion(f32[2,4,16,2880]{3,2,1,0:T(8,128)} %master.1, f32[]{:T(128)S(1)} %bitcast.8, bf16[2,4,16,2880]{3,2,1,0:T(8,128)(2,1)S(1)} %copy-done.12, f32[2,4,16,2880]{3,2,1,0:T(8,128)} %mone.1, f32[2,4,16,2880]{3,2,1,0:T(8,128)} %mtwo.1), kind=kLoop, calls=%fused_computation.2 | loop fusion | flops 6266880 | bytes 9584644 | tf_op jit(solution)/shard_map/sub | solution.py:51
  70.7 6.2 %collective-permute-done.8.rest_2_ = f32[8,5760]{1,0:T(8,128)S(1)} collective-permute-done((f32[8,5760]{1,0:T(8,128)S(1)}, f32[8,5760]{1,0:T(8,128)S(1)}, u32[]{:S(2)}, u32[]{:S(2)}) %collective-permute-start.8) | collective-permute-done | bytes 184352 | tf_op jit(solution)/shard_map/ppermute | solution.py:296
  76.9 4.0 %collective-permute-done.9.rest_3_ = f32[8,5760]{1,0:T(8,128)S(1)} collective-permute-done((f32[8,5760]{1,0:T(8,128)S(1)}, f32[8,5760]{1,0:T(8,128)S(1)}, u32[]{:S(2)}, u32[]{:S(2)}) %collective-permute-start.9) | collective-permute-done | bytes 184352 | tf_op jit(solution)/shard_map/ppermute | solution.py:296
  81.0 2.4 %land.1 = (f32[2,4,16,2880]{3,2,1,0:T(8,128)}, f32[2,4,16,2880]{3,2,1,0:T(8,128)}, f32[2,4,16,2880]{3,2,1,0:T(8,128)}) custom-call(s32[1]{0:T(128)} %bitcast.me_ref, s32[2,17]{1,0:T(2,128)} %get-tuple-element.22.plan, f32[8,5760]{1,0:T(8,128)} %copy-done.7, ...), custom_call_target="tpu_custom_call", output_to_operand_aliasing={{0}: (10, {}), {1}: (11, {}), {2}: (12, {})} | custom-call | tf_op jit(solution)/shard_map/land/pallas_call | solution.py:274
  (51 shorter events, 8.0 us)
Async XLA Ops:
  2.6 11.1 %all-to-all-start = ((f32[32,1,128]{2,1,0:T(1,128)}), f32[32,1,128]{2,1,0:T(1,128)S(1)}, u32[]{:S(2)}, u32[]{:S(2)}) async-start(f32[32,1,128]{2,1,0:T(1,128)} %bitcast.2), calls=%async_computation | async-start | bytes 32768 | tf_op jit(solution)/shard_map/all_to_all | solution.py:313
  12.0 45.6 %copy-start = (f32[8,7168]{1,0:T(8,128)}, f32[8,7168]{1,0:T(8,128)S(1)}, u32[]{:S(2)}) copy-start(f32[8,7168]{1,0:T(8,128)S(1)} %get-tuple-element.25.rest_1_) | copy-start | bytes 688132
  13.8 33.8 %copy-start.10 = (f32[1,128]{1,0:T(1,128)}, f32[1,128]{1,0:T(1,128)S(1)}, u32[]{:S(2)}) copy-start(f32[1,128]{1,0:T(1,128)S(1)} %get-tuple-element.24.rest_0_) | copy-start | bytes 1540
  13.8 35.7 %copy-start.8 = (f32[8,3072]{1,0:T(8,128)}, f32[8,3072]{1,0:T(8,128)S(1)}, u32[]{:S(2)}) copy-start(f32[8,3072]{1,0:T(8,128)S(1)} %get-tuple-element.33.rest_0_) | copy-start | bytes 294916
  13.8 6.3 %collective-permute-start.10 = (f32[8,3072]{1,0:T(8,128)S(1)}, f32[8,3072]{1,0:T(8,128)S(1)}, u32[]{:S(2)}, u32[]{:S(2)}) collective-permute-start(f32[8,3072]{1,0:T(8,128)S(1)} %get-tuple-element.34), channel_id=1, source_target_pairs={{0,2},{1,3},{2,0},{3,1},{4,6},{5,7},{6,4},{7,5},{8,10},{9,11},{10,... | collective-permute-start | bytes 294920 | tf_op jit(solution)/shard_map/ppermute | solution.py:296
  15.4 6.6 %collective-permute-start.11 = (f32[8,3072]{1,0:T(8,128)S(1)}, f32[8,3072]{1,0:T(8,128)S(1)}, u32[]{:S(2)}, u32[]{:S(2)}) collective-permute-start(f32[8,3072]{1,0:T(8,128)S(1)} %get-tuple-element.35), channel_id=1, source_target_pairs={{0,4},{1,5},{2,6},{3,7},{4,0},{5,1},{6,2},{7,3},{8,12},{9,13},{10,... | collective-permute-start | bytes 294920 | tf_op jit(solution)/shard_map/ppermute | solution.py:296
  15.9 31.2 %collective-permute-start = (f32[8,7168]{1,0:T(8,128)}, f32[8,7168]{1,0:T(8,128)S(1)}, u32[]{:S(2)}, u32[]{:S(2)}) collective-permute-start(f32[8,7168]{1,0:T(8,128)} %get-tuple-element.26), channel_id=1, source_target_pairs={{0,2},{1,3},{2,0},{3,1},{4,6},{5,7},{6,4},{7,5},{8,10},{9,11},{10,... | collective-permute-start | bytes 688136 | tf_op jit(solution)/shard_map/ppermute | solution.py:296
  16.7 30.7 %collective-permute-start.1 = (f32[8,7168]{1,0:T(8,128)}, f32[8,7168]{1,0:T(8,128)S(1)}, u32[]{:S(2)}, u32[]{:S(2)}) collective-permute-start(f32[8,7168]{1,0:T(8,128)} %get-tuple-element.27), channel_id=1, source_target_pairs={{0,4},{1,5},{2,6},{3,7},{4,0},{5,1},{6,2},{7,3},{8,12},{9,13},{10,... | collective-permute-start | bytes 688136 | tf_op jit(solution)/shard_map/ppermute | solution.py:296
  18.9 28.8 %collective-permute-start.2 = (f32[8,7168]{1,0:T(8,128)S(1)}, f32[8,7168]{1,0:T(8,128)S(1)}, u32[]{:S(2)}, u32[]{:S(2)}) collective-permute-start(f32[8,7168]{1,0:T(8,128)S(1)} %get-tuple-element.28), channel_id=1, source_target_pairs={{0,6},{1,7},{2,4},{3,5},{4,2},{5,3},{6,0},{7,1},{8,14},{9,15},{10,... | collective-permute-start | bytes 688136 | tf_op jit(solution)/shard_map/ppermute | solution.py:296
  20.1 25.6 %collective-permute-start.12 = (f32[8,3072]{1,0:T(8,128)S(1)}, f32[8,3072]{1,0:T(8,128)S(1)}, u32[]{:S(2)}, u32[]{:S(2)}) collective-permute-start(f32[8,3072]{1,0:T(8,128)S(1)} %get-tuple-element.36), channel_id=1, source_target_pairs={{0,6},{1,7},{2,4},{3,5},{4,2},{5,3},{6,0},{7,1},{8,14},{9,15},{10,... | collective-permute-start | bytes 294920 | tf_op jit(solution)/shard_map/ppermute | solution.py:296
  22.0 23.7 %collective-permute-start.13 = (f32[8,3072]{1,0:T(8,128)S(1)}, f32[8,3072]{1,0:T(8,128)S(1)}, u32[]{:S(2)}, u32[]{:S(2)}) collective-permute-start(f32[8,3072]{1,0:T(8,128)S(1)} %get-tuple-element.33.rest_0_), channel_id=1, source_target_pairs={{0,1},{1,0},{2,3},{3,2},{4,5},{5,4},{6,7},{7,6},{8,9},{9,8},{10,11... | collective-permute-start | bytes 294920 | tf_op jit(solution)/shard_map/ppermute | solution.py:302
  45.6 1.3 %collective-permute-start.14 = (f32[8,3072]{1,0:T(8,128)S(1)}, f32[8,3072]{1,0:T(8,128)S(1)}, u32[]{:S(2)}, u32[]{:S(2)}) collective-permute-start(f32[8,3072]{1,0:T(8,128)S(1)} %collective-permute-done.10.rest_1_), channel_id=1, source_target_pairs={{0,1},{1,0},{2,3},{3,2},{4,5},{5,4},{6,7},{7,6},{8,9},{9,8},{10,11... | collective-permute-start | bytes 294920 | tf_op jit(solution)/shard_map/ppermute | solution.py:302
  45.7 2.4 %collective-permute-start.15 = (f32[8,3072]{1,0:T(8,128)S(1)}, f32[8,3072]{1,0:T(8,128)S(1)}, u32[]{:S(2)}, u32[]{:S(2)}) collective-permute-start(f32[8,3072]{1,0:T(8,128)S(1)} %collective-permute-done.11.rest_2_), channel_id=1, source_target_pairs={{0,1},{1,0},{2,3},{3,2},{4,5},{5,4},{6,7},{7,6},{8,9},{9,8},{10,11... | collective-permute-start | bytes 294920 | tf_op jit(solution)/shard_map/ppermute | solution.py:302
  46.9 5.1 %collective-permute-start.3 = (f32[8,7168]{1,0:T(8,128)S(1)}, f32[8,7168]{1,0:T(8,128)S(1)}, u32[]{:S(2)}, u32[]{:S(2)}) collective-permute-start(f32[8,7168]{1,0:T(8,128)S(1)} %get-tuple-element.25.rest_1_), channel_id=1, source_target_pairs={{0,1},{1,0},{2,3},{3,2},{4,5},{5,4},{6,7},{7,6},{8,9},{9,8},{10,11... | collective-permute-start | bytes 688136 | tf_op jit(solution)/shard_map/ppermute | solution.py:302
  47.1 6.9 %collective-permute-start.4 = (f32[8,7168]{1,0:T(8,128)S(1)}, f32[8,7168]{1,0:T(8,128)S(1)}, u32[]{:S(2)}, u32[]{:S(2)}) collective-permute-start(f32[8,7168]{1,0:T(8,128)S(1)} %collective-permute-done.rest_2_), channel_id=1, source_target_pairs={{0,1},{1,0},{2,3},{3,2},{4,5},{5,4},{6,7},{7,6},{8,9},{9,8},{10,11... | collective-permute-start | bytes 688136 | tf_op jit(solution)/shard_map/ppermute | solution.py:302
  47.5 8.7 %collective-permute-start.5 = (f32[8,7168]{1,0:T(8,128)S(1)}, f32[8,7168]{1,0:T(8,128)S(1)}, u32[]{:S(2)}, u32[]{:S(2)}) collective-permute-start(f32[8,7168]{1,0:T(8,128)S(1)} %collective-permute-done.1.rest_3_), channel_id=1, source_target_pairs={{0,1},{1,0},{2,3},{3,2},{4,5},{5,4},{6,7},{7,6},{8,9},{9,8},{10,11... | collective-permute-start | bytes 688136 | tf_op jit(solution)/shard_map/ppermute | solution.py:302
  47.6 9.3 %collective-permute-start.6 = (f32[8,7168]{1,0:T(8,128)S(1)}, f32[8,7168]{1,0:T(8,128)S(1)}, u32[]{:S(2)}, u32[]{:S(2)}) collective-permute-start(f32[8,7168]{1,0:T(8,128)S(1)} %collective-permute-done.2.rest_4_), channel_id=1, source_target_pairs={{0,1},{1,0},{2,3},{3,2},{4,5},{5,4},{6,7},{7,6},{8,9},{9,8},{10,11... | collective-permute-start | bytes 688136 | tf_op jit(solution)/shard_map/ppermute | solution.py:302
  48.0 1.5 %collective-permute-start.16 = (f32[8,3072]{1,0:T(8,128)S(1)}, f32[8,3072]{1,0:T(8,128)S(1)}, u32[]{:S(2)}, u32[]{:S(2)}) collective-permute-start(f32[8,3072]{1,0:T(8,128)S(1)} %collective-permute-done.12.rest_3_), channel_id=1, source_target_pairs={{0,1},{1,0},{2,3},{3,2},{4,5},{5,4},{6,7},{7,6},{8,9},{9,8},{10,11... | collective-permute-start | bytes 294920 | tf_op jit(solution)/shard_map/ppermute | solution.py:302
  52.0 12.0 %collective-permute-start.17 = (f32[8,3072]{1,0:T(8,128)}, f32[8,3072]{1,0:T(8,128)}, u32[]{:S(2)}, u32[]{:S(2)}) collective-permute-start(f32[8,3072]{1,0:T(8,128)} %get-tuple-element.38), channel_id=1, source_target_pairs={{0,2},{1,3},{2,0},{3,1},{4,6},{5,7},{6,4},{7,5},{8,10},{9,11},{10,... | collective-permute-start | bytes 294920 | tf_op jit(solution)/shard_map/ppermute | solution.py:296
  52.0 18.7 %collective-permute-start.18 = (f32[8,3072]{1,0:T(8,128)}, f32[8,3072]{1,0:T(8,128)}, u32[]{:S(2)}, u32[]{:S(2)}) collective-permute-start(f32[8,3072]{1,0:T(8,128)} %get-tuple-element.39), channel_id=1, source_target_pairs={{0,4},{1,5},{2,6},{3,7},{4,0},{5,1},{6,2},{7,3},{8,12},{9,13},{10,... | collective-permute-start | bytes 294920 | tf_op jit(solution)/shard_map/ppermute | solution.py:296
  54.7 16.0 %collective-permute-start.19 = (f32[8,3072]{1,0:T(8,128)}, f32[8,3072]{1,0:T(8,128)S(1)}, u32[]{:S(2)}, u32[]{:S(2)}) collective-permute-start(f32[8,3072]{1,0:T(8,128)} %get-tuple-element.40), channel_id=1, source_target_pairs={{0,6},{1,7},{2,4},{3,5},{4,2},{5,3},{6,0},{7,1},{8,14},{9,15},{10,... | collective-permute-start | bytes 294920 | tf_op jit(solution)/shard_map/ppermute | solution.py:296
  61.9 8.8 %collective-permute-start.7 = (f32[8,5760]{1,0:T(8,128)S(1)}, f32[8,5760]{1,0:T(8,128)S(1)}, u32[]{:S(2)}, u32[]{:S(2)}) collective-permute-start(f32[8,5760]{1,0:T(8,128)S(1)} %get-tuple-element.30), channel_id=1, source_target_pairs={{0,2},{1,3},{2,0},{3,1},{4,6},{5,7},{6,4},{7,5},{8,10},{9,11},{10,... | collective-permute-start | bytes 552968 | tf_op jit(solution)/shard_map/ppermute | solution.py:296
  62.9 14.0 %collective-permute-start.8 = (f32[8,5760]{1,0:T(8,128)S(1)}, f32[8,5760]{1,0:T(8,128)S(1)}, u32[]{:S(2)}, u32[]{:S(2)}) collective-permute-start(f32[8,5760]{1,0:T(8,128)S(1)} %get-tuple-element.31), channel_id=1, source_target_pairs={{0,4},{1,5},{2,6},{3,7},{4,0},{5,1},{6,2},{7,3},{8,12},{9,13},{10,... | collective-permute-start | bytes 552968 | tf_op jit(solution)/shard_map/ppermute | solution.py:296
  64.0 17.0 %collective-permute-start.9 = (f32[8,5760]{1,0:T(8,128)S(1)}, f32[8,5760]{1,0:T(8,128)S(1)}, u32[]{:S(2)}, u32[]{:S(2)}) collective-permute-start(f32[8,5760]{1,0:T(8,128)S(1)} %get-tuple-element.32), channel_id=1, source_target_pairs={{0,6},{1,7},{2,4},{3,5},{4,2},{5,3},{6,0},{7,1},{8,14},{9,15},{10,... | collective-permute-start | bytes 552968 | tf_op jit(solution)/shard_map/ppermute | solution.py:296
  (10 other events, 37.2 us)
where the time goes:
time: 84.7 us; the launch traced here: 83.4 us
  waiting for transfers between devices  39.5 us (47%)
  starting transfers between devices  21.1 us (25%)
  Pallas kernels  11.2 us (13%)
  local copies, waits for them, and re-layouts  5.52 us (7%)
  other arithmetic  5.22 us (6%)
    ppermute x12, waiting for transfers between devices, spread(): got.append(lax.ppermute(arrays[x], 'expert', pairs))  35.7 us
    ppermute x12, starting transfers between devices, spread(): got.append(lax.ppermute(arrays[x], 'expert', pairs))  13.4 us
    all_to_all x1, starting transfers between devices, shards(): sums = lax.all_to_all(partial, ('dp', 'expert'), 0, 0, tiled=True)  6 us
    unnamed x26, local copies, waits for them, and re-layouts  5.52 us
    sub x1, other arithmetic, new_weights(): return master - LEARN_RATE * (step_dir + DECAY_RATE * master)  5.22 us
    pallas_call x1, Pallas kernels, prep(): pl.pallas_call(functools.partial(prep_kernel, sz), in_specs=[SMEM, SMEM,...  3.38 us
    pallas_call x2, Pallas kernels, pick(): pl.pallas_call(functools.partial(pick_kernel, sz, early), in_specs=[SMEM,...  3.33 us
    pallas_call x1, Pallas kernels, land(): pl.pallas_call(functools.partial(land_kernel, sz), in_specs=[SMEM, SMEM]...  2.42 us
  transfers between devices with their start and end apart: 21, of which 8 were waited for; matrix products, arithmetic and copies ran while one was open for 6% of the time, Pallas kernels for 8%

commit v1 on v0

--- a/solution.py
+++ b/solution.py
@@ -64,9 +64,12 @@
         self.late = self.cols - early
         self.lat = up(self.late)
         self.full = up(self.cols)
-        self.w_one = self.full + 3 * early
-        self.w_two = self.full + 2 * early
-        self.w_late = 2 * self.lat
+        self.groups = ((self.full, 0, early, early), (0, early, self.late, self.lat))
+
+
+def width(group, parts):
+    head, _, _, stride = group
+    return head + parts * stride
 
 
 def peer(i, x, n):
@@ -79,9 +82,8 @@
 
 def prep_kernel(sz, me_ref, old_ref, new_ref, master, mone, mtwo, grad, *rest):
     c = sz.chips
-    pieces = rest[:c]
-    late_raw, plan = rest[c : c + 2]
-    mv, m1v, m2v, gv, st, sem = rest[c + 2 :]
+    pieces = rest[:c], rest[c : 2 * c]
+    plan, mv, m1v, m2v, gv, st, sem = rest[2 * c :]
     me = me_ref[0]
     chip = lax.div(me, CORES)
     n_slots = sz.layers * sz.group
@@ -112,24 +114,22 @@
             st[3, k] = g[r, :]
     for x in range(c):
         k = dyn_peer(chip, x, c)
-        pieces[x][:, : sz.cols] = st[0, k]
-        for a in range(3):
-            lo = sz.full + a * sz.early
-            pieces[x][:, lo : lo + sz.early] = st[a + 1, k, :, : sz.early]
-            late_raw[a, x] = st[a + 1, k, :, sz.early :]
+        pieces[0][x][:, : sz.cols] = st[0, k]
+        for refs, (head, start, size, stride) in zip(pieces, sz.groups):
+            for a in range(3):
+                lo = head + a * stride
+                refs[x][:, lo : lo + size] = st[a + 1, k, :, start : start + size]
 
 
 def prep(sz, me, old_slot, new_slot, master, mone, mtwo, grad):
     f32 = jnp.float32
     slot = (sz.layers, sz.rows, sz.cols)
-    outs = [out(sz.piece, sz.w_one)] * sz.chips + [
-        out(3, sz.chips, sz.piece, sz.late),
-        jax.ShapeDtypeStruct((2, sz.layers * sz.group + 1), jnp.int32),
-    ]
+    outs = [out(sz.piece, width(g, 3)) for g in sz.groups for _ in range(sz.chips)]
+    outs.append(jax.ShapeDtypeStruct((2, sz.layers * sz.group + 1), jnp.int32))
     return pl.pallas_call(
         functools.partial(prep_kernel, sz),
         in_specs=[SMEM, SMEM, SMEM, ANY, ANY, ANY, ANY],
-        out_specs=[VMEM] * (sz.chips + 1) + [SMEM],
+        out_specs=[VMEM] * (2 * sz.chips) + [SMEM],
         out_shape=outs,
         scratch_shapes=[
             pltpu.VMEM(slot, f32),
@@ -161,7 +161,7 @@
         functools.partial(square_kernel, sz),
         in_specs=[ANY],
         out_specs=VMEM,
-        out_shape=out(sz.devices, LANES),
+        out_shape=out(1, LANES),
         scratch_shapes=[
             pltpu.VMEM(grad.shape, grad.dtype),
             pltpu.SemaphoreType.DMA((sz.layers,)),
@@ -170,34 +170,32 @@
     )(grad)
 
 
-def scale_kernel(sz, total, raw, clip, *late):
+def scale_kernel(sz, *refs):
     entries = sz.layers * sz.slots * sz.rows * sz.cols * sz.devices
-    square_sum = jnp.sum(total[:, 0:1])
-    root = jnp.sqrt(jnp.full((1, LANES), square_sum, jnp.float32))
-    scale = jnp.minimum(1.0, CLIP_RMS * math.sqrt(entries) / (root + 1e-06))
-    clip[...] = scale
-    for x in range(sz.chips):
-        first, second = moments(raw[0, x], raw[1, x], raw[2, x], scale[:, 0:1])
-        late[x][:, : sz.late] = first
-        late[x][:, sz.lat : sz.lat + sz.late] = second
-
-
-def scale_and_late(sz, total, raw):
+    square_sum = refs[0][...]
+    for part in refs[1:-1]:
+        square_sum = square_sum + part[...]
+    refs[-1][...] = jnp.minimum(
+        1.0, CLIP_RMS * math.sqrt(entries) / (jnp.sqrt(square_sum) + 1e-06)
+    )
+
+
+def clip_scale(sz, parts):
     return pl.pallas_call(
         functools.partial(scale_kernel, sz),
-        in_specs=[VMEM, VMEM],
-        out_specs=[VMEM] * (sz.chips + 1),
-        out_shape=[out(1, LANES)] + [out(sz.piece, sz.w_late)] * sz.chips,
-        name="scale_late",
-    )(*near((total, raw)))
-
-
-def pick_kernel(sz, early, me_ref, plan, *rest):
-    c = sz.chips
-    if early:
-        clip, rest = rest[0], rest[1:]
+        in_specs=[VMEM] * len(parts),
+        out_specs=VMEM,
+        out_shape=out(1, LANES),
+        name="clip_scale",
+    )(*parts)
+
+
+def pick_kernel(sz, group, me_ref, plan, clip, *rest):
+    c = sz.chips
     refs = rest[: 2 * c]
     outs = rest[2 * c : 3 * c]
+    head, _, size, stride = group
+    at = [head + a * stride for a in range(3)]
     me = me_ref[0]
     chip = lax.div(me, CORES)
     core = lax.rem(me, CORES)
@@ -211,28 +209,24 @@
         for q in range(2 * c):
             @pl.when(choice == q)
             def _():
-                if not early:
-                    outs[x][...] = refs[q][...]
-                    return
-                at = [sz.full + a * sz.early for a in range(3)]
-                parts = [refs[q][:, lo : lo + sz.early] for lo in at]
+                parts = [refs[q][:, lo : lo + size] for lo in at]
                 first, second = moments(*parts, clip[:, 0:1])
-                outs[x][:, : sz.full] = refs[q][:, : sz.full]
-                outs[x][:, at[0] : at[0] + sz.early] = first
-                outs[x][:, at[1] : at[1] + sz.early] = second
-
-
-def pick(sz, early, me, plan, clip, own, other):
-    c = sz.chips
-    width = sz.w_two if early else sz.w_late
-    vectors = ([clip] if early else []) + own + other
-    return pl.pallas_call(
-        functools.partial(pick_kernel, sz, early),
-        in_specs=[SMEM, SMEM] + [VMEM] * len(vectors),
+                if head:
+                    outs[x][:, :head] = refs[q][:, :head]
+                outs[x][:, at[0] : at[0] + size] = first
+                outs[x][:, at[1] : at[1] + size] = second
+
+
+def pick(sz, which, me, plan, clip, own, other):
+    c = sz.chips
+    group = sz.groups[which]
+    return pl.pallas_call(
+        functools.partial(pick_kernel, sz, group),
+        in_specs=[SMEM, SMEM] + [VMEM] * (2 * c + 1),
         out_specs=[VMEM] * c,
-        out_shape=[out(sz.piece, width)] * c,
-        name="pick_early" if early else "pick_late",
-    )(me, plan, *vectors)
+        out_shape=[out(sz.piece, width(group, 2))] * c,
+        name="pick",
+    )(me, plan, clip, *own, *other)
 
 
 def land_kernel(sz, me_ref, plan, *rest):
@@ -297,9 +291,16 @@
     return got[:1] + near(got[1:])
 
 
+def from_others(value, axis):
+    n = lax.axis_size(axis)
+    return sum(
+        lax.ppermute(value, axis, [(i, peer(i, x, n)) for i in range(n)]) for x in range(1, n)
+    )
+
+
 def swap(sz, arrays):
     pairs = [(i, i ^ 1) for i in range(sz.group)]
-    return near([lax.ppermute(a, "expert", pairs) for a in arrays])
+    return [lax.ppermute(a, "expert", pairs) for a in arrays]
 
 
 def shards(master, moment_one, moment_two, gradient, old_slot, new_slot):
@@ -307,17 +308,19 @@
     me = lax.axis_index("expert").reshape(1)
     c = sz.chips
     got = prep(sz, me, old_slot, new_slot, master, moment_one, moment_two, gradient)
-    pieces, raw, plan = list(got[:c]), got[c], got[c + 1]
+    pieces, late, plan = list(got[:c]), list(got[c : 2 * c]), got[2 * c]
     held = spread(sz, pieces)
-    partial = squares(sz, gradient)
-    sums = lax.all_to_all(partial, ("dp", "expert"), 0, 0, tiled=True)
-    clip, *late = scale_and_late(sz, sums, raw)
+    total = squares(sz, gradient)
+    total = total + swap(sz, [total])[0]
+    total = total + from_others(total, "dp")
+    totals = spread(sz, [total] * c)
     late_held = spread(sz, late)
-    other = swap(sz, held)
-    early_out = pick(sz, True, me, plan, clip, held, other)
+    clip = clip_scale(sz, totals)
+    other = near(swap(sz, held))
+    early_out = pick(sz, 0, me, plan, clip, held, other)
     early_in = spread(sz, list(early_out))
-    late_other = swap(sz, late_held)
-    late_out = pick(sz, False, me, plan, None, late_held, late_other)
+    late_other = near(swap(sz, late_held))
+    late_out = pick(sz, 1, me, plan, clip, late_held, late_other)
     late_in = spread(sz, list(late_out))
     scale = clip[0, 0]
     wide = gradient.astype(jnp.float32)

time: 84.7 us -> 99 us (1.17)
  local copies, waits for them, and re-layouts: 5.52 us -> 18.3 us
  waiting for transfers between devices: 39.5 us -> 43.1 us
    unnamed x26 -> x58, local copies, waits for them, and re-layouts: 5.52 us -> 18.3 us
    ppermute x12 -> x15, waiting for transfers between devices: 35.7 us -> 41.9 us  [spread(): got.append(lax.ppermute(arrays[x], 'expert', pairs))]
    all_to_all x1 -> x0, starting transfers between devices: 6 us -> none  [shards(): sums = lax.all_to_all(partial, ('dp', 'expert'), 0, 0, tiled=True)]
    ppermute x8 -> x12, starting transfers between devices: 1.75 us -> 4.65 us  [the longest x3 3.55 us: from_others(): lax.ppermute(value, axis, [(i, peer(i, x, n)) for i in range(n)])]
    ppermute x12 -> x15, starting transfers between devices: 13.4 us -> 15.8 us  [spread(): got.append(lax.ppermute(arrays[x], 'expert', pairs))]
    all_to_all x1 -> x0, waiting for transfers between devices: 1.65 us -> none  [shards(): sums = lax.all_to_all(partial, ('dp', 'expert'), 0, 0, tiled=True)]
    ppermute x8 -> x12, waiting for transfers between devices: 2.16 us -> 1.17 us  [the longest x9 1.16 us: swap(): return [lax.ppermute(a, 'expert', pairs) for a in arrays]]
  transfers between devices with their start and end apart: 21 -> 27, of which waited for: 8 -> 9; matrix products, arithmetic and copies ran while one was open for 6% -> 6% of each run, Pallas kernels for 8% -> 7%
where the time goes in v1:
time: 99 us; the launch traced here: 98.4 us
  waiting for transfers between devices  43.1 us (44%)
  starting transfers between devices  20.4 us (21%)
  local copies, waits for them, and re-layouts  18.3 us (18%)
  Pallas kernels  10.3 us (10%)
  other arithmetic  5.45 us (6%)
    ppermute x15, waiting for transfers between devices, spread(): got.append(lax.ppermute(arrays[x], 'expert', pairs))  41.9 us
    unnamed x58, local copies, waits for them, and re-layouts  18.3 us
    ppermute x15, starting transfers between devices, spread(): got.append(lax.ppermute(arrays[x], 'expert', pairs))  15.8 us
    sub x1, other arithmetic, new_weights(): return master - LEARN_RATE * (step_dir + DECAY_RATE * master)  5.44 us
    ppermute x3, starting transfers between devices, from_others(): lax.ppermute(value, axis, [(i, peer(i, x, n)) for i in range(n)])  3.55 us
    pallas_call x1, Pallas kernels, prep(): pl.pallas_call(functools.partial(prep_kernel, sz), in_specs=[SMEM, SMEM,...  3.07 us
    pallas_call x2, Pallas kernels, pick(): pl.pallas_call(functools.partial(pick_kernel, sz, group), in_specs=[SMEM,...  2.85 us
    pallas_call x1, Pallas kernels, land(): pl.pallas_call(functools.partial(land_kernel, sz), in_specs=[SMEM, SMEM]...  2.32 us
  transfers between devices with their start and end apart: 27, of which 9 were waited for; matrix products, arithmetic and copies ran while one was open for 6% of the time, Pallas kernels for 7%

profile of v1, /device:TPU:12, one launch (start us, length us, event | category | flops | bytes accessed | tf_op | source)
XLA Modules:
  0.0 98.4 jit_solution(4342676846139307825)
XLA Ops:
  0.6 1.3 %squares.1 = f32[1,128]{1,0:T(1,128)S(1)} custom-call(bf16[2,4,16,2880]{3,2,1,0:T(8,128)(2,1)} %grad.3), custom_call_target="tpu_custom_call" | custom-call | tf_op jit(solution)/shard_map/squares/pallas_call | solution.py:160
  2.0 1.1 %collective-permute-done = f32[1,128]{1,0:T(1,128)S(1)} collective-permute-done((f32[1,128]{1,0:T(1,128)S(1)}, f32[1,128]{1,0:T(1,128)S(1)}, u32[]{:S(2)}, u32[]{:S(2)}) %collective-permute-start) | collective-permute-done | bytes 544 | tf_op jit(solution)/shard_map/ppermute | solution.py:303
  3.2 1.4 %collective-permute-start.3 = (f32[1,128]{1,0:T(1,128)S(1)}, f32[1,128]{1,0:T(1,128)S(1)}, u32[]{:S(2)}, u32[]{:S(2)}) collective-permute-start(f32[1,128]{1,0:T(1,128)S(1)} %add.27), channel_id=1, source_target_pairs={{0,24},{8,16},{16,8},{24,0},{1,25},{9,17},{17,9},{25,1},{2,26},{10... | collective-permute-start | bytes 1544 | tf_op jit(solution)/shard_map/ppermute | solution.py:297
  4.6 1.5 %collective-permute-start.2 = (f32[1,128]{1,0:T(1,128)S(1)}, f32[1,128]{1,0:T(1,128)S(1)}, u32[]{:S(2)}, u32[]{:S(2)}) collective-permute-start(f32[1,128]{1,0:T(1,128)S(1)} %add.27), channel_id=1, source_target_pairs={{0,16},{8,24},{16,0},{24,8},{1,17},{9,25},{17,1},{25,9},{2,18},{10... | collective-permute-start | bytes 1544 | tf_op jit(solution)/shard_map/ppermute | solution.py:297
  6.1 3.1 %prep.1 = (f32[8,7168]{1,0:T(8,128)S(1)}, f32[8,7168]{1,0:T(8,128)S(1)}, f32[8,7168]{1,0:T(8,128)S(1)}, f32[8,7168]{1,0:T(8,128)S(1)}, f32[8,4608]{1,0:T(8,128)S...) custom-call(s32[1]{0:T(128)} %bitcast.me_ref, s32[2,32]{1,0:T(2,128)} %old_ref.1, ...), custom_call_target="tpu_custom_call" | custom-call | tf_op jit(solution)/shard_map/prep/pallas_call | solution.py:129
  10.3 2.6 %collective-permute-start.18 = (f32[8,4608]{1,0:T(8,128)S(1)}, f32[8,4608]{1,0:T(8,128)S(1)}, u32[]{:S(2)}, u32[]{:S(2)}) collective-permute-start(f32[8,4608]{1,0:T(8,128)S(1)} %get-tuple-element.31), channel_id=1, source_target_pairs={{0,4},{1,5},{2,6},{3,7},{4,0},{5,1},{6,2},{7,3},{8,12},{9,13},{10,... | collective-permute-start | bytes 442376 | tf_op jit(solution)/shard_map/ppermute | solution.py:290
  13.4 1.6 %collective-permute-start.6 = (f32[1,128]{1,0:T(1,128)S(1)}, f32[1,128]{1,0:T(1,128)S(1)}, u32[]{:S(2)}, u32[]{:S(2)}) collective-permute-start(f32[1,128]{1,0:T(1,128)S(1)} %add_add_fusion.refs_0_), channel_id=1, source_target_pairs={{0,6},{1,7},{2,4},{3,5},{4,2},{5,3},{6,0},{7,1},{8,14},{9,15},{10,... | collective-permute-start | bytes 1544 | tf_op jit(solution)/shard_map/ppermute | solution.py:290
  15.0 10.7 %collective-permute-done.6.refs_3_ = f32[1,128]{1,0:T(1,128)S(1)} collective-permute-done((f32[1,128]{1,0:T(1,128)S(1)}, f32[1,128]{1,0:T(1,128)S(1)}, u32[]{:S(2)}, u32[]{:S(2)}) %collective-permute-start.6) | collective-permute-done | bytes 544 | tf_op jit(solution)/shard_map/ppermute | solution.py:290
  25.7 4.5 %collective-permute-done.5.refs_2_ = f32[1,128]{1,0:T(1,128)S(1)} collective-permute-done((f32[1,128]{1,0:T(1,128)S(1)}, f32[1,128]{1,0:T(1,128)S(1)}, u32[]{:S(2)}, u32[]{:S(2)}) %collective-permute-start.5) | collective-permute-done | bytes 544 | tf_op jit(solution)/shard_map/ppermute | solution.py:290
  30.3 3.4 %collective-permute-done.4.refs_1_ = f32[1,128]{1,0:T(1,128)S(1)} collective-permute-done((f32[1,128]{1,0:T(1,128)S(1)}, f32[1,128]{1,0:T(1,128)S(1)}, u32[]{:S(2)}, u32[]{:S(2)}) %collective-permute-start.4) | collective-permute-done | bytes 544 | tf_op jit(solution)/shard_map/ppermute | solution.py:290
  33.9 2.9 %collective-permute-start.8 = (f32[8,7168]{1,0:T(8,128)S(1)}, f32[8,7168]{1,0:T(8,128)S(1)}, u32[]{:S(2)}, u32[]{:S(2)}) collective-permute-start(f32[8,7168]{1,0:T(8,128)S(1)} %get-tuple-element.23), channel_id=1, source_target_pairs={{0,4},{1,5},{2,6},{3,7},{4,0},{5,1},{6,2},{7,3},{8,12},{9,13},{10,... | collective-permute-start | bytes 688136 | tf_op jit(solution)/shard_map/ppermute | solution.py:290
  39.8 2.4 %collective-permute-done.7.rest_1_ = f32[8,7168]{1,0:T(8,128)S(1)} collective-permute-done((f32[8,7168]{1,0:T(8,128)S(1)}, f32[8,7168]{1,0:T(8,128)S(1)}, u32[]{:S(2)}, u32[]{:S(2)}) %collective-permute-start.7) | collective-permute-done | bytes 229408 | tf_op jit(solution)/shard_map/ppermute | solution.py:290
  42.8 6.5 %collective-permute-done.8.rest_2_ = f32[8,7168]{1,0:T(8,128)S(1)} collective-permute-done((f32[8,7168]{1,0:T(8,128)S(1)}, f32[8,7168]{1,0:T(8,128)S(1)}, u32[]{:S(2)}, u32[]{:S(2)}) %collective-permute-start.8) | collective-permute-done | bytes 229408 | tf_op jit(solution)/shard_map/ppermute | solution.py:290
  49.3 3.9 %collective-permute-done.9.rest_3_ = f32[8,7168]{1,0:T(8,128)S(1)} collective-permute-done((f32[8,7168]{1,0:T(8,128)S(1)}, f32[8,7168]{1,0:T(8,128)S(1)}, u32[]{:S(2)}, u32[]{:S(2)}) %collective-permute-start.9) | collective-permute-done | bytes 229408 | tf_op jit(solution)/shard_map/ppermute | solution.py:290
  63.3 1.4 %pick.3 = (f32[8,3072]{1,0:T(8,128)S(1)}, f32[8,3072]{1,0:T(8,128)S(1)}, f32[8,3072]{1,0:T(8,128)S(1)}, f32[8,3072]{1,0:T(8,128)S(1)}) custom-call(s32[1]{0:T(128)} %bitcast.me_ref, s32[2,17]{1,0:T(2,128)} %get-tuple-element.20.plan, f32[1,128]{1,0:T(1,128)} %copy-done.24, f32[8,4608]{1,0:T(8,128)} %copy-done.8, f32[8,4608]{1,0:T(8,128)S(1)} %copy-done.10, ...), custom_call_target="tpu_custom_call" | custom-call | tf_op jit(solution)/shard_map/pick/pallas_call | solution.py:223
  66.7 3.4 %collective-permute-start.25 = (f32[8,3072]{1,0:T(8,128)}, f32[8,3072]{1,0:T(8,128)S(1)}, u32[]{:S(2)}, u32[]{:S(2)}) collective-permute-start(f32[8,3072]{1,0:T(8,128)} %copy-done.27), channel_id=1, source_target_pairs={{0,4},{1,5},{2,6},{3,7},{4,0},{5,1},{6,2},{7,3},{8,12},{9,13},{10,... | collective-permute-start | bytes 294920 | tf_op jit(solution)/shard_map/ppermute | solution.py:290
  72.2 0.9 copy-done.2
  75.1 1.4 %pick.2 = (f32[8,5760]{1,0:T(8,128)S(1)}, f32[8,5760]{1,0:T(8,128)S(1)}, f32[8,5760]{1,0:T(8,128)S(1)}, f32[8,5760]{1,0:T(8,128)S(1)}) custom-call(s32[1]{0:T(128)} %bitcast.me_ref, s32[2,17]{1,0:T(2,128)} %get-tuple-element.20.plan, f32[1,128]{1,0:T(1,128)} %copy-done.24, f32[8,7168]{1,0:T(8,128)} %copy-done, f32[8,7168]{1,0:T(8,128)S(1)} %collective-permute-done.7.rest_1_, ...), custom_call_target="tpu_custom_call" | custom-call | tf_op jit(solution)/shard_map/pick/pallas_call | solution.py:223
  76.5 1.5 %collective-permute-start.14 = (f32[8,5760]{1,0:T(8,128)S(1)}, f32[8,5760]{1,0:T(8,128)S(1)}, u32[]{:S(2)}, u32[]{:S(2)}) collective-permute-start(f32[8,5760]{1,0:T(8,128)S(1)} %get-tuple-element.26), channel_id=1, source_target_pairs={{0,2},{1,3},{2,0},{3,1},{4,6},{5,7},{6,4},{7,5},{8,10},{9,11},{10,... | collective-permute-start | bytes 552968 | tf_op jit(solution)/shard_map/ppermute | solution.py:290
  78.0 2.0 %collective-permute-start.15 = (f32[8,5760]{1,0:T(8,128)S(1)}, f32[8,5760]{1,0:T(8,128)S(1)}, u32[]{:S(2)}, u32[]{:S(2)}) collective-permute-start(f32[8,5760]{1,0:T(8,128)S(1)} %get-tuple-element.27), channel_id=1, source_target_pairs={{0,4},{1,5},{2,6},{3,7},{4,0},{5,1},{6,2},{7,3},{8,12},{9,13},{10,... | collective-permute-start | bytes 552968 | tf_op jit(solution)/shard_map/ppermute | solution.py:290
  80.1 5.4 %multiply_subtract_fusion = (f32[2,4,16,2880]{3,2,1,0:T(8,128)}, f32[2,4,16,2880]{3,2,1,0:T(8,128)}, f32[2,4,16,2880]{3,2,1,0:T(8,128)}) fusion(f32[2,4,16,2880]{3,2,1,0:T(8,128)} %master.1, f32[]{:T(128)S(1)} %bitcast.3, bf16[2,4,16,2880]{3,2,1,0:T(8,128)(2,1)} %grad.3, f32[2,4,16,2880]{3,2,1,0:T(8,128)} %mone.1, f32[2,4,16,2880]{3,2,1,0:T(8,128)} %mtwo.1), kind=kLoop, calls=%fused_computation.2 | loop fusion | flops 6266880 | bytes 9584644 | tf_op jit(solution)/shard_map/sub | solution.py:51
  85.5 7.3 %collective-permute-done.15.rest_2_ = f32[8,5760]{1,0:T(8,128)S(1)} collective-permute-done((f32[8,5760]{1,0:T(8,128)S(1)}, f32[8,5760]{1,0:T(8,128)S(1)}, u32[]{:S(2)}, u32[]{:S(2)}) %collective-permute-start.15) | collective-permute-done | bytes 184352 | tf_op jit(solution)/shard_map/ppermute | solution.py:290
  92.8 3.2 %collective-permute-done.16.rest_3_ = f32[8,5760]{1,0:T(8,128)S(1)} collective-permute-done((f32[8,5760]{1,0:T(8,128)S(1)}, f32[8,5760]{1,0:T(8,128)S(1)}, u32[]{:S(2)}, u32[]{:S(2)}) %collective-permute-start.16) | collective-permute-done | bytes 184352 | tf_op jit(solution)/shard_map/ppermute | solution.py:290
  96.1 2.3 %land.1 = (f32[2,4,16,2880]{3,2,1,0:T(8,128)}, f32[2,4,16,2880]{3,2,1,0:T(8,128)}, f32[2,4,16,2880]{3,2,1,0:T(8,128)}) custom-call(s32[1]{0:T(128)} %bitcast.me_ref, s32[2,17]{1,0:T(2,128)} %get-tuple-element.20.plan, f32[8,5760]{1,0:T(8,128)} %copy-done.7, ...), custom_call_target="tpu_custom_call", output_to_operand_aliasing={{0}: (10, {}), {1}: (11, {}), {2}: (12, {})} | custom-call | tf_op jit(solution)/shard_map/land/pallas_call | solution.py:268
  (97 shorter events, 21.6 us)
Async XLA Ops:
  3.2 9.7 %collective-permute-start.3 = (f32[1,128]{1,0:T(1,128)S(1)}, f32[1,128]{1,0:T(1,128)S(1)}, u32[]{:S(2)}, u32[]{:S(2)}) collective-permute-start(f32[1,128]{1,0:T(1,128)S(1)} %add.27), channel_id=1, source_target_pairs={{0,24},{8,16},{16,8},{24,0},{1,25},{9,17},{17,9},{25,1},{2,26},{10... | collective-permute-start | bytes 1544 | tf_op jit(solution)/shard_map/ppermute | solution.py:297
  4.6 8.7 %collective-permute-start.2 = (f32[1,128]{1,0:T(1,128)S(1)}, f32[1,128]{1,0:T(1,128)S(1)}, u32[]{:S(2)}, u32[]{:S(2)}) collective-permute-start(f32[1,128]{1,0:T(1,128)S(1)} %add.27), channel_id=1, source_target_pairs={{0,16},{8,24},{16,0},{24,8},{1,17},{9,25},{17,1},{25,9},{2,18},{10... | collective-permute-start | bytes 1544 | tf_op jit(solution)/shard_map/ppermute | solution.py:297
  9.9 24.1 %collective-permute-start.17 = (f32[8,4608]{1,0:T(8,128)S(1)}, f32[8,4608]{1,0:T(8,128)S(1)}, u32[]{:S(2)}, u32[]{:S(2)}) collective-permute-start(f32[8,4608]{1,0:T(8,128)S(1)} %get-tuple-element.30), channel_id=1, source_target_pairs={{0,2},{1,3},{2,0},{3,1},{4,6},{5,7},{6,4},{7,5},{8,10},{9,11},{10,... | collective-permute-start | bytes 442376 | tf_op jit(solution)/shard_map/ppermute | solution.py:290
  10.3 26.5 %collective-permute-start.18 = (f32[8,4608]{1,0:T(8,128)S(1)}, f32[8,4608]{1,0:T(8,128)S(1)}, u32[]{:S(2)}, u32[]{:S(2)}) collective-permute-start(f32[8,4608]{1,0:T(8,128)S(1)} %get-tuple-element.31), channel_id=1, source_target_pairs={{0,4},{1,5},{2,6},{3,7},{4,0},{5,1},{6,2},{7,3},{8,12},{9,13},{10,... | collective-permute-start | bytes 442376 | tf_op jit(solution)/shard_map/ppermute | solution.py:290
  12.9 24.4 %collective-permute-start.19 = (f32[8,4608]{1,0:T(8,128)S(1)}, f32[8,4608]{1,0:T(8,128)S(1)}, u32[]{:S(2)}, u32[]{:S(2)}) collective-permute-start(f32[8,4608]{1,0:T(8,128)S(1)} %get-tuple-element.32), channel_id=1, source_target_pairs={{0,6},{1,7},{2,4},{3,5},{4,2},{5,3},{6,0},{7,1},{8,14},{9,15},{10,... | collective-permute-start | bytes 442376 | tf_op jit(solution)/shard_map/ppermute | solution.py:290
  13.3 24.6 %collective-permute-start.20 = (f32[8,4608]{1,0:T(8,128)S(1)}, f32[8,4608]{1,0:T(8,128)S(1)}, u32[]{:S(2)}, u32[]{:S(2)}) collective-permute-start(f32[8,4608]{1,0:T(8,128)S(1)} %get-tuple-element.29.rest_0_), channel_id=1, source_target_pairs={{0,1},{1,0},{2,3},{3,2},{4,5},{5,4},{6,7},{7,6},{8,9},{9,8},{10,11... | collective-permute-start | bytes 442376 | tf_op jit(solution)/shard_map/ppermute | solution.py:303
  13.4 12.4 %collective-permute-start.6 = (f32[1,128]{1,0:T(1,128)S(1)}, f32[1,128]{1,0:T(1,128)S(1)}, u32[]{:S(2)}, u32[]{:S(2)}) collective-permute-start(f32[1,128]{1,0:T(1,128)S(1)} %add_add_fusion.refs_0_), channel_id=1, source_target_pairs={{0,6},{1,7},{2,4},{3,5},{4,2},{5,3},{6,0},{7,1},{8,14},{9,15},{10,... | collective-permute-start | bytes 1544 | tf_op jit(solution)/shard_map/ppermute | solution.py:290
  25.7 4.5 %collective-permute-start.5 = (f32[1,128]{1,0:T(1,128)S(1)}, f32[1,128]{1,0:T(1,128)S(1)}, u32[]{:S(2)}, u32[]{:S(2)}) collective-permute-start(f32[1,128]{1,0:T(1,128)S(1)} %add_add_fusion.refs_0_), channel_id=1, source_target_pairs={{0,4},{1,5},{2,6},{3,7},{4,0},{5,1},{6,2},{7,3},{8,12},{9,13},{10,... | collective-permute-start | bytes 1544 | tf_op jit(solution)/shard_map/ppermute | solution.py:290
  33.8 8.4 %collective-permute-start.7 = (f32[8,7168]{1,0:T(8,128)S(1)}, f32[8,7168]{1,0:T(8,128)S(1)}, u32[]{:S(2)}, u32[]{:S(2)}) collective-permute-start(f32[8,7168]{1,0:T(8,128)S(1)} %get-tuple-element.22), channel_id=1, source_target_pairs={{0,2},{1,3},{2,0},{3,1},{4,6},{5,7},{6,4},{7,5},{8,10},{9,11},{10,... | collective-permute-start | bytes 688136 | tf_op jit(solution)/shard_map/ppermute | solution.py:290
  33.9 15.4 %collective-permute-start.8 = (f32[8,7168]{1,0:T(8,128)S(1)}, f32[8,7168]{1,0:T(8,128)S(1)}, u32[]{:S(2)}, u32[]{:S(2)}) collective-permute-start(f32[8,7168]{1,0:T(8,128)S(1)} %get-tuple-element.23), channel_id=1, source_target_pairs={{0,4},{1,5},{2,6},{3,7},{4,0},{5,1},{6,2},{7,3},{8,12},{9,13},{10,... | collective-permute-start | bytes 688136 | tf_op jit(solution)/shard_map/ppermute | solution.py:290
  36.8 16.4 %collective-permute-start.9 = (f32[8,7168]{1,0:T(8,128)S(1)}, f32[8,7168]{1,0:T(8,128)S(1)}, u32[]{:S(2)}, u32[]{:S(2)}) collective-permute-start(f32[8,7168]{1,0:T(8,128)S(1)} %get-tuple-element.24), channel_id=1, source_target_pairs={{0,6},{1,7},{2,4},{3,5},{4,2},{5,3},{6,0},{7,1},{8,14},{9,15},{10,... | collective-permute-start | bytes 688136 | tf_op jit(solution)/shard_map/ppermute | solution.py:290
  37.3 15.9 %collective-permute-start.21 = (f32[8,4608]{1,0:T(8,128)S(1)}, f32[8,4608]{1,0:T(8,128)S(1)}, u32[]{:S(2)}, u32[]{:S(2)}) collective-permute-start(f32[8,4608]{1,0:T(8,128)S(1)} %collective-permute-done.17.rest_1_), channel_id=1, source_target_pairs={{0,1},{1,0},{2,3},{3,2},{4,5},{5,4},{6,7},{7,6},{8,9},{9,8},{10,11... | collective-permute-start | bytes 442376 | tf_op jit(solution)/shard_map/ppermute | solution.py:303
  38.6 15.8 %collective-permute-start.22 = (f32[8,4608]{1,0:T(8,128)S(1)}, f32[8,4608]{1,0:T(8,128)S(1)}, u32[]{:S(2)}, u32[]{:S(2)}) collective-permute-start(f32[8,4608]{1,0:T(8,128)S(1)} %collective-permute-done.18.rest_2_), channel_id=1, source_target_pairs={{0,1},{1,0},{2,3},{3,2},{4,5},{5,4},{6,7},{7,6},{8,9},{9,8},{10,11... | collective-permute-start | bytes 442376 | tf_op jit(solution)/shard_map/ppermute | solution.py:303
  42.2 14.1 %collective-permute-start.23 = (f32[8,4608]{1,0:T(8,128)S(1)}, f32[8,4608]{1,0:T(8,128)S(1)}, u32[]{:S(2)}, u32[]{:S(2)}) collective-permute-start(f32[8,4608]{1,0:T(8,128)S(1)} %collective-permute-done.19.rest_3_), channel_id=1, source_target_pairs={{0,1},{1,0},{2,3},{3,2},{4,5},{5,4},{6,7},{7,6},{8,9},{9,8},{10,11... | collective-permute-start | bytes 442376 | tf_op jit(solution)/shard_map/ppermute | solution.py:303
  49.3 17.3 %collective-permute-start.10 = (f32[8,7168]{1,0:T(8,128)S(1)}, f32[8,7168]{1,0:T(8,128)S(1)}, u32[]{:S(2)}, u32[]{:S(2)}) collective-permute-start(f32[8,7168]{1,0:T(8,128)S(1)} %get-tuple-element.21.rest_0_), channel_id=1, source_target_pairs={{0,1},{1,0},{2,3},{3,2},{4,5},{5,4},{6,7},{7,6},{8,9},{9,8},{10,11... | collective-permute-start | bytes 688136 | tf_op jit(solution)/shard_map/ppermute | solution.py:303
  53.2 16.9 %collective-permute-start.11 = (f32[8,7168]{1,0:T(8,128)S(1)}, f32[8,7168]{1,0:T(8,128)S(1)}, u32[]{:S(2)}, u32[]{:S(2)}) collective-permute-start(f32[8,7168]{1,0:T(8,128)S(1)} %collective-permute-done.7.rest_1_), channel_id=1, source_target_pairs={{0,1},{1,0},{2,3},{3,2},{4,5},{5,4},{6,7},{7,6},{8,9},{9,8},{10,11... | collective-permute-start | bytes 688136 | tf_op jit(solution)/shard_map/ppermute | solution.py:303
  53.9 17.0 %collective-permute-start.12 = (f32[8,7168]{1,0:T(8,128)S(1)}, f32[8,7168]{1,0:T(8,128)S(1)}, u32[]{:S(2)}, u32[]{:S(2)}) collective-permute-start(f32[8,7168]{1,0:T(8,128)S(1)} %collective-permute-done.8.rest_2_), channel_id=1, source_target_pairs={{0,1},{1,0},{2,3},{3,2},{4,5},{5,4},{6,7},{7,6},{8,9},{9,8},{10,11... | collective-permute-start | bytes 688136 | tf_op jit(solution)/shard_map/ppermute | solution.py:303
  55.0 16.5 %collective-permute-start.13 = (f32[8,7168]{1,0:T(8,128)S(1)}, f32[8,7168]{1,0:T(8,128)S(1)}, u32[]{:S(2)}, u32[]{:S(2)}) collective-permute-start(f32[8,7168]{1,0:T(8,128)S(1)} %collective-permute-done.9.rest_3_), channel_id=1, source_target_pairs={{0,1},{1,0},{2,3},{3,2},{4,5},{5,4},{6,7},{7,6},{8,9},{9,8},{10,11... | collective-permute-start | bytes 688136 | tf_op jit(solution)/shard_map/ppermute | solution.py:303
  66.7 13.3 %collective-permute-start.24 = (f32[8,3072]{1,0:T(8,128)S(1)}, f32[8,3072]{1,0:T(8,128)S(1)}, u32[]{:S(2)}, u32[]{:S(2)}) collective-permute-start(f32[8,3072]{1,0:T(8,128)S(1)} %get-tuple-element.34), channel_id=1, source_target_pairs={{0,2},{1,3},{2,0},{3,1},{4,6},{5,7},{6,4},{7,5},{8,10},{9,11},{10,... | collective-permute-start | bytes 294920 | tf_op jit(solution)/shard_map/ppermute | solution.py:290
  66.7 18.8 %collective-permute-start.25 = (f32[8,3072]{1,0:T(8,128)}, f32[8,3072]{1,0:T(8,128)S(1)}, u32[]{:S(2)}, u32[]{:S(2)}) collective-permute-start(f32[8,3072]{1,0:T(8,128)} %copy-done.27), channel_id=1, source_target_pairs={{0,4},{1,5},{2,6},{3,7},{4,0},{5,1},{6,2},{7,3},{8,12},{9,13},{10,... | collective-permute-start | bytes 294920 | tf_op jit(solution)/shard_map/ppermute | solution.py:290
  70.8 14.7 %collective-permute-start.26 = (f32[8,3072]{1,0:T(8,128)}, f32[8,3072]{1,0:T(8,128)S(1)}, u32[]{:S(2)}, u32[]{:S(2)}) collective-permute-start(f32[8,3072]{1,0:T(8,128)} %copy-done.26), channel_id=1, source_target_pairs={{0,6},{1,7},{2,4},{3,5},{4,2},{5,3},{6,0},{7,1},{8,14},{9,15},{10,... | collective-permute-start | bytes 294920 | tf_op jit(solution)/shard_map/ppermute | solution.py:290
  76.5 9.0 %collective-permute-start.14 = (f32[8,5760]{1,0:T(8,128)S(1)}, f32[8,5760]{1,0:T(8,128)S(1)}, u32[]{:S(2)}, u32[]{:S(2)}) collective-permute-start(f32[8,5760]{1,0:T(8,128)S(1)} %get-tuple-element.26), channel_id=1, source_target_pairs={{0,2},{1,3},{2,0},{3,1},{4,6},{5,7},{6,4},{7,5},{8,10},{9,11},{10,... | collective-permute-start | bytes 552968 | tf_op jit(solution)/shard_map/ppermute | solution.py:290
  78.0 14.8 %collective-permute-start.15 = (f32[8,5760]{1,0:T(8,128)S(1)}, f32[8,5760]{1,0:T(8,128)S(1)}, u32[]{:S(2)}, u32[]{:S(2)}) collective-permute-start(f32[8,5760]{1,0:T(8,128)S(1)} %get-tuple-element.27), channel_id=1, source_target_pairs={{0,4},{1,5},{2,6},{3,7},{4,0},{5,1},{6,2},{7,3},{8,12},{9,13},{10,... | collective-permute-start | bytes 552968 | tf_op jit(solution)/shard_map/ppermute | solution.py:290
  80.0 16.1 %collective-permute-start.16 = (f32[8,5760]{1,0:T(8,128)S(1)}, f32[8,5760]{1,0:T(8,128)S(1)}, u32[]{:S(2)}, u32[]{:S(2)}) collective-permute-start(f32[8,5760]{1,0:T(8,128)S(1)} %get-tuple-element.28), channel_id=1, source_target_pairs={{0,6},{1,7},{2,4},{3,5},{4,2},{5,3},{6,0},{7,1},{8,14},{9,15},{10,... | collective-permute-start | bytes 552968 | tf_op jit(solution)/shard_map/ppermute | solution.py:290
  (32 other events, 204.7 us)

commit v2 on v1

--- a/solution.py
+++ b/solution.py
@@ -20,7 +20,7 @@
 
 LANES = 128
 CORES = 2
-EARLY = 0.5
+EARLY = 0.25
 
 ANY = pl.BlockSpec(memory_space=pl.ANY)
 SMEM = pl.BlockSpec(memory_space=pltpu.SMEM)
@@ -59,7 +59,7 @@
         self.chips = group // CORES
         self.piece = self.layers * self.rows // self.chips
         self.per_layer = self.rows // self.piece
-        early = up(int(self.cols * EARLY)) - LANES
+        early = round(self.cols * EARLY / LANES) * LANES
         self.early = early
         self.late = self.cols - early
         self.lat = up(self.late)
@@ -82,8 +82,10 @@
 
 def prep_kernel(sz, me_ref, old_ref, new_ref, master, mone, mtwo, grad, *rest):
     c = sz.chips
-    pieces = rest[:c], rest[c : 2 * c]
-    plan, mv, m1v, m2v, gv, st, sem = rest[2 * c :]
+    pieces = rest[:c]
+    late_raw, total, plan, mv, m1v, m2v, gv, st, sem_g, sem = rest[c:]
+    for i in range(sz.layers):
+        pltpu.make_async_copy(grad.at[i], gv.at[i], sem_g.at[i]).start()
     me = me_ref[0]
     chip = lax.div(me, CORES)
     n_slots = sz.layers * sz.group
@@ -99,12 +101,19 @@
 
         lax.fori_loop(0, old_ref.shape[1], note, 0, unroll=8)
         slot = plan[1, i * sz.group + me]
-        for a, (src, dst) in enumerate(((master, mv), (mone, m1v), (mtwo, m2v), (grad, gv))):
+        for a, (src, dst) in enumerate(((master, mv), (mone, m1v), (mtwo, m2v))):
             pltpu.make_async_copy(src.at[i, slot], dst.at[i], sem.at[i, a]).start()
-    for i in range(sz.layers):
-        for a, (src, dst) in enumerate(((master, mv), (mone, m1v), (mtwo, m2v), (grad, gv))):
+    acc = jnp.zeros((sz.rows, sz.cols), jnp.float32)
+    for i in range(sz.layers):
+        pltpu.make_async_copy(grad.at[i], gv.at[i], sem_g.at[i]).wait()
+        for s in range(sz.slots):
+            x = gv[i, s].astype(jnp.float32)
+            acc = acc + x * x
+    total[...] = jnp.broadcast_to(jnp.sum(acc), total.shape)
+    for i in range(sz.layers):
+        for a, (src, dst) in enumerate(((master, mv), (mone, m1v), (mtwo, m2v))):
             pltpu.make_async_copy(src.at[i, 0], dst.at[i], sem.at[i, a]).wait()
-        g = gv[i].astype(jnp.float32)
+        g = gv[i, plan[1, i * sz.group + me]].astype(jnp.float32)
         for q in range(sz.per_layer):
             k = i * sz.per_layer + q
             r = slice(q * sz.piece, (q + 1) * sz.piece)
@@ -114,80 +123,59 @@
             st[3, k] = g[r, :]
     for x in range(c):
         k = dyn_peer(chip, x, c)
-        pieces[0][x][:, : sz.cols] = st[0, k]
-        for refs, (head, start, size, stride) in zip(pieces, sz.groups):
-            for a in range(3):
-                lo = head + a * stride
-                refs[x][:, lo : lo + size] = st[a + 1, k, :, start : start + size]
+        pieces[x][:, : sz.cols] = st[0, k]
+        for a in range(3):
+            lo = sz.full + a * sz.early
+            pieces[x][:, lo : lo + sz.early] = st[a + 1, k, :, : sz.early]
+            late_raw[a, x] = st[a + 1, k, :, sz.early :]
 
 
 def prep(sz, me, old_slot, new_slot, master, mone, mtwo, grad):
     f32 = jnp.float32
     slot = (sz.layers, sz.rows, sz.cols)
-    outs = [out(sz.piece, width(g, 3)) for g in sz.groups for _ in range(sz.chips)]
-    outs.append(jax.ShapeDtypeStruct((2, sz.layers * sz.group + 1), jnp.int32))
+    outs = [out(sz.piece, width(sz.groups[0], 3))] * sz.chips + [
+        out(3, sz.chips, sz.piece, sz.late),
+        out(1, LANES),
+        jax.ShapeDtypeStruct((2, sz.layers * sz.group + 1), jnp.int32),
+    ]
     return pl.pallas_call(
         functools.partial(prep_kernel, sz),
         in_specs=[SMEM, SMEM, SMEM, ANY, ANY, ANY, ANY],
-        out_specs=[VMEM] * (2 * sz.chips) + [SMEM],
+        out_specs=[VMEM] * (sz.chips + 2) + [SMEM],
         out_shape=outs,
         scratch_shapes=[
             pltpu.VMEM(slot, f32),
             pltpu.VMEM(slot, f32),
             pltpu.VMEM(slot, f32),
-            pltpu.VMEM(slot, grad.dtype),
+            pltpu.VMEM(grad.shape, grad.dtype),
             pltpu.VMEM((4, sz.chips, sz.piece, sz.cols), f32),
-            pltpu.SemaphoreType.DMA((sz.layers, 4)),
+            pltpu.SemaphoreType.DMA((sz.layers,)),
+            pltpu.SemaphoreType.DMA((sz.layers, 3)),
         ],
         name="prep",
     )(me, old_slot, new_slot, master, mone, mtwo, grad)
 
 
-def square_kernel(sz, grad, total, gv, sem):
-    copies = [pltpu.make_async_copy(grad.at[i], gv.at[i], sem.at[i]) for i in range(sz.layers)]
-    for cp in copies:
-        cp.start()
-    acc = jnp.zeros((sz.rows, sz.cols), jnp.float32)
-    for i in range(sz.layers):
-        copies[i].wait()
-        for s in range(sz.slots):
-            x = gv[i, s].astype(jnp.float32)
-            acc = acc + x * x
-    total[...] = jnp.broadcast_to(jnp.sum(acc), total.shape)
-
-
-def squares(sz, grad):
-    return pl.pallas_call(
-        functools.partial(square_kernel, sz),
-        in_specs=[ANY],
-        out_specs=VMEM,
-        out_shape=out(1, LANES),
-        scratch_shapes=[
-            pltpu.VMEM(grad.shape, grad.dtype),
-            pltpu.SemaphoreType.DMA((sz.layers,)),
-        ],
-        name="squares",
-    )(grad)
-
-
-def scale_kernel(sz, *refs):
+def scale_kernel(sz, total, raw, clip, *late):
     entries = sz.layers * sz.slots * sz.rows * sz.cols * sz.devices
-    square_sum = refs[0][...]
-    for part in refs[1:-1]:
-        square_sum = square_sum + part[...]
-    refs[-1][...] = jnp.minimum(
-        1.0, CLIP_RMS * math.sqrt(entries) / (jnp.sqrt(square_sum) + 1e-06)
+    scale = jnp.minimum(
+        1.0, CLIP_RMS * math.sqrt(entries) / (jnp.sqrt(total[...]) + 1e-06)
     )
-
-
-def clip_scale(sz, parts):
+    clip[...] = scale
+    for x in range(sz.chips):
+        first, second = moments(raw[0, x], raw[1, x], raw[2, x], scale[:, 0:1])
+        late[x][:, : sz.late] = first
+        late[x][:, sz.lat : sz.lat + sz.late] = second
+
+
+def scale_and_late(sz, total, raw):
     return pl.pallas_call(
         functools.partial(scale_kernel, sz),
-        in_specs=[VMEM] * len(parts),
-        out_specs=VMEM,
-        out_shape=out(1, LANES),
-        name="clip_scale",
-    )(*parts)
+        in_specs=[VMEM, VMEM],
+        out_specs=[VMEM] * (sz.chips + 1),
+        out_shape=[out(1, LANES)] + [out(sz.piece, width(sz.groups[1], 2))] * sz.chips,
+        name="scale_late",
+    )(*near((total, raw)))
 
 
 def pick_kernel(sz, group, me_ref, plan, clip, *rest):
@@ -209,10 +197,12 @@
         for q in range(2 * c):
             @pl.when(choice == q)
             def _():
+                if not head:
+                    outs[x][...] = refs[q][...]
+                    return
                 parts = [refs[q][:, lo : lo + size] for lo in at]
                 first, second = moments(*parts, clip[:, 0:1])
-                if head:
-                    outs[x][:, :head] = refs[q][:, :head]
+                outs[x][:, :head] = refs[q][:, :head]
                 outs[x][:, at[0] : at[0] + size] = first
                 outs[x][:, at[1] : at[1] + size] = second
 
@@ -280,7 +270,7 @@
     )(me, plan, *early, *late, *outs)
 
 
-def spread(sz, arrays):
+def shifts(sz, arrays):
     c = sz.chips
     got = [arrays[0]]
     for x in range(1, c):
@@ -288,6 +278,11 @@
             (i * CORES + k, peer(i, x, c) * CORES + k) for i in range(c) for k in range(CORES)
         ]
         got.append(lax.ppermute(arrays[x], "expert", pairs))
+    return got
+
+
+def spread(sz, arrays):
+    got = shifts(sz, arrays)
     return got[:1] + near(got[1:])
 
 
@@ -308,14 +303,14 @@
     me = lax.axis_index("expert").reshape(1)
     c = sz.chips
     got = prep(sz, me, old_slot, new_slot, master, moment_one, moment_two, gradient)
-    pieces, late, plan = list(got[:c]), list(got[c : 2 * c]), got[2 * c]
+    pieces, raw, total, plan = list(got[:c]), got[c], got[c + 1], got[c + 2]
+    totals = shifts(sz, [total] * c)
     held = spread(sz, pieces)
-    total = squares(sz, gradient)
+    total = sum(totals)
     total = total + swap(sz, [total])[0]
     total = total + from_others(total, "dp")
-    totals = spread(sz, [total] * c)
+    clip, *late = scale_and_late(sz, total, raw)
     late_held = spread(sz, late)
-    clip = clip_scale(sz, totals)
     other = near(swap(sz, held))
     early_out = pick(sz, 0, me, plan, clip, held, other)
     early_in = spread(sz, list(early_out))

time: 99 us -> 82.1 us (0.83)
  local copies, waits for them, and re-layouts: 18.3 us -> 0.68 us
  starting transfers between devices: 20.4 us -> 24 us
  Pallas kernels: 10.3 us -> 8.69 us
  waiting for transfers between devices: 43.1 us -> 42.1 us
    unnamed x58 -> x12, local copies, waits for them, and re-layouts: 18.3 us -> 0.68 us
    ppermute x15, waiting for transfers between devices: 41.9 us -> 37.9 us  [shifts(): got.append(lax.ppermute(arrays[x], 'expert', pairs))]
    ppermute x15, starting transfers between devices: 15.8 us -> 19.3 us  [shifts(): got.append(lax.ppermute(arrays[x], 'expert', pairs))]
    ppermute x3, waiting for transfers between devices: 0.01 us -> 3.03 us  [from_others(): lax.ppermute(value, axis, [(i, peer(i, x, n)) for i in range(n)])]
    pallas_call x2 -> x1, Pallas kernels: 2 us -> 0.17 us  [scale_and_late(): pl.pallas_call(functools.partial(scale_kernel, sz), in_specs=[VMEM, VMEM]...]
  transfers between devices with their start and end apart: 27 -> 27, of which waited for: 9 -> 14; matrix products, arithmetic and copies ran while one was open for 6% -> 7% of each run, Pallas kernels for 7% -> 4%
where the time goes in v2:
time: 82.1 us; the launch traced here: 81.6 us
  waiting for transfers between devices  42.1 us (51%)
  starting transfers between devices  24 us (29%)
  Pallas kernels  8.69 us (11%)
  other arithmetic  5.46 us (7%)
    ppermute x15, waiting for transfers between devices, shifts(): got.append(lax.ppermute(arrays[x], 'expert', pairs))  37.9 us
    ppermute x15, starting transfers between devices, shifts(): got.append(lax.ppermute(arrays[x], 'expert', pairs))  19.3 us
    sub x1, other arithmetic, new_weights(): return master - LEARN_RATE * (step_dir + DECAY_RATE * master)  5.44 us
    ppermute x3, starting transfers between devices, from_others(): lax.ppermute(value, axis, [(i, peer(i, x, n)) for i in range(n)])  3.49 us
    pallas_call x1, Pallas kernels, prep(): pl.pallas_call(functools.partial(prep_kernel, sz), in_specs=[SMEM, SMEM,...  3.09 us
    pallas_call x2, Pallas kernels, pick(): pl.pallas_call(functools.partial(pick_kernel, sz, group), in_specs=[SMEM,...  3.07 us
    ppermute x3, waiting for transfers between devices, from_others(): lax.ppermute(value, axis, [(i, peer(i, x, n)) for i in range(n)])  3.03 us
    pallas_call x1, Pallas kernels, land(): pl.pallas_call(functools.partial(land_kernel, sz), in_specs=[SMEM, SMEM]...  2.36 us
  transfers between devices with their start and end apart: 27, of which 14 were waited for; matrix products, arithmetic and copies ran while one was open for 7% of the time, Pallas kernels for 4%

profile of v2, /device:TPU:12, one launch (start us, length us, event | category | flops | bytes accessed | tf_op | source)
XLA Modules:
  0.0 81.6 jit_solution(13613656692829968005)
XLA Ops:
  0.6 3.1 %prep.1 = (f32[8,5248]{1,0:T(8,128)S(1)}, f32[8,5248]{1,0:T(8,128)S(1)}, f32[8,5248]{1,0:T(8,128)S(1)}, f32[8,5248]{1,0:T(8,128)S(1)}, f32[3,4,8,2112]{3,2,1,0:T...) custom-call(s32[1]{0:T(128)} %bitcast.me_ref, s32[2,32]{1,0:T(2,128)} %old_ref.1, s32[2,32]{1,0:T(2,128)} %new_ref.1, ...), custom_call_target="tpu_custom_call" | custom-call | tf_op jit(solution)/shard_map/prep/pallas_call | solution.py:141
  3.7 1.6 %collective-permute-start.2 = (f32[1,128]{1,0:T(1,128)S(1)}, f32[1,128]{1,0:T(1,128)S(1)}, u32[]{:S(2)}, u32[]{:S(2)}) collective-permute-start(f32[1,128]{1,0:T(1,128)S(1)} %get-tuple-element.24), channel_id=1, source_target_pairs={{0,6},{1,7},{2,4},{3,5},{4,2},{5,3},{6,0},{7,1},{8,14},{9,15},{10,... | collective-permute-start | bytes 1544 | tf_op jit(solution)/shard_map/ppermute | solution.py:280
  6.6 1.2 %collective-permute-start = (f32[1,128]{1,0:T(1,128)S(1)}, f32[1,128]{1,0:T(1,128)S(1)}, u32[]{:S(2)}, u32[]{:S(2)}) collective-permute-start(f32[1,128]{1,0:T(1,128)S(1)} %get-tuple-element.24), channel_id=1, source_target_pairs={{0,2},{1,3},{2,0},{3,1},{4,6},{5,7},{6,4},{7,5},{8,10},{9,11},{10,... | collective-permute-start | bytes 1544 | tf_op jit(solution)/shard_map/ppermute | solution.py:280
  7.9 2.0 %collective-permute-done.1 = f32[1,128]{1,0:T(1,128)S(1)} collective-permute-done((f32[1,128]{1,0:T(1,128)S(1)}, f32[1,128]{1,0:T(1,128)S(1)}, u32[]{:S(2)}, u32[]{:S(2)}) %collective-permute-start.1) | collective-permute-done | bytes 544 | tf_op jit(solution)/shard_map/ppermute | solution.py:280
  11.4 1.4 %collective-permute-start.6 = (f32[1,128]{1,0:T(1,128)S(1)}, f32[1,128]{1,0:T(1,128)S(1)}, u32[]{:S(2)}, u32[]{:S(2)}) collective-permute-start(f32[1,128]{1,0:T(1,128)S(1)} %add.39), channel_id=1, source_target_pairs={{0,24},{8,16},{16,8},{24,0},{1,25},{9,17},{17,9},{25,1},{2,26},{10... | collective-permute-start | bytes 1544 | tf_op jit(solution)/shard_map/ppermute | solution.py:292
  12.8 1.5 %collective-permute-start.5 = (f32[1,128]{1,0:T(1,128)S(1)}, f32[1,128]{1,0:T(1,128)S(1)}, u32[]{:S(2)}, u32[]{:S(2)}) collective-permute-start(f32[1,128]{1,0:T(1,128)S(1)} %add.39), channel_id=1, source_target_pairs={{0,16},{8,24},{16,0},{24,8},{1,17},{9,25},{17,1},{25,9},{2,18},{10... | collective-permute-start | bytes 1544 | tf_op jit(solution)/shard_map/ppermute | solution.py:292
  16.4 1.5 %collective-permute-done.4 = f32[1,128]{1,0:T(1,128)S(1)} collective-permute-done((f32[1,128]{1,0:T(1,128)S(1)}, f32[1,128]{1,0:T(1,128)S(1)}, u32[]{:S(2)}, u32[]{:S(2)}) %collective-permute-start.4) | collective-permute-done | bytes 544 | tf_op jit(solution)/shard_map/ppermute | solution.py:292
  18.1 2.3 %collective-permute-start.17 = (f32[8,4352]{1,0:T(8,128)S(1)}, f32[8,4352]{1,0:T(8,128)S(1)}, u32[]{:S(2)}, u32[]{:S(2)}) collective-permute-start(f32[8,4352]{1,0:T(8,128)S(1)} %get-tuple-element.36), channel_id=1, source_target_pairs={{0,2},{1,3},{2,0},{3,1},{4,6},{5,7},{6,4},{7,5},{8,10},{9,11},{10,... | collective-permute-start | bytes 417800 | tf_op jit(solution)/shard_map/ppermute | solution.py:280
  20.4 2.0 %collective-permute-start.18 = (f32[8,4352]{1,0:T(8,128)S(1)}, f32[8,4352]{1,0:T(8,128)S(1)}, u32[]{:S(2)}, u32[]{:S(2)}) collective-permute-start(f32[8,4352]{1,0:T(8,128)S(1)} %get-tuple-element.37), channel_id=1, source_target_pairs={{0,4},{1,5},{2,6},{3,7},{4,0},{5,1},{6,2},{7,3},{8,12},{9,13},{10,... | collective-permute-start | bytes 417800 | tf_op jit(solution)/shard_map/ppermute | solution.py:280
  22.3 2.4 %collective-permute-start.7 = (f32[8,5248]{1,0:T(8,128)S(1)}, f32[8,5248]{1,0:T(8,128)S(1)}, u32[]{:S(2)}, u32[]{:S(2)}) collective-permute-start(f32[8,5248]{1,0:T(8,128)S(1)} %get-tuple-element.28), channel_id=1, source_target_pairs={{0,2},{1,3},{2,0},{3,1},{4,6},{5,7},{6,4},{7,5},{8,10},{9,11},{10,... | collective-permute-start | bytes 503816 | tf_op jit(solution)/shard_map/ppermute | solution.py:280
  24.9 1.5 %collective-permute-start.8 = (f32[8,5248]{1,0:T(8,128)S(1)}, f32[8,5248]{1,0:T(8,128)S(1)}, u32[]{:S(2)}, u32[]{:S(2)}) collective-permute-start(f32[8,5248]{1,0:T(8,128)S(1)} %get-tuple-element.29), channel_id=1, source_target_pairs={{0,4},{1,5},{2,6},{3,7},{4,0},{5,1},{6,2},{7,3},{8,12},{9,13},{10,... | collective-permute-start | bytes 503816 | tf_op jit(solution)/shard_map/ppermute | solution.py:280
  26.4 4.9 %collective-permute-done.18.rest_2_ = f32[8,4352]{1,0:T(8,128)S(1)} collective-permute-done((f32[8,4352]{1,0:T(8,128)S(1)}, f32[8,4352]{1,0:T(8,128)S(1)}, u32[]{:S(2)}, u32[]{:S(2)}) %collective-permute-start.18) | collective-permute-done | bytes 139296 | tf_op jit(solution)/shard_map/ppermute | solution.py:280
  31.3 10.8 %collective-permute-done.19.rest_3_ = f32[8,4352]{1,0:T(8,128)S(1)} collective-permute-done((f32[8,4352]{1,0:T(8,128)S(1)}, f32[8,4352]{1,0:T(8,128)S(1)}, u32[]{:S(2)}, u32[]{:S(2)}) %collective-permute-start.19) | collective-permute-done | bytes 139296 | tf_op jit(solution)/shard_map/ppermute | solution.py:280
  42.7 1.8 %collective-permute-done.8.rest_2_ = f32[8,5248]{1,0:T(8,128)S(1)} collective-permute-done((f32[8,5248]{1,0:T(8,128)S(1)}, f32[8,5248]{1,0:T(8,128)S(1)}, u32[]{:S(2)}, u32[]{:S(2)}) %collective-permute-start.8) | collective-permute-done | bytes 167968 | tf_op jit(solution)/shard_map/ppermute | solution.py:280
  44.4 3.2 %collective-permute-done.9.rest_3_ = f32[8,5248]{1,0:T(8,128)S(1)} collective-permute-done((f32[8,5248]{1,0:T(8,128)S(1)}, f32[8,5248]{1,0:T(8,128)S(1)}, u32[]{:S(2)}, u32[]{:S(2)}) %collective-permute-start.9) | collective-permute-done | bytes 167968 | tf_op jit(solution)/shard_map/ppermute | solution.py:280
  48.3 1.8 %pick.3 = (f32[8,4352]{1,0:T(8,128)S(1)}, f32[8,4352]{1,0:T(8,128)}, f32[8,4352]{1,0:T(8,128)S(1)}, f32[8,4352]{1,0:T(8,128)S(1)}) custom-call(s32[1]{0:T(128)} %bitcast.me_ref, s32[2,17]{1,0:T(2,128)} %get-tuple-element.23.plan, f32[1,128]{1,0:T(1,128)} %copy-done.4, f32[8,4352]{1,0:T(8,128)} %copy-done.2, f32[8,4352]{1,0:T(8,128)S(1)} %collective-permute-done.17.rest_1_, ...), custom_call_target="tpu_custom_call" | custom-call | tf_op jit(solution)/shard_map/pick/pallas_call | solution.py:213
  50.7 3.0 %collective-permute-start.25 = (f32[8,4352]{1,0:T(8,128)S(1)}, f32[8,4352]{1,0:T(8,128)S(1)}, u32[]{:S(2)}, u32[]{:S(2)}) collective-permute-start(f32[8,4352]{1,0:T(8,128)S(1)} %get-tuple-element.41), channel_id=1, source_target_pairs={{0,4},{1,5},{2,6},{3,7},{4,0},{5,1},{6,2},{7,3},{8,12},{9,13},{10,... | collective-permute-start | bytes 417800 | tf_op jit(solution)/shard_map/ppermute | solution.py:280
  54.2 1.3 %pick.2 = (f32[8,4480]{1,0:T(8,128)S(1)}, f32[8,4480]{1,0:T(8,128)S(1)}, f32[8,4480]{1,0:T(8,128)S(1)}, f32[8,4480]{1,0:T(8,128)S(1)}) custom-call(s32[1]{0:T(128)} %bitcast.me_ref, s32[2,17]{1,0:T(2,128)} %get-tuple-element.23.plan, f32[1,128]{1,0:T(1,128)} %copy-done.4, f32[8,5248]{1,0:T(8,128)} %copy-done, f32[8,5248]{1,0:T(8,128)S(1)} %collective-permute-done.7.rest_1_, ...), custom_call_target="tpu_custom_call" | custom-call | tf_op jit(solution)/shard_map/pick/pallas_call | solution.py:213
  56.7 1.9 %collective-permute-start.15 = (f32[8,4480]{1,0:T(8,128)S(1)}, f32[8,4480]{1,0:T(8,128)S(1)}, u32[]{:S(2)}, u32[]{:S(2)}) collective-permute-start(f32[8,4480]{1,0:T(8,128)S(1)} %get-tuple-element.33), channel_id=1, source_target_pairs={{0,4},{1,5},{2,6},{3,7},{4,0},{5,1},{6,2},{7,3},{8,12},{9,13},{10,... | collective-permute-start | bytes 430088 | tf_op jit(solution)/shard_map/ppermute | solution.py:280
  59.1 5.4 %multiply_subtract_fusion = (f32[2,4,16,2880]{3,2,1,0:T(8,128)}, f32[2,4,16,2880]{3,2,1,0:T(8,128)}, f32[2,4,16,2880]{3,2,1,0:T(8,128)}) fusion(f32[2,4,16,2880]{3,2,1,0:T(8,128)} %master.1, f32[]{:T(128)S(1)} %bitcast.3, bf16[2,4,16,2880]{3,2,1,0:T(8,128)(2,1)} %grad.1, f32[2,4,16,2880]{3,2,1,0:T(8,128)} %mone.1, f32[2,4,16,2880]{3,2,1,0:T(8,128)} %mtwo.1), kind=kLoop, calls=%fused_computation.2 | loop fusion | flops 6266880 | bytes 9584644 | tf_op jit(solution)/shard_map/sub | solution.py:51
  64.5 9.4 %collective-permute-done.26.rest_7_ = f32[8,4352]{1,0:T(8,128)S(1)} collective-permute-done((f32[8,4352]{1,0:T(8,128)S(1)}, f32[8,4352]{1,0:T(8,128)S(1)}, u32[]{:S(2)}, u32[]{:S(2)}) %collective-permute-start.26) | collective-permute-done | bytes 139296 | tf_op jit(solution)/shard_map/ppermute | solution.py:280
  73.9 2.2 %collective-permute-done.15.rest_2_ = f32[8,4480]{1,0:T(8,128)S(1)} collective-permute-done((f32[8,4480]{1,0:T(8,128)S(1)}, f32[8,4480]{1,0:T(8,128)S(1)}, u32[]{:S(2)}, u32[]{:S(2)}) %collective-permute-start.15) | collective-permute-done | bytes 143392 | tf_op jit(solution)/shard_map/ppermute | solution.py:280
  76.1 3.2 %collective-permute-done.16.rest_3_ = f32[8,4480]{1,0:T(8,128)S(1)} collective-permute-done((f32[8,4480]{1,0:T(8,128)S(1)}, f32[8,4480]{1,0:T(8,128)S(1)}, u32[]{:S(2)}, u32[]{:S(2)}) %collective-permute-start.16) | collective-permute-done | bytes 143392 | tf_op jit(solution)/shard_map/ppermute | solution.py:280
  79.2 2.4 %land.1 = (f32[2,4,16,2880]{3,2,1,0:T(8,128)}, f32[2,4,16,2880]{3,2,1,0:T(8,128)}, f32[2,4,16,2880]{3,2,1,0:T(8,128)}) custom-call(s32[1]{0:T(128)} %bitcast.me_ref, s32[2,17]{1,0:T(2,128)} %get-tuple-element.23.plan, f32[8,4480]{1,0:T(8,128)} %copy-done.1, ...), custom_call_target="tpu_custom_call", output_to_operand_aliasing={{0}: (10, {}), {1}: (11, {}), {2}: (12, {})} | custom-call | tf_op jit(solution)/shard_map/land/pallas_call | solution.py:258
  (51 shorter events, 9.0 us)
Async XLA Ops:
  3.7 4.1 %collective-permute-start.2 = (f32[1,128]{1,0:T(1,128)S(1)}, f32[1,128]{1,0:T(1,128)S(1)}, u32[]{:S(2)}, u32[]{:S(2)}) collective-permute-start(f32[1,128]{1,0:T(1,128)S(1)} %get-tuple-element.24), channel_id=1, source_target_pairs={{0,6},{1,7},{2,4},{3,5},{4,2},{5,3},{6,0},{7,1},{8,14},{9,15},{10,... | collective-permute-start | bytes 1544 | tf_op jit(solution)/shard_map/ppermute | solution.py:280
  5.4 4.5 %collective-permute-start.1 = (f32[1,128]{1,0:T(1,128)S(1)}, f32[1,128]{1,0:T(1,128)S(1)}, u32[]{:S(2)}, u32[]{:S(2)}) collective-permute-start(f32[1,128]{1,0:T(1,128)S(1)} %get-tuple-element.24), channel_id=1, source_target_pairs={{0,4},{1,5},{2,6},{3,7},{4,0},{5,1},{6,2},{7,3},{8,12},{9,13},{10,... | collective-permute-start | bytes 1544 | tf_op jit(solution)/shard_map/ppermute | solution.py:280
  11.4 4.5 %collective-permute-start.6 = (f32[1,128]{1,0:T(1,128)S(1)}, f32[1,128]{1,0:T(1,128)S(1)}, u32[]{:S(2)}, u32[]{:S(2)}) collective-permute-start(f32[1,128]{1,0:T(1,128)S(1)} %add.39), channel_id=1, source_target_pairs={{0,24},{8,16},{16,8},{24,0},{1,25},{9,17},{17,9},{25,1},{2,26},{10... | collective-permute-start | bytes 1544 | tf_op jit(solution)/shard_map/ppermute | solution.py:292
  12.8 3.6 %collective-permute-start.5 = (f32[1,128]{1,0:T(1,128)S(1)}, f32[1,128]{1,0:T(1,128)S(1)}, u32[]{:S(2)}, u32[]{:S(2)}) collective-permute-start(f32[1,128]{1,0:T(1,128)S(1)} %add.39), channel_id=1, source_target_pairs={{0,16},{8,24},{16,0},{24,8},{1,17},{9,25},{17,1},{25,9},{2,18},{10... | collective-permute-start | bytes 1544 | tf_op jit(solution)/shard_map/ppermute | solution.py:292
  18.1 6.8 %collective-permute-start.17 = (f32[8,4352]{1,0:T(8,128)S(1)}, f32[8,4352]{1,0:T(8,128)S(1)}, u32[]{:S(2)}, u32[]{:S(2)}) collective-permute-start(f32[8,4352]{1,0:T(8,128)S(1)} %get-tuple-element.36), channel_id=1, source_target_pairs={{0,2},{1,3},{2,0},{3,1},{4,6},{5,7},{6,4},{7,5},{8,10},{9,11},{10,... | collective-permute-start | bytes 417800 | tf_op jit(solution)/shard_map/ppermute | solution.py:280
  20.4 10.9 %collective-permute-start.18 = (f32[8,4352]{1,0:T(8,128)S(1)}, f32[8,4352]{1,0:T(8,128)S(1)}, u32[]{:S(2)}, u32[]{:S(2)}) collective-permute-start(f32[8,4352]{1,0:T(8,128)S(1)} %get-tuple-element.37), channel_id=1, source_target_pairs={{0,4},{1,5},{2,6},{3,7},{4,0},{5,1},{6,2},{7,3},{8,12},{9,13},{10,... | collective-permute-start | bytes 417800 | tf_op jit(solution)/shard_map/ppermute | solution.py:280
  22.3 19.7 %collective-permute-start.19 = (f32[8,4352]{1,0:T(8,128)S(1)}, f32[8,4352]{1,0:T(8,128)S(1)}, u32[]{:S(2)}, u32[]{:S(2)}) collective-permute-start(f32[8,4352]{1,0:T(8,128)S(1)} %get-tuple-element.38), channel_id=1, source_target_pairs={{0,6},{1,7},{2,4},{3,5},{4,2},{5,3},{6,0},{7,1},{8,14},{9,15},{10,... | collective-permute-start | bytes 417800 | tf_op jit(solution)/shard_map/ppermute | solution.py:280
  22.3 19.8 %collective-permute-start.20 = (f32[8,4352]{1,0:T(8,128)S(1)}, f32[8,4352]{1,0:T(8,128)S(1)}, u32[]{:S(2)}, u32[]{:S(2)}) collective-permute-start(f32[8,4352]{1,0:T(8,128)S(1)} %get-tuple-element.35.rest_0_), channel_id=1, source_target_pairs={{0,1},{1,0},{2,3},{3,2},{4,5},{5,4},{6,7},{7,6},{8,9},{9,8},{10,11... | collective-permute-start | bytes 417800 | tf_op jit(solution)/shard_map/ppermute | solution.py:298
  22.3 20.3 %collective-permute-start.7 = (f32[8,5248]{1,0:T(8,128)S(1)}, f32[8,5248]{1,0:T(8,128)S(1)}, u32[]{:S(2)}, u32[]{:S(2)}) collective-permute-start(f32[8,5248]{1,0:T(8,128)S(1)} %get-tuple-element.28), channel_id=1, source_target_pairs={{0,2},{1,3},{2,0},{3,1},{4,6},{5,7},{6,4},{7,5},{8,10},{9,11},{10,... | collective-permute-start | bytes 503816 | tf_op jit(solution)/shard_map/ppermute | solution.py:280
  24.9 19.5 %collective-permute-start.8 = (f32[8,5248]{1,0:T(8,128)S(1)}, f32[8,5248]{1,0:T(8,128)S(1)}, u32[]{:S(2)}, u32[]{:S(2)}) collective-permute-start(f32[8,5248]{1,0:T(8,128)S(1)} %get-tuple-element.29), channel_id=1, source_target_pairs={{0,4},{1,5},{2,6},{3,7},{4,0},{5,1},{6,2},{7,3},{8,12},{9,13},{10,... | collective-permute-start | bytes 503816 | tf_op jit(solution)/shard_map/ppermute | solution.py:280
  31.3 16.4 %collective-permute-start.9 = (f32[8,5248]{1,0:T(8,128)S(1)}, f32[8,5248]{1,0:T(8,128)S(1)}, u32[]{:S(2)}, u32[]{:S(2)}) collective-permute-start(f32[8,5248]{1,0:T(8,128)S(1)} %get-tuple-element.30), channel_id=1, source_target_pairs={{0,6},{1,7},{2,4},{3,5},{4,2},{5,3},{6,0},{7,1},{8,14},{9,15},{10,... | collective-permute-start | bytes 503816 | tf_op jit(solution)/shard_map/ppermute | solution.py:280
  42.1 5.6 %collective-permute-start.21 = (f32[8,4352]{1,0:T(8,128)S(1)}, f32[8,4352]{1,0:T(8,128)S(1)}, u32[]{:S(2)}, u32[]{:S(2)}) collective-permute-start(f32[8,4352]{1,0:T(8,128)S(1)} %collective-permute-done.17.rest_1_), channel_id=1, source_target_pairs={{0,1},{1,0},{2,3},{3,2},{4,5},{5,4},{6,7},{7,6},{8,9},{9,8},{10,11... | collective-permute-start | bytes 417800 | tf_op jit(solution)/shard_map/ppermute | solution.py:298
  42.1 6.1 %collective-permute-start.22 = (f32[8,4352]{1,0:T(8,128)S(1)}, f32[8,4352]{1,0:T(8,128)S(1)}, u32[]{:S(2)}, u32[]{:S(2)}) collective-permute-start(f32[8,4352]{1,0:T(8,128)S(1)} %collective-permute-done.18.rest_2_), channel_id=1, source_target_pairs={{0,1},{1,0},{2,3},{3,2},{4,5},{5,4},{6,7},{7,6},{8,9},{9,8},{10,11... | collective-permute-start | bytes 417800 | tf_op jit(solution)/shard_map/ppermute | solution.py:298
  42.6 5.7 %collective-permute-start.23 = (f32[8,4352]{1,0:T(8,128)S(1)}, f32[8,4352]{1,0:T(8,128)S(1)}, u32[]{:S(2)}, u32[]{:S(2)}) collective-permute-start(f32[8,4352]{1,0:T(8,128)S(1)} %collective-permute-done.19.rest_3_), channel_id=1, source_target_pairs={{0,1},{1,0},{2,3},{3,2},{4,5},{5,4},{6,7},{7,6},{8,9},{9,8},{10,11... | collective-permute-start | bytes 417800 | tf_op jit(solution)/shard_map/ppermute | solution.py:298
  44.4 6.3 %collective-permute-start.10 = (f32[8,5248]{1,0:T(8,128)S(1)}, f32[8,5248]{1,0:T(8,128)S(1)}, u32[]{:S(2)}, u32[]{:S(2)}) collective-permute-start(f32[8,5248]{1,0:T(8,128)S(1)} %get-tuple-element.27.rest_0_), channel_id=1, source_target_pairs={{0,1},{1,0},{2,3},{3,2},{4,5},{5,4},{6,7},{7,6},{8,9},{9,8},{10,11... | collective-permute-start | bytes 503816 | tf_op jit(solution)/shard_map/ppermute | solution.py:298
  47.6 6.1 %collective-permute-start.11 = (f32[8,5248]{1,0:T(8,128)S(1)}, f32[8,5248]{1,0:T(8,128)S(1)}, u32[]{:S(2)}, u32[]{:S(2)}) collective-permute-start(f32[8,5248]{1,0:T(8,128)S(1)} %collective-permute-done.7.rest_1_), channel_id=1, source_target_pairs={{0,1},{1,0},{2,3},{3,2},{4,5},{5,4},{6,7},{7,6},{8,9},{9,8},{10,11... | collective-permute-start | bytes 503816 | tf_op jit(solution)/shard_map/ppermute | solution.py:298
  47.7 6.6 %collective-permute-start.12 = (f32[8,5248]{1,0:T(8,128)S(1)}, f32[8,5248]{1,0:T(8,128)S(1)}, u32[]{:S(2)}, u32[]{:S(2)}) collective-permute-start(f32[8,5248]{1,0:T(8,128)S(1)} %collective-permute-done.8.rest_2_), channel_id=1, source_target_pairs={{0,1},{1,0},{2,3},{3,2},{4,5},{5,4},{6,7},{7,6},{8,9},{9,8},{10,11... | collective-permute-start | bytes 503816 | tf_op jit(solution)/shard_map/ppermute | solution.py:298
  48.2 6.1 %collective-permute-start.13 = (f32[8,5248]{1,0:T(8,128)S(1)}, f32[8,5248]{1,0:T(8,128)S(1)}, u32[]{:S(2)}, u32[]{:S(2)}) collective-permute-start(f32[8,5248]{1,0:T(8,128)S(1)} %collective-permute-done.9.rest_3_), channel_id=1, source_target_pairs={{0,1},{1,0},{2,3},{3,2},{4,5},{5,4},{6,7},{7,6},{8,9},{9,8},{10,11... | collective-permute-start | bytes 503816 | tf_op jit(solution)/shard_map/ppermute | solution.py:298
  50.7 7.9 %collective-permute-start.24 = (f32[8,4352]{1,0:T(8,128)}, f32[8,4352]{1,0:T(8,128)S(1)}, u32[]{:S(2)}, u32[]{:S(2)}) collective-permute-start(f32[8,4352]{1,0:T(8,128)} %get-tuple-element.40), channel_id=1, source_target_pairs={{0,2},{1,3},{2,0},{3,1},{4,6},{5,7},{6,4},{7,5},{8,10},{9,11},{10,... | collective-permute-start | bytes 417800 | tf_op jit(solution)/shard_map/ppermute | solution.py:280
  50.7 13.8 %collective-permute-start.25 = (f32[8,4352]{1,0:T(8,128)S(1)}, f32[8,4352]{1,0:T(8,128)S(1)}, u32[]{:S(2)}, u32[]{:S(2)}) collective-permute-start(f32[8,4352]{1,0:T(8,128)S(1)} %get-tuple-element.41), channel_id=1, source_target_pairs={{0,4},{1,5},{2,6},{3,7},{4,0},{5,1},{6,2},{7,3},{8,12},{9,13},{10,... | collective-permute-start | bytes 417800 | tf_op jit(solution)/shard_map/ppermute | solution.py:280
  53.8 20.1 %collective-permute-start.26 = (f32[8,4352]{1,0:T(8,128)S(1)}, f32[8,4352]{1,0:T(8,128)S(1)}, u32[]{:S(2)}, u32[]{:S(2)}) collective-permute-start(f32[8,4352]{1,0:T(8,128)S(1)} %get-tuple-element.42), channel_id=1, source_target_pairs={{0,6},{1,7},{2,4},{3,5},{4,2},{5,3},{6,0},{7,1},{8,14},{9,15},{10,... | collective-permute-start | bytes 417800 | tf_op jit(solution)/shard_map/ppermute | solution.py:280
  55.5 18.4 %collective-permute-start.14 = (f32[8,4480]{1,0:T(8,128)S(1)}, f32[8,4480]{1,0:T(8,128)S(1)}, u32[]{:S(2)}, u32[]{:S(2)}) collective-permute-start(f32[8,4480]{1,0:T(8,128)S(1)} %get-tuple-element.32), channel_id=1, source_target_pairs={{0,2},{1,3},{2,0},{3,1},{4,6},{5,7},{6,4},{7,5},{8,10},{9,11},{10,... | collective-permute-start | bytes 430088 | tf_op jit(solution)/shard_map/ppermute | solution.py:280
  56.7 19.4 %collective-permute-start.15 = (f32[8,4480]{1,0:T(8,128)S(1)}, f32[8,4480]{1,0:T(8,128)S(1)}, u32[]{:S(2)}, u32[]{:S(2)}) collective-permute-start(f32[8,4480]{1,0:T(8,128)S(1)} %get-tuple-element.33), channel_id=1, source_target_pairs={{0,4},{1,5},{2,6},{3,7},{4,0},{5,1},{6,2},{7,3},{8,12},{9,13},{10,... | collective-permute-start | bytes 430088 | tf_op jit(solution)/shard_map/ppermute | solution.py:280
  58.6 20.6 %collective-permute-start.16 = (f32[8,4480]{1,0:T(8,128)S(1)}, f32[8,4480]{1,0:T(8,128)S(1)}, u32[]{:S(2)}, u32[]{:S(2)}) collective-permute-start(f32[8,4480]{1,0:T(8,128)S(1)} %get-tuple-element.34), channel_id=1, source_target_pairs={{0,6},{1,7},{2,4},{3,5},{4,2},{5,3},{6,0},{7,1},{8,14},{9,15},{10,... | collective-permute-start | bytes 430088 | tf_op jit(solution)/shard_map/ppermute | solution.py:280
  (9 other events, 139.6 us)

commit v3 on v2

--- a/solution.py
+++ b/solution.py
@@ -57,8 +57,10 @@
         self.group = group
         self.devices = group * dp
         self.chips = group // CORES
+        self.order = [*range(self.chips // 2, self.chips), *range(1, self.chips // 2)]
         self.piece = self.layers * self.rows // self.chips
         self.per_layer = self.rows // self.piece
+        self.by_piece = self.piece % 8 == 0
         early = round(self.cols * EARLY / LANES) * LANES
         self.early = early
         self.late = self.cols - early
@@ -156,12 +158,13 @@
     )(me, old_slot, new_slot, master, mone, mtwo, grad)
 
 
-def scale_kernel(sz, total, raw, clip, *late):
+def scale_kernel(sz, total, raw, clip, clip_copy, *late):
     entries = sz.layers * sz.slots * sz.rows * sz.cols * sz.devices
     scale = jnp.minimum(
         1.0, CLIP_RMS * math.sqrt(entries) / (jnp.sqrt(total[...]) + 1e-06)
     )
     clip[...] = scale
+    clip_copy[...] = scale
     for x in range(sz.chips):
         first, second = moments(raw[0, x], raw[1, x], raw[2, x], scale[:, 0:1])
         late[x][:, : sz.late] = first
@@ -172,8 +175,9 @@
     return pl.pallas_call(
         functools.partial(scale_kernel, sz),
         in_specs=[VMEM, VMEM],
-        out_specs=[VMEM] * (sz.chips + 1),
-        out_shape=[out(1, LANES)] + [out(sz.piece, width(sz.groups[1], 2))] * sz.chips,
+        out_specs=[VMEM] * (sz.chips + 2),
+        out_shape=[out(1, LANES), jax.ShapeDtypeStruct((1, LANES), jnp.float32)]
+        + [out(sz.piece, width(sz.groups[1], 2))] * sz.chips,
         name="scale_late",
     )(*near((total, raw)))
 
@@ -219,71 +223,82 @@
     )(me, plan, clip, *own, *other)
 
 
-def land_kernel(sz, me_ref, plan, *rest):
-    c = sz.chips
-    early, late = rest[:c], rest[c : 2 * c]
-    outs = rest[2 * c + 3 : 2 * c + 6]
-    st, full, sem = rest[2 * c + 6 :]
+def land_kernel(sz, which, me_ref, plan, *rest):
+    c, n = sz.chips, len(which)
+    early, late = rest[:n], rest[n : 2 * n]
+    outs = rest[2 * n + 3 : 2 * n + 6]
+    st, full, sem = rest[2 * n + 6 :]
     me = me_ref[0]
     chip = lax.div(me, CORES)
     e, f = sz.early, sz.full
-    for x in range(c):
+    copies = []
+    for j, x in enumerate(which):
         k = dyn_peer(chip, x, c) if c & (c - 1) == 0 else lax.rem(chip - x + c, c)
-        a, b = early[x], late[x]
+        a, b = early[j], late[j]
+        spot = j if sz.by_piece else k
         first, second = a[:, f : f + e], a[:, f + e : f + 2 * e]
-        st[0, k, :, :e] = new_weights(a[:, :e], first, second)
-        st[1, k, :, :e] = first
-        st[2, k, :, :e] = second
+        st[0, spot, :, :e] = new_weights(a[:, :e], first, second)
+        st[1, spot, :, :e] = first
+        st[2, spot, :, :e] = second
         first, second = b[:, : sz.late], b[:, sz.lat : sz.lat + sz.late]
-        st[0, k, :, e:] = new_weights(a[:, e : sz.cols], first, second)
-        st[1, k, :, e:] = first
-        st[2, k, :, e:] = second
-    copies = []
-    for i in range(sz.layers):
-        slot = plan[1, i * sz.group + me]
-        for a in range(3):
-            for q in range(sz.per_layer):
-                r = slice(q * sz.piece, (q + 1) * sz.piece)
-                full[a, i, r, :] = st[a, i * sz.per_layer + q]
-            cp = pltpu.make_async_copy(full.at[a, i], outs[a].at[i, slot], sem.at[a, i])
-            cp.start()
-            copies.append(cp)
+        st[0, spot, :, e:] = new_weights(a[:, e : sz.cols], first, second)
+        st[1, spot, :, e:] = first
+        st[2, spot, :, e:] = second
+        if sz.by_piece:
+            layer = lax.div(k, sz.per_layer)
+            row = pl.multiple_of(lax.rem(k, sz.per_layer) * sz.piece, sz.piece)
+            slot = plan[1, layer * sz.group + me]
+            for i in range(3):
+                there = outs[i].at[layer, slot, pl.ds(row, sz.piece)]
+                copies.append(pltpu.make_async_copy(st.at[i, j], there, sem.at[i, j]))
+                copies[-1].start()
+    if not sz.by_piece:
+        for i in range(sz.layers):
+            slot = plan[1, i * sz.group + me]
+            for a in range(3):
+                for q in range(sz.per_layer):
+                    r = slice(q * sz.piece, (q + 1) * sz.piece)
+                    full[a, i, r, :] = st[a, i * sz.per_layer + q]
+                copies.append(
+                    pltpu.make_async_copy(full.at[a, i], outs[a].at[i, slot], sem.at[a, i])
+                )
+                copies[-1].start()
     for cp in copies:
         cp.wait()
 
 
-def land(sz, me, plan, early, late, outs):
+def land(sz, which, me, plan, early, late, outs):
     f32 = jnp.float32
-    c = sz.chips
+    n = len(which)
+    whole = (8, LANES) if sz.by_piece else (3, sz.layers, sz.rows, sz.cols)
     return pl.pallas_call(
-        functools.partial(land_kernel, sz),
-        in_specs=[SMEM, SMEM] + [VMEM] * (2 * c) + [ANY] * 3,
+        functools.partial(land_kernel, sz, which),
+        in_specs=[SMEM, SMEM] + [VMEM] * (2 * n) + [ANY] * 3,
         out_specs=[ANY] * 3,
         out_shape=[jax.ShapeDtypeStruct(o.shape, o.dtype) for o in outs],
         scratch_shapes=[
-            pltpu.VMEM((3, c, sz.piece, sz.cols), f32),
-            pltpu.VMEM((3, sz.layers, sz.rows, sz.cols), f32),
-            pltpu.SemaphoreType.DMA((3, sz.layers)),
+            pltpu.VMEM((3, n, sz.piece, sz.cols), f32),
+            pltpu.VMEM(whole, f32),
+            pltpu.SemaphoreType.DMA((3, max(n, sz.layers))),
         ],
-        input_output_aliases={2 + 2 * c + a: a for a in range(3)},
+        input_output_aliases={2 + 2 * n + a: a for a in range(3)},
         name="land",
-    )(me, plan, *early, *late, *outs)
+    )(me, plan, *[early[x] for x in which], *[late[x] for x in which], *outs)
 
 
 def shifts(sz, arrays):
     c = sz.chips
-    got = [arrays[0]]
-    for x in range(1, c):
+    got = [arrays[0]] * c
+    for x in sz.order:
         pairs = [
             (i * CORES + k, peer(i, x, c) * CORES + k) for i in range(c) for k in range(CORES)
         ]
-        got.append(lax.ppermute(arrays[x], "expert", pairs))
+        got[x] = lax.ppermute(arrays[x], "expert", pairs)
     return got
 
 
 def spread(sz, arrays):
-    got = shifts(sz, arrays)
-    return got[:1] + near(got[1:])
+    return near(shifts(sz, arrays))
 
 
 def from_others(value, axis):
@@ -309,7 +324,8 @@
     total = sum(totals)
     total = total + swap(sz, [total])[0]
     total = total + from_others(total, "dp")
-    clip, *late = scale_and_late(sz, total, raw)
+    clip, clip_copy, *late = scale_and_late(sz, total, raw)
+    (clip,) = near([clip])
     late_held = spread(sz, late)
     other = near(swap(sz, held))
     early_out = pick(sz, 0, me, plan, clip, held, other)
@@ -317,11 +333,16 @@
     late_other = near(swap(sz, late_held))
     late_out = pick(sz, 1, me, plan, clip, late_held, late_other)
     late_in = spread(sz, list(late_out))
-    scale = clip[0, 0]
+    scale = clip_copy[0, 0]
     wide = gradient.astype(jnp.float32)
     first, second = moments(moment_one, moment_two, wide, scale)
     weights = new_weights(master, first, second)
-    return tuple(land(sz, me, plan, early_in, late_in, (weights, first, second)))
+    outs = (weights, first, second)
+    half = c // 2
+    batches = [range(half), range(half, c)] if sz.by_piece else [range(c)]
+    for which in batches:
+        outs = land(sz, list(which), me, plan, early_in, late_in, outs)
+    return tuple(outs)
 
 
 def solution(mesh):

time: 82.1 us -> 81 us (0.987)
  waiting for transfers between devices: 42.1 us -> 38.9 us
  starting transfers between devices: 24 us -> 25.9 us
    ppermute x15, waiting for transfers between devices: 37.9 us -> 34.7 us  [shifts(): got[x] = lax.ppermute(arrays[x], 'expert', pairs)]
    ppermute x15, starting transfers between devices: 19.3 us -> 21.2 us  [shifts(): got[x] = lax.ppermute(arrays[x], 'expert', pairs)]
    pallas_call x1 -> x2, Pallas kernels: 2.36 us -> 3.19 us  [land(): pl.pallas_call(functools.partial(land_kernel, sz, which), in_specs=[SMEM,...]
  transfers between devices with their start and end apart: 27 -> 27, of which waited for: 14 -> 15; matrix products, arithmetic and copies ran while one was open for 7% -> 7% of each run, Pallas kernels for 4% -> 5%
where the time goes in v3:
time: 81 us; the launch traced here: 80.5 us
  waiting for transfers between devices  38.9 us (48%)
  starting transfers between devices  25.9 us (32%)
  Pallas kernels  9.47 us (12%)
  other arithmetic  5.48 us (7%)
    ppermute x15, waiting for transfers between devices, shifts(): got[x] = lax.ppermute(arrays[x], 'expert', pairs)  34.7 us
    ppermute x15, starting transfers between devices, shifts(): got[x] = lax.ppermute(arrays[x], 'expert', pairs)  21.2 us
    sub x1, other arithmetic, new_weights(): return master - LEARN_RATE * (step_dir + DECAY_RATE * master)  5.47 us
    ppermute x3, starting transfers between devices, from_others(): lax.ppermute(value, axis, [(i, peer(i, x, n)) for i in range(n)])  3.49 us
    pallas_call x2, Pallas kernels, land(): pl.pallas_call(functools.partial(land_kernel, sz, which), in_specs=[SMEM,...  3.19 us
    pallas_call x1, Pallas kernels, prep(): pl.pallas_call(functools.partial(prep_kernel, sz), in_specs=[SMEM, SMEM,...  3.09 us
    ppermute x3, waiting for transfers between devices, from_others(): lax.ppermute(value, axis, [(i, peer(i, x, n)) for i in range(n)])  3.03 us
    pallas_call x2, Pallas kernels, pick(): pl.pallas_call(functools.partial(pick_kernel, sz, group), in_specs=[SMEM,...  2.67 us
  transfers between devices with their start and end apart: 27, of which 15 were waited for; matrix products, arithmetic and copies ran while one was open for 7% of the time, Pallas kernels for 5%

profile of v3, /device:TPU:12, one launch (start us, length us, event | category | flops | bytes accessed | tf_op | source)
XLA Modules:
  0.0 80.5 jit_solution(17136928587385444182)
XLA Ops:
  0.6 3.1 %prep.1 = (f32[8,5248]{1,0:T(8,128)S(1)}, f32[8,5248]{1,0:T(8,128)S(1)}, f32[8,5248]{1,0:T(8,128)S(1)}, f32[8,5248]{1,0:T(8,128)S(1)}, f32[3,4,8,2112]{3,2,1,0:T...) custom-call(s32[1]{0:T(128)} %bitcast.me_ref, s32[2,32]{1,0:T(2,128)} %old_ref.1, s32[2,32]{1,0:T(2,128)} %new_ref.1, ...), custom_call_target="tpu_custom_call" | custom-call | tf_op jit(solution)/shard_map/prep/pallas_call | solution.py:143
  3.7 1.6 %collective-permute-start.2 = (f32[1,128]{1,0:T(1,128)S(1)}, f32[1,128]{1,0:T(1,128)S(1)}, u32[]{:S(2)}, u32[]{:S(2)}) collective-permute-start(f32[1,128]{1,0:T(1,128)S(1)} %get-tuple-element.28), channel_id=1, source_target_pairs={{0,6},{1,7},{2,4},{3,5},{4,2},{5,3},{6,0},{7,1},{8,14},{9,15},{10,... | collective-permute-start | bytes 1544 | tf_op jit(solution)/shard_map/ppermute | solution.py:296
  7.9 2.0 %collective-permute-done.1 = f32[1,128]{1,0:T(1,128)S(1)} collective-permute-done((f32[1,128]{1,0:T(1,128)S(1)}, f32[1,128]{1,0:T(1,128)S(1)}, u32[]{:S(2)}, u32[]{:S(2)}) %collective-permute-start.1) | collective-permute-done | bytes 544 | tf_op jit(solution)/shard_map/ppermute | solution.py:296
  11.3 1.4 %collective-permute-start.6 = (f32[1,128]{1,0:T(1,128)S(1)}, f32[1,128]{1,0:T(1,128)S(1)}, u32[]{:S(2)}, u32[]{:S(2)}) collective-permute-start(f32[1,128]{1,0:T(1,128)S(1)} %add.39), channel_id=1, source_target_pairs={{0,24},{8,16},{16,8},{24,0},{1,25},{9,17},{17,9},{25,1},{2,26},{10... | collective-permute-start | bytes 1544 | tf_op jit(solution)/shard_map/ppermute | solution.py:307
  12.8 1.5 %collective-permute-start.5 = (f32[1,128]{1,0:T(1,128)S(1)}, f32[1,128]{1,0:T(1,128)S(1)}, u32[]{:S(2)}, u32[]{:S(2)}) collective-permute-start(f32[1,128]{1,0:T(1,128)S(1)} %add.39), channel_id=1, source_target_pairs={{0,16},{8,24},{16,0},{24,8},{1,17},{9,25},{17,1},{25,9},{2,18},{10... | collective-permute-start | bytes 1544 | tf_op jit(solution)/shard_map/ppermute | solution.py:307
  16.4 1.5 %collective-permute-done.4 = f32[1,128]{1,0:T(1,128)S(1)} collective-permute-done((f32[1,128]{1,0:T(1,128)S(1)}, f32[1,128]{1,0:T(1,128)S(1)}, u32[]{:S(2)}, u32[]{:S(2)}) %collective-permute-start.4) | collective-permute-done | bytes 544 | tf_op jit(solution)/shard_map/ppermute | solution.py:307
  18.4 2.2 %collective-permute-start.16 = (f32[8,4352]{1,0:T(8,128)S(1)}, f32[8,4352]{1,0:T(8,128)S(1)}, u32[]{:S(2)}, u32[]{:S(2)}) collective-permute-start(f32[8,4352]{1,0:T(8,128)S(1)} %get-tuple-element.38), channel_id=1, source_target_pairs={{0,2},{1,3},{2,0},{3,1},{4,6},{5,7},{6,4},{7,5},{8,10},{9,11},{10,... | collective-permute-start | bytes 417800 | tf_op jit(solution)/shard_map/ppermute | solution.py:296
  20.6 2.0 %collective-permute-start.17 = (f32[8,4352]{1,0:T(8,128)S(1)}, f32[8,4352]{1,0:T(8,128)S(1)}, u32[]{:S(2)}, u32[]{:S(2)}) collective-permute-start(f32[8,4352]{1,0:T(8,128)S(1)} %get-tuple-element.39), channel_id=1, source_target_pairs={{0,4},{1,5},{2,6},{3,7},{4,0},{5,1},{6,2},{7,3},{8,12},{9,13},{10,... | collective-permute-start | bytes 417800 | tf_op jit(solution)/shard_map/ppermute | solution.py:296
  22.6 2.4 %collective-permute-start.7 = (f32[8,5248]{1,0:T(8,128)S(1)}, f32[8,5248]{1,0:T(8,128)S(1)}, u32[]{:S(2)}, u32[]{:S(2)}) collective-permute-start(f32[8,5248]{1,0:T(8,128)S(1)} %get-tuple-element.32), channel_id=1, source_target_pairs={{0,2},{1,3},{2,0},{3,1},{4,6},{5,7},{6,4},{7,5},{8,10},{9,11},{10,... | collective-permute-start | bytes 503816 | tf_op jit(solution)/shard_map/ppermute | solution.py:296
  25.1 2.6 %collective-permute-start.8 = (f32[8,5248]{1,0:T(8,128)S(1)}, f32[8,5248]{1,0:T(8,128)S(1)}, u32[]{:S(2)}, u32[]{:S(2)}) collective-permute-start(f32[8,5248]{1,0:T(8,128)S(1)} %get-tuple-element.33), channel_id=1, source_target_pairs={{0,4},{1,5},{2,6},{3,7},{4,0},{5,1},{6,2},{7,3},{8,12},{9,13},{10,... | collective-permute-start | bytes 503816 | tf_op jit(solution)/shard_map/ppermute | solution.py:296
  27.7 3.9 %collective-permute-done.17.rest_2_ = f32[8,4352]{1,0:T(8,128)S(1)} collective-permute-done((f32[8,4352]{1,0:T(8,128)S(1)}, f32[8,4352]{1,0:T(8,128)S(1)}, u32[]{:S(2)}, u32[]{:S(2)}) %collective-permute-start.17) | collective-permute-done | bytes 139296 | tf_op jit(solution)/shard_map/ppermute | solution.py:296
  31.6 10.7 %collective-permute-done.18.rest_3_ = f32[8,4352]{1,0:T(8,128)S(1)} collective-permute-done((f32[8,4352]{1,0:T(8,128)S(1)}, f32[8,4352]{1,0:T(8,128)S(1)}, u32[]{:S(2)}, u32[]{:S(2)}) %collective-permute-start.18) | collective-permute-done | bytes 139296 | tf_op jit(solution)/shard_map/ppermute | solution.py:296
  42.9 1.7 %collective-permute-done.8.rest_2_ = f32[8,5248]{1,0:T(8,128)S(1)} collective-permute-done((f32[8,5248]{1,0:T(8,128)S(1)}, f32[8,5248]{1,0:T(8,128)S(1)}, u32[]{:S(2)}, u32[]{:S(2)}) %collective-permute-start.8) | collective-permute-done | bytes 167968 | tf_op jit(solution)/shard_map/ppermute | solution.py:296
  44.6 3.3 %collective-permute-done.9.rest_3_ = f32[8,5248]{1,0:T(8,128)S(1)} collective-permute-done((f32[8,5248]{1,0:T(8,128)S(1)}, f32[8,5248]{1,0:T(8,128)S(1)}, u32[]{:S(2)}, u32[]{:S(2)}) %collective-permute-start.9) | collective-permute-done | bytes 167968 | tf_op jit(solution)/shard_map/ppermute | solution.py:296
  48.5 1.6 %pick.3 = (f32[8,4352]{1,0:T(8,128)S(1)}, f32[8,4352]{1,0:T(8,128)}, f32[8,4352]{1,0:T(8,128)}, f32[8,4352]{1,0:T(8,128)}) custom-call(s32[1]{0:T(128)} %bitcast.me_ref, s32[2,17]{1,0:T(2,128)} %get-tuple-element.27.plan, f32[1,128]{1,0:T(1,128)S(1)} %get-tuple-element.30.clip, f32[8,4352]{1,0:T(8,128)S(1)} %get-tuple-element.37.rest_0_, ...), custom_call_target="tpu_custom_call" | custom-call | tf_op jit(solution)/shard_map/pick/pallas_call | solution.py:217
  50.2 3.0 %collective-permute-start.23 = (f32[8,4352]{1,0:T(8,128)}, f32[8,4352]{1,0:T(8,128)S(1)}, u32[]{:S(2)}, u32[]{:S(2)}) collective-permute-start(f32[8,4352]{1,0:T(8,128)} %get-tuple-element.41), channel_id=1, source_target_pairs={{0,4},{1,5},{2,6},{3,7},{4,0},{5,1},{6,2},{7,3},{8,12},{9,13},{10,... | collective-permute-start | bytes 417800 | tf_op jit(solution)/shard_map/ppermute | solution.py:296
  54.7 2.0 %collective-permute-start.14 = (f32[8,4480]{1,0:T(8,128)S(1)}, f32[8,4480]{1,0:T(8,128)S(1)}, u32[]{:S(2)}, u32[]{:S(2)}) collective-permute-start(f32[8,4480]{1,0:T(8,128)S(1)} %get-tuple-element.35), channel_id=1, source_target_pairs={{0,4},{1,5},{2,6},{3,7},{4,0},{5,1},{6,2},{7,3},{8,12},{9,13},{10,... | collective-permute-start | bytes 430088 | tf_op jit(solution)/shard_map/ppermute | solution.py:296
  57.3 1.9 %collective-permute-start.25 = (f32[8,4480]{1,0:T(8,128)S(1)}, f32[8,4480]{1,0:T(8,128)S(1)}, u32[]{:S(2)}, u32[]{:S(2)}) collective-permute-start(f32[8,4480]{1,0:T(8,128)S(1)} %get-tuple-element.44), channel_id=1, source_target_pairs={{0,2},{1,3},{2,0},{3,1},{4,6},{5,7},{6,4},{7,5},{8,10},{9,11},{10,... | collective-permute-start | bytes 430088 | tf_op jit(solution)/shard_map/ppermute | solution.py:296
  59.1 5.5 %multiply_subtract_fusion = (f32[2,4,16,2880]{3,2,1,0:T(8,128)}, f32[2,4,16,2880]{3,2,1,0:T(8,128)}, f32[2,4,16,2880]{3,2,1,0:T(8,128)}) fusion(f32[2,4,16,2880]{3,2,1,0:T(8,128)} %master.1, f32[]{:T(128)S(1)} %bitcast.3, bf16[2,4,16,2880]{3,2,1,0:T(8,128)(2,1)} %grad.1, f32[2,4,16,2880]{3,2,1,0:T(8,128)} %mone.1, f32[2,4,16,2880]{3,2,1,0:T(8,128)} %mtwo.1), kind=kLoop, calls=%fused_computation.2 | loop fusion | flops 6266880 | bytes 9584644 | tf_op jit(solution)/shard_map/sub | solution.py:51
  64.6 7.0 %collective-permute-done.25.rest_1_ = f32[8,4480]{1,0:T(8,128)S(1)} collective-permute-done((f32[8,4480]{1,0:T(8,128)S(1)}, f32[8,4480]{1,0:T(8,128)S(1)}, u32[]{:S(2)}, u32[]{:S(2)}) %collective-permute-start.25) | collective-permute-done | bytes 143392 | tf_op jit(solution)/shard_map/ppermute | solution.py:296
  71.7 1.6 %land.2 = (f32[2,4,16,2880]{3,2,1,0:T(8,128)}, f32[2,4,16,2880]{3,2,1,0:T(8,128)}, f32[2,4,16,2880]{3,2,1,0:T(8,128)}) custom-call(s32[1]{0:T(128)} %bitcast.me_ref, s32[2,17]{1,0:T(2,128)} %get-tuple-element.27.plan, f32[8,4480]{1,0:T(8,128)S(1)} %get-tuple-element.43.rest_0_, ...), custom_call_target="tpu_custom_call", output_to_operand_aliasing={{0}: (6, {}), {1}: (7, {}), {2}: (8, {})} | custom-call | tf_op jit(solution)/shard_map/land/pallas_call | solution.py:274
  73.6 2.1 %collective-permute-done.14.rest_0_ = f32[8,4480]{1,0:T(8,128)S(1)} collective-permute-done((f32[8,4480]{1,0:T(8,128)S(1)}, f32[8,4480]{1,0:T(8,128)S(1)}, u32[]{:S(2)}, u32[]{:S(2)}) %collective-permute-start.14) | collective-permute-done | bytes 143392 | tf_op jit(solution)/shard_map/ppermute | solution.py:296
  75.7 3.2 %collective-permute-done.15.rest_1_ = f32[8,4480]{1,0:T(8,128)S(1)} collective-permute-done((f32[8,4480]{1,0:T(8,128)S(1)}, f32[8,4480]{1,0:T(8,128)S(1)}, u32[]{:S(2)}, u32[]{:S(2)}) %collective-permute-start.15) | collective-permute-done | bytes 143392 | tf_op jit(solution)/shard_map/ppermute | solution.py:296
  78.9 1.6 %land.3 = (f32[2,4,16,2880]{3,2,1,0:T(8,128)}, f32[2,4,16,2880]{3,2,1,0:T(8,128)}, f32[2,4,16,2880]{3,2,1,0:T(8,128)}) custom-call(s32[1]{0:T(128)} %bitcast.me_ref, s32[2,17]{1,0:T(2,128)} %get-tuple-element.27.plan, f32[8,4480]{1,0:T(8,128)S(1)} %collective-permute-done.14.rest_0_, ...), custom_call_target="tpu_custom_call", output_to_operand_aliasing={{0}: (6, {}), {1}: (7, {}), {2}: (8, {})} | custom-call | tf_op jit(solution)/shard_map/land/pallas_call | solution.py:274
  (46 shorter events, 10.3 us)
Async XLA Ops:
  3.7 4.1 %collective-permute-start.2 = (f32[1,128]{1,0:T(1,128)S(1)}, f32[1,128]{1,0:T(1,128)S(1)}, u32[]{:S(2)}, u32[]{:S(2)}) collective-permute-start(f32[1,128]{1,0:T(1,128)S(1)} %get-tuple-element.28), channel_id=1, source_target_pairs={{0,6},{1,7},{2,4},{3,5},{4,2},{5,3},{6,0},{7,1},{8,14},{9,15},{10,... | collective-permute-start | bytes 1544 | tf_op jit(solution)/shard_map/ppermute | solution.py:296
  5.4 4.5 %collective-permute-start.1 = (f32[1,128]{1,0:T(1,128)S(1)}, f32[1,128]{1,0:T(1,128)S(1)}, u32[]{:S(2)}, u32[]{:S(2)}) collective-permute-start(f32[1,128]{1,0:T(1,128)S(1)} %get-tuple-element.28), channel_id=1, source_target_pairs={{0,4},{1,5},{2,6},{3,7},{4,0},{5,1},{6,2},{7,3},{8,12},{9,13},{10,... | collective-permute-start | bytes 1544 | tf_op jit(solution)/shard_map/ppermute | solution.py:296
  6.6 3.6 %collective-permute-start = (f32[1,128]{1,0:T(1,128)S(1)}, f32[1,128]{1,0:T(1,128)S(1)}, u32[]{:S(2)}, u32[]{:S(2)}) collective-permute-start(f32[1,128]{1,0:T(1,128)S(1)} %get-tuple-element.28), channel_id=1, source_target_pairs={{0,2},{1,3},{2,0},{3,1},{4,6},{5,7},{6,4},{7,5},{8,10},{9,11},{10,... | collective-permute-start | bytes 1544 | tf_op jit(solution)/shard_map/ppermute | solution.py:296
  11.3 4.5 %collective-permute-start.6 = (f32[1,128]{1,0:T(1,128)S(1)}, f32[1,128]{1,0:T(1,128)S(1)}, u32[]{:S(2)}, u32[]{:S(2)}) collective-permute-start(f32[1,128]{1,0:T(1,128)S(1)} %add.39), channel_id=1, source_target_pairs={{0,24},{8,16},{16,8},{24,0},{1,25},{9,17},{17,9},{25,1},{2,26},{10... | collective-permute-start | bytes 1544 | tf_op jit(solution)/shard_map/ppermute | solution.py:307
  18.4 6.7 %collective-permute-start.16 = (f32[8,4352]{1,0:T(8,128)S(1)}, f32[8,4352]{1,0:T(8,128)S(1)}, u32[]{:S(2)}, u32[]{:S(2)}) collective-permute-start(f32[8,4352]{1,0:T(8,128)S(1)} %get-tuple-element.38), channel_id=1, source_target_pairs={{0,2},{1,3},{2,0},{3,1},{4,6},{5,7},{6,4},{7,5},{8,10},{9,11},{10,... | collective-permute-start | bytes 417800 | tf_op jit(solution)/shard_map/ppermute | solution.py:296
  20.6 11.0 %collective-permute-start.17 = (f32[8,4352]{1,0:T(8,128)S(1)}, f32[8,4352]{1,0:T(8,128)S(1)}, u32[]{:S(2)}, u32[]{:S(2)}) collective-permute-start(f32[8,4352]{1,0:T(8,128)S(1)} %get-tuple-element.39), channel_id=1, source_target_pairs={{0,4},{1,5},{2,6},{3,7},{4,0},{5,1},{6,2},{7,3},{8,12},{9,13},{10,... | collective-permute-start | bytes 417800 | tf_op jit(solution)/shard_map/ppermute | solution.py:296
  22.6 19.7 %collective-permute-start.18 = (f32[8,4352]{1,0:T(8,128)S(1)}, f32[8,4352]{1,0:T(8,128)S(1)}, u32[]{:S(2)}, u32[]{:S(2)}) collective-permute-start(f32[8,4352]{1,0:T(8,128)S(1)} %get-tuple-element.40), channel_id=1, source_target_pairs={{0,6},{1,7},{2,4},{3,5},{4,2},{5,3},{6,0},{7,1},{8,14},{9,15},{10,... | collective-permute-start | bytes 417800 | tf_op jit(solution)/shard_map/ppermute | solution.py:296
  22.6 19.8 %collective-permute-start.19 = (f32[8,4352]{1,0:T(8,128)S(1)}, f32[8,4352]{1,0:T(8,128)S(1)}, u32[]{:S(2)}, u32[]{:S(2)}) collective-permute-start(f32[8,4352]{1,0:T(8,128)S(1)} %get-tuple-element.37.rest_0_), channel_id=1, source_target_pairs={{0,1},{1,0},{2,3},{3,2},{4,5},{5,4},{6,7},{7,6},{8,9},{9,8},{10,11... | collective-permute-start | bytes 417800 | tf_op jit(solution)/shard_map/ppermute | solution.py:313
  22.6 20.3 %collective-permute-start.7 = (f32[8,5248]{1,0:T(8,128)S(1)}, f32[8,5248]{1,0:T(8,128)S(1)}, u32[]{:S(2)}, u32[]{:S(2)}) collective-permute-start(f32[8,5248]{1,0:T(8,128)S(1)} %get-tuple-element.32), channel_id=1, source_target_pairs={{0,2},{1,3},{2,0},{3,1},{4,6},{5,7},{6,4},{7,5},{8,10},{9,11},{10,... | collective-permute-start | bytes 503816 | tf_op jit(solution)/shard_map/ppermute | solution.py:296
  25.1 19.5 %collective-permute-start.8 = (f32[8,5248]{1,0:T(8,128)S(1)}, f32[8,5248]{1,0:T(8,128)S(1)}, u32[]{:S(2)}, u32[]{:S(2)}) collective-permute-start(f32[8,5248]{1,0:T(8,128)S(1)} %get-tuple-element.33), channel_id=1, source_target_pairs={{0,4},{1,5},{2,6},{3,7},{4,0},{5,1},{6,2},{7,3},{8,12},{9,13},{10,... | collective-permute-start | bytes 503816 | tf_op jit(solution)/shard_map/ppermute | solution.py:296
  31.6 16.3 %collective-permute-start.9 = (f32[8,5248]{1,0:T(8,128)S(1)}, f32[8,5248]{1,0:T(8,128)S(1)}, u32[]{:S(2)}, u32[]{:S(2)}) collective-permute-start(f32[8,5248]{1,0:T(8,128)S(1)} %get-tuple-element.34), channel_id=1, source_target_pairs={{0,6},{1,7},{2,4},{3,5},{4,2},{5,3},{6,0},{7,1},{8,14},{9,15},{10,... | collective-permute-start | bytes 503816 | tf_op jit(solution)/shard_map/ppermute | solution.py:296
  42.3 5.6 %collective-permute-start.20 = (f32[8,4352]{1,0:T(8,128)S(1)}, f32[8,4352]{1,0:T(8,128)S(1)}, u32[]{:S(2)}, u32[]{:S(2)}) collective-permute-start(f32[8,4352]{1,0:T(8,128)S(1)} %collective-permute-done.16.rest_1_), channel_id=1, source_target_pairs={{0,1},{1,0},{2,3},{3,2},{4,5},{5,4},{6,7},{7,6},{8,9},{9,8},{10,11... | collective-permute-start | bytes 417800 | tf_op jit(solution)/shard_map/ppermute | solution.py:313
  42.3 6.1 %collective-permute-start.21 = (f32[8,4352]{1,0:T(8,128)S(1)}, f32[8,4352]{1,0:T(8,128)S(1)}, u32[]{:S(2)}, u32[]{:S(2)}) collective-permute-start(f32[8,4352]{1,0:T(8,128)S(1)} %collective-permute-done.17.rest_2_), channel_id=1, source_target_pairs={{0,1},{1,0},{2,3},{3,2},{4,5},{5,4},{6,7},{7,6},{8,9},{9,8},{10,11... | collective-permute-start | bytes 417800 | tf_op jit(solution)/shard_map/ppermute | solution.py:313
  42.8 5.7 %collective-permute-start.22 = (f32[8,4352]{1,0:T(8,128)S(1)}, f32[8,4352]{1,0:T(8,128)S(1)}, u32[]{:S(2)}, u32[]{:S(2)}) collective-permute-start(f32[8,4352]{1,0:T(8,128)S(1)} %collective-permute-done.18.rest_3_), channel_id=1, source_target_pairs={{0,1},{1,0},{2,3},{3,2},{4,5},{5,4},{6,7},{7,6},{8,9},{9,8},{10,11... | collective-permute-start | bytes 417800 | tf_op jit(solution)/shard_map/ppermute | solution.py:313
  44.6 5.5 %collective-permute-start.10 = (f32[8,5248]{1,0:T(8,128)S(1)}, f32[8,5248]{1,0:T(8,128)S(1)}, u32[]{:S(2)}, u32[]{:S(2)}) collective-permute-start(f32[8,5248]{1,0:T(8,128)S(1)} %get-tuple-element.31.rest_0_), channel_id=1, source_target_pairs={{0,1},{1,0},{2,3},{3,2},{4,5},{5,4},{6,7},{7,6},{8,9},{9,8},{10,11... | collective-permute-start | bytes 503816 | tf_op jit(solution)/shard_map/ppermute | solution.py:313
  47.9 5.2 %collective-permute-start.11 = (f32[8,5248]{1,0:T(8,128)S(1)}, f32[8,5248]{1,0:T(8,128)S(1)}, u32[]{:S(2)}, u32[]{:S(2)}) collective-permute-start(f32[8,5248]{1,0:T(8,128)S(1)} %collective-permute-done.7.rest_1_), channel_id=1, source_target_pairs={{0,1},{1,0},{2,3},{3,2},{4,5},{5,4},{6,7},{7,6},{8,9},{9,8},{10,11... | collective-permute-start | bytes 503816 | tf_op jit(solution)/shard_map/ppermute | solution.py:313
  47.9 5.7 %collective-permute-start.12 = (f32[8,5248]{1,0:T(8,128)S(1)}, f32[8,5248]{1,0:T(8,128)S(1)}, u32[]{:S(2)}, u32[]{:S(2)}) collective-permute-start(f32[8,5248]{1,0:T(8,128)S(1)} %collective-permute-done.8.rest_2_), channel_id=1, source_target_pairs={{0,1},{1,0},{2,3},{3,2},{4,5},{5,4},{6,7},{7,6},{8,9},{9,8},{10,11... | collective-permute-start | bytes 503816 | tf_op jit(solution)/shard_map/ppermute | solution.py:313
  48.4 5.2 %collective-permute-start.13 = (f32[8,5248]{1,0:T(8,128)S(1)}, f32[8,5248]{1,0:T(8,128)S(1)}, u32[]{:S(2)}, u32[]{:S(2)}) collective-permute-start(f32[8,5248]{1,0:T(8,128)S(1)} %collective-permute-done.9.rest_3_), channel_id=1, source_target_pairs={{0,1},{1,0},{2,3},{3,2},{4,5},{5,4},{6,7},{7,6},{8,9},{9,8},{10,11... | collective-permute-start | bytes 503816 | tf_op jit(solution)/shard_map/ppermute | solution.py:313
  50.2 7.1 %collective-permute-start.26 = (f32[8,4352]{1,0:T(8,128)}, f32[8,4352]{1,0:T(8,128)S(1)}, u32[]{:S(2)}, u32[]{:S(2)}) collective-permute-start(f32[8,4352]{1,0:T(8,128)} %get-tuple-element.46), channel_id=1, source_target_pairs={{0,2},{1,3},{2,0},{3,1},{4,6},{5,7},{6,4},{7,5},{8,10},{9,11},{10,... | collective-permute-start | bytes 417800 | tf_op jit(solution)/shard_map/ppermute | solution.py:296
  50.2 23.1 %collective-permute-start.23 = (f32[8,4352]{1,0:T(8,128)}, f32[8,4352]{1,0:T(8,128)S(1)}, u32[]{:S(2)}, u32[]{:S(2)}) collective-permute-start(f32[8,4352]{1,0:T(8,128)} %get-tuple-element.41), channel_id=1, source_target_pairs={{0,4},{1,5},{2,6},{3,7},{4,0},{5,1},{6,2},{7,3},{8,12},{9,13},{10,... | collective-permute-start | bytes 417800 | tf_op jit(solution)/shard_map/ppermute | solution.py:296
  53.2 20.4 %collective-permute-start.24 = (f32[8,4352]{1,0:T(8,128)}, f32[8,4352]{1,0:T(8,128)S(1)}, u32[]{:S(2)}, u32[]{:S(2)}) collective-permute-start(f32[8,4352]{1,0:T(8,128)} %get-tuple-element.42), channel_id=1, source_target_pairs={{0,6},{1,7},{2,4},{3,5},{4,2},{5,3},{6,0},{7,1},{8,14},{9,15},{10,... | collective-permute-start | bytes 417800 | tf_op jit(solution)/shard_map/ppermute | solution.py:296
  54.7 21.0 %collective-permute-start.14 = (f32[8,4480]{1,0:T(8,128)S(1)}, f32[8,4480]{1,0:T(8,128)S(1)}, u32[]{:S(2)}, u32[]{:S(2)}) collective-permute-start(f32[8,4480]{1,0:T(8,128)S(1)} %get-tuple-element.35), channel_id=1, source_target_pairs={{0,4},{1,5},{2,6},{3,7},{4,0},{5,1},{6,2},{7,3},{8,12},{9,13},{10,... | collective-permute-start | bytes 430088 | tf_op jit(solution)/shard_map/ppermute | solution.py:296
  56.7 22.2 %collective-permute-start.15 = (f32[8,4480]{1,0:T(8,128)S(1)}, f32[8,4480]{1,0:T(8,128)S(1)}, u32[]{:S(2)}, u32[]{:S(2)}) collective-permute-start(f32[8,4480]{1,0:T(8,128)S(1)} %get-tuple-element.36), channel_id=1, source_target_pairs={{0,6},{1,7},{2,4},{3,5},{4,2},{5,3},{6,0},{7,1},{8,14},{9,15},{10,... | collective-permute-start | bytes 430088 | tf_op jit(solution)/shard_map/ppermute | solution.py:296
  57.3 14.4 %collective-permute-start.25 = (f32[8,4480]{1,0:T(8,128)S(1)}, f32[8,4480]{1,0:T(8,128)S(1)}, u32[]{:S(2)}, u32[]{:S(2)}) collective-permute-start(f32[8,4480]{1,0:T(8,128)S(1)} %get-tuple-element.44), channel_id=1, source_target_pairs={{0,2},{1,3},{2,0},{3,1},{4,6},{5,7},{6,4},{7,5},{8,10},{9,11},{10,... | collective-permute-start | bytes 430088 | tf_op jit(solution)/shard_map/ppermute | solution.py:296
  (6 other events, 66.1 us)

commit v4 on v3

--- a/solution.py
+++ b/solution.py
@@ -20,7 +20,7 @@
 
 LANES = 128
 CORES = 2
-EARLY = 0.25
+EARLY = 0.18
 
 ANY = pl.BlockSpec(memory_space=pl.ANY)
 SMEM = pl.BlockSpec(memory_space=pltpu.SMEM)
@@ -64,7 +64,7 @@
         early = round(self.cols * EARLY / LANES) * LANES
         self.early = early
         self.late = self.cols - early
-        self.lat = up(self.late)
+        self.lat = self.late if self.late % (LANES // 2) == 0 else up(self.late)
         self.full = up(self.cols)
         self.groups = ((self.full, 0, early, early), (0, early, self.late, self.lat))
 
@@ -74,6 +74,11 @@
     return head + parts * stride
 
 
+def read(note, place):
+    lane = lax.broadcasted_iota(jnp.int32, note.shape, 1)
+    return jnp.max(jnp.where(lane == place, note[...], 0))
+
+
 def peer(i, x, n):
     return i ^ x if n & (n - 1) == 0 else (i + x) % n
 
@@ -85,9 +90,7 @@
 def prep_kernel(sz, me_ref, old_ref, new_ref, master, mone, mtwo, grad, *rest):
     c = sz.chips
     pieces = rest[:c]
-    late_raw, total, plan, mv, m1v, m2v, gv, st, sem_g, sem = rest[c:]
-    for i in range(sz.layers):
-        pltpu.make_async_copy(grad.at[i], gv.at[i], sem_g.at[i]).start()
+    late_raw, notes, plan, mv, m1v, m2v, gv, st, sem = rest[c:]
     me = me_ref[0]
     chip = lax.div(me, CORES)
     n_slots = sz.layers * sz.group
@@ -103,19 +106,12 @@
 
         lax.fori_loop(0, old_ref.shape[1], note, 0, unroll=8)
         slot = plan[1, i * sz.group + me]
-        for a, (src, dst) in enumerate(((master, mv), (mone, m1v), (mtwo, m2v))):
+        for a, (src, dst) in enumerate(((master, mv), (mone, m1v), (mtwo, m2v), (grad, gv))):
             pltpu.make_async_copy(src.at[i, slot], dst.at[i], sem.at[i, a]).start()
-    acc = jnp.zeros((sz.rows, sz.cols), jnp.float32)
     for i in range(sz.layers):
-        pltpu.make_async_copy(grad.at[i], gv.at[i], sem_g.at[i]).wait()
-        for s in range(sz.slots):
-            x = gv[i, s].astype(jnp.float32)
-            acc = acc + x * x
-    total[...] = jnp.broadcast_to(jnp.sum(acc), total.shape)
-    for i in range(sz.layers):
-        for a, (src, dst) in enumerate(((master, mv), (mone, m1v), (mtwo, m2v))):
+        for a, (src, dst) in enumerate(((master, mv), (mone, m1v), (mtwo, m2v), (grad, gv))):
             pltpu.make_async_copy(src.at[i, 0], dst.at[i], sem.at[i, a]).wait()
-        g = gv[i, plan[1, i * sz.group + me]].astype(jnp.float32)
+        g = gv[i].astype(jnp.float32)
         for q in range(sz.per_layer):
             k = i * sz.per_layer + q
             r = slice(q * sz.piece, (q + 1) * sz.piece)
@@ -123,6 +119,13 @@
             st[1, k] = m1v[i, r, :]
             st[2, k] = m2v[i, r, :]
             st[3, k] = g[r, :]
+    lane = lax.broadcasted_iota(jnp.int32, notes.shape, 1)
+    table = jnp.where(lane == n_slots + sz.layers, me, 0)
+    for i in range(n_slots):
+        table = jnp.where(lane == i, plan[0, i], table)
+    for i in range(sz.layers):
+        table = jnp.where(lane == n_slots + i, plan[1, i * sz.group + me], table)
+    notes[...] = table
     for x in range(c):
         k = dyn_peer(chip, x, c)
         pieces[x][:, : sz.cols] = st[0, k]
@@ -137,25 +140,51 @@
     slot = (sz.layers, sz.rows, sz.cols)
     outs = [out(sz.piece, width(sz.groups[0], 3))] * sz.chips + [
         out(3, sz.chips, sz.piece, sz.late),
-        out(1, LANES),
-        jax.ShapeDtypeStruct((2, sz.layers * sz.group + 1), jnp.int32),
+        out(1, up(sz.layers * (sz.group + 1) + 1), dtype=jnp.int32),
     ]
     return pl.pallas_call(
         functools.partial(prep_kernel, sz),
         in_specs=[SMEM, SMEM, SMEM, ANY, ANY, ANY, ANY],
-        out_specs=[VMEM] * (sz.chips + 2) + [SMEM],
+        out_specs=[VMEM] * (sz.chips + 2),
         out_shape=outs,
         scratch_shapes=[
+            pltpu.SMEM((2, sz.layers * sz.group + 1), jnp.int32),
             pltpu.VMEM(slot, f32),
             pltpu.VMEM(slot, f32),
             pltpu.VMEM(slot, f32),
-            pltpu.VMEM(grad.shape, grad.dtype),
+            pltpu.VMEM(slot, grad.dtype),
             pltpu.VMEM((4, sz.chips, sz.piece, sz.cols), f32),
-            pltpu.SemaphoreType.DMA((sz.layers,)),
-            pltpu.SemaphoreType.DMA((sz.layers, 3)),
+            pltpu.SemaphoreType.DMA((sz.layers, 4)),
         ],
         name="prep",
     )(me, old_slot, new_slot, master, mone, mtwo, grad)
+
+
+def square_kernel(sz, grad, total, gv, sem):
+    copies = [pltpu.make_async_copy(grad.at[i], gv.at[i], sem.at[i]) for i in range(sz.layers)]
+    for cp in copies:
+        cp.start()
+    acc = jnp.zeros((sz.rows, sz.cols), jnp.float32)
+    for i in range(sz.layers):
+        copies[i].wait()
+        for s in range(sz.slots):
+            x = gv[i, s].astype(jnp.float32)
+            acc = acc + x * x
+    total[...] = jnp.broadcast_to(jnp.sum(acc), total.shape)
+
+
+def squares(sz, grad):
+    return pl.pallas_call(
+        functools.partial(square_kernel, sz),
+        in_specs=[ANY],
+        out_specs=VMEM,
+        out_shape=out(1, LANES),
+        scratch_shapes=[
+            pltpu.VMEM(grad.shape, grad.dtype),
+            pltpu.SemaphoreType.DMA((sz.layers,)),
+        ],
+        name="squares",
+    )(grad)
 
 
 def scale_kernel(sz, total, raw, clip, clip_copy, *late):
@@ -182,19 +211,19 @@
     )(*near((total, raw)))
 
 
-def pick_kernel(sz, group, me_ref, plan, clip, *rest):
+def pick_kernel(sz, group, notes, clip, *rest):
     c = sz.chips
     refs = rest[: 2 * c]
     outs = rest[2 * c : 3 * c]
     head, _, size, stride = group
     at = [head + a * stride for a in range(3)]
-    me = me_ref[0]
+    me = read(notes, sz.layers * (sz.group + 1))
     chip = lax.div(me, CORES)
     core = lax.rem(me, CORES)
     layer = lax.div(chip, sz.per_layer)
     for x in range(c):
         target = dyn_peer(chip, x, c) * CORES + core
-        sender = plan[0, layer * sz.group + target]
+        sender = read(notes, layer * sz.group + target)
         from_chip = lax.div(sender, CORES)
         shift = from_chip ^ chip if c & (c - 1) == 0 else lax.rem(chip - from_chip + c, c)
         choice = shift + jnp.where(lax.rem(sender, CORES) == core, 0, c)
@@ -211,25 +240,25 @@
                 outs[x][:, at[1] : at[1] + size] = second
 
 
-def pick(sz, which, me, plan, clip, own, other):
+def pick(sz, which, notes, clip, own, other):
     c = sz.chips
     group = sz.groups[which]
     return pl.pallas_call(
         functools.partial(pick_kernel, sz, group),
-        in_specs=[SMEM, SMEM] + [VMEM] * (2 * c + 1),
+        in_specs=[VMEM] * (2 * c + 2),
         out_specs=[VMEM] * c,
         out_shape=[out(sz.piece, width(group, 2))] * c,
         name="pick",
-    )(me, plan, clip, *own, *other)
-
-
-def land_kernel(sz, which, me_ref, plan, *rest):
+    )(notes, clip, *own, *other)
+
+
+def land_kernel(sz, which, notes, *rest):
     c, n = sz.chips, len(which)
     early, late = rest[:n], rest[n : 2 * n]
     outs = rest[2 * n + 3 : 2 * n + 6]
     st, full, sem = rest[2 * n + 6 :]
-    me = me_ref[0]
-    chip = lax.div(me, CORES)
+    n_slots = sz.layers * sz.group
+    chip = lax.div(read(notes, n_slots + sz.layers), CORES)
     e, f = sz.early, sz.full
     copies = []
     for j, x in enumerate(which):
@@ -247,14 +276,14 @@
         if sz.by_piece:
             layer = lax.div(k, sz.per_layer)
             row = pl.multiple_of(lax.rem(k, sz.per_layer) * sz.piece, sz.piece)
-            slot = plan[1, layer * sz.group + me]
+            slot = read(notes, n_slots + layer)
             for i in range(3):
                 there = outs[i].at[layer, slot, pl.ds(row, sz.piece)]
                 copies.append(pltpu.make_async_copy(st.at[i, j], there, sem.at[i, j]))
                 copies[-1].start()
     if not sz.by_piece:
         for i in range(sz.layers):
-            slot = plan[1, i * sz.group + me]
+            slot = read(notes, n_slots + i)
             for a in range(3):
                 for q in range(sz.per_layer):
                     r = slice(q * sz.piece, (q + 1) * sz.piece)
@@ -267,13 +296,13 @@
         cp.wait()
 
 
-def land(sz, which, me, plan, early, late, outs):
+def land(sz, which, notes, early, late, outs):
     f32 = jnp.float32
     n = len(which)
     whole = (8, LANES) if sz.by_piece else (3, sz.layers, sz.rows, sz.cols)
     return pl.pallas_call(
         functools.partial(land_kernel, sz, which),
-        in_specs=[SMEM, SMEM] + [VMEM] * (2 * n) + [ANY] * 3,
+        in_specs=[VMEM] * (2 * n + 1) + [ANY] * 3,
         out_specs=[ANY] * 3,
         out_shape=[jax.ShapeDtypeStruct(o.shape, o.dtype) for o in outs],
         scratch_shapes=[
@@ -281,9 +310,9 @@
             pltpu.VMEM(whole, f32),
             pltpu.SemaphoreType.DMA((3, max(n, sz.layers))),
         ],
-        input_output_aliases={2 + 2 * n + a: a for a in range(3)},
+        input_output_aliases={1 + 2 * n + a: a for a in range(3)},
         name="land",
-    )(me, plan, *[early[x] for x in which], *[late[x] for x in which], *outs)
+    )(notes, *[early[x] for x in which], *[late[x] for x in which], *outs)
 
 
 def shifts(sz, arrays):
@@ -317,9 +346,11 @@
     sz = Sizes(master.shape, lax.axis_size("expert"), lax.axis_size("dp"))
     me = lax.axis_index("expert").reshape(1)
     c = sz.chips
+    total = squares(sz, gradient)
+    totals = shifts(sz, [total] * c)
     got = prep(sz, me, old_slot, new_slot, master, moment_one, moment_two, gradient)
-    pieces, raw, total, plan = list(got[:c]), got[c], got[c + 1], got[c + 2]
-    totals = shifts(sz, [total] * c)
+    pieces, raw = list(got[:c]), got[c]
+    (notes,) = near([got[c + 1]])
     held = spread(sz, pieces)
     total = sum(totals)
     total = total + swap(sz, [total])[0]
@@ -328,10 +359,10 @@
     (clip,) = near([clip])
     late_held = spread(sz, late)
     other = near(swap(sz, held))
-    early_out = pick(sz, 0, me, plan, clip, held, other)
+    early_out = pick(sz, 0, notes, clip, held, other)
     early_in = spread(sz, list(early_out))
     late_other = near(swap(sz, late_held))
-    late_out = pick(sz, 1, me, plan, clip, late_held, late_other)
+    late_out = pick(sz, 1, notes, clip, late_held, late_other)
     late_in = spread(sz, list(late_out))
     scale = clip_copy[0, 0]
     wide = gradient.astype(jnp.float32)
@@ -341,7 +372,7 @@
     half = c // 2
     batches = [range(half), range(half, c)] if sz.by_piece else [range(c)]
     for which in batches:
-        outs = land(sz, list(which), me, plan, early_in, late_in, outs)
+        outs = land(sz, list(which), notes, early_in, late_in, outs)
     return tuple(outs)
 
 

time: 81 us -> 77.4 us (0.956)
  waiting for transfers between devices: 38.9 us -> 36.1 us
  starting transfers between devices: 25.9 us -> 24.5 us
  Pallas kernels: 9.47 us -> 10.3 us
    ppermute x3, waiting for transfers between devices: 3.03 us -> 0.01 us  [from_others(): lax.ppermute(value, axis, [(i, peer(i, x, n)) for i in range(n)])]
    ppermute x15, starting transfers between devices: 21.2 us -> 19.7 us  [shifts(): got[x] = lax.ppermute(arrays[x], 'expert', pairs)]
    pallas_call x4 -> x5, Pallas kernels: 5.86 us -> 7.07 us  [the longest x2 3.25 us: pick(): pl.pallas_call(functools.partial(pick_kernel, sz, group), in_specs=[VMEM]...]
  transfers between devices with their start and end apart: 27 -> 27, of which waited for: 15 -> 11; matrix products, arithmetic and copies ran while one was open for 7% -> 7% of each run, Pallas kernels for 5% -> 10%
where the time goes in v4:
time: 77.4 us; the launch traced here: 76.8 us
  waiting for transfers between devices  36.1 us (47%)
  starting transfers between devices  24.5 us (32%)
  Pallas kernels  10.3 us (13%)
  other arithmetic  5.26 us (7%)
    ppermute x15, waiting for transfers between devices, shifts(): got[x] = lax.ppermute(arrays[x], 'expert', pairs)  34.9 us
    ppermute x15, starting transfers between devices, shifts(): got[x] = lax.ppermute(arrays[x], 'expert', pairs)  19.7 us
    sub x1, other arithmetic, new_weights(): return master - LEARN_RATE * (step_dir + DECAY_RATE * master)  5.24 us
    ppermute x3, starting transfers between devices, from_others(): lax.ppermute(value, axis, [(i, peer(i, x, n)) for i in range(n)])  3.55 us
    pallas_call x2, Pallas kernels, pick(): pl.pallas_call(functools.partial(pick_kernel, sz, group), in_specs=[VMEM]...  3.25 us
    pallas_call x1, Pallas kernels, prep(): pl.pallas_call(functools.partial(prep_kernel, sz), in_specs=[SMEM, SMEM,...  2.65 us
    pallas_call x2, Pallas kernels, land(): pl.pallas_call(functools.partial(land_kernel, sz, which), in_specs=[VMEM]...  2.5 us
  transfers between devices with their start and end apart: 27, of which 11 were waited for; matrix products, arithmetic and copies ran while one was open for 7% of the time, Pallas kernels for 10%

profile of v4, /device:TPU:12, one launch (start us, length us, event | category | flops | bytes accessed | tf_op | source)
XLA Modules:
  0.0 76.8 jit_solution(6921687578760610902)
XLA Ops:
  0.6 1.3 %squares.1 = f32[1,128]{1,0:T(1,128)S(1)} custom-call(bf16[2,4,16,2880]{3,2,1,0:T(8,128)(2,1)} %grad.3), custom_call_target="tpu_custom_call" | custom-call | tf_op jit(solution)/shard_map/squares/pallas_call | solution.py:177
  2.0 1.6 %collective-permute-start.2 = (f32[1,128]{1,0:T(1,128)S(1)}, f32[1,128]{1,0:T(1,128)S(1)}, u32[]{:S(2)}, u32[]{:S(2)}) collective-permute-start(f32[1,128]{1,0:T(1,128)S(1)} %squares.1), channel_id=1, source_target_pairs={{0,6},{1,7},{2,4},{3,5},{4,2},{5,3},{6,0},{7,1},{8,14},{9,15},{10,... | collective-permute-start | bytes 1544 | tf_op jit(solution)/shard_map/ppermute | solution.py:325
  4.8 1.2 %collective-permute-start = (f32[1,128]{1,0:T(1,128)S(1)}, f32[1,128]{1,0:T(1,128)S(1)}, u32[]{:S(2)}, u32[]{:S(2)}) collective-permute-start(f32[1,128]{1,0:T(1,128)S(1)} %squares.1), channel_id=1, source_target_pairs={{0,2},{1,3},{2,0},{3,1},{4,6},{5,7},{6,4},{7,5},{8,10},{9,11},{10,... | collective-permute-start | bytes 1544 | tf_op jit(solution)/shard_map/ppermute | solution.py:325
  6.1 2.0 %collective-permute-done.1 = f32[1,128]{1,0:T(1,128)S(1)} collective-permute-done((f32[1,128]{1,0:T(1,128)S(1)}, f32[1,128]{1,0:T(1,128)S(1)}, u32[]{:S(2)}, u32[]{:S(2)}) %collective-permute-start.1) | collective-permute-done | bytes 544 | tf_op jit(solution)/shard_map/ppermute | solution.py:325
  9.6 1.4 %collective-permute-start.6 = (f32[1,128]{1,0:T(1,128)S(1)}, f32[1,128]{1,0:T(1,128)S(1)}, u32[]{:S(2)}, u32[]{:S(2)}) collective-permute-start(f32[1,128]{1,0:T(1,128)S(1)} %add.39), channel_id=1, source_target_pairs={{0,24},{8,16},{16,8},{24,0},{1,25},{9,17},{17,9},{25,1},{2,26},{10... | collective-permute-start | bytes 1544 | tf_op jit(solution)/shard_map/ppermute | solution.py:336
  11.0 1.5 %collective-permute-start.5 = (f32[1,128]{1,0:T(1,128)S(1)}, f32[1,128]{1,0:T(1,128)S(1)}, u32[]{:S(2)}, u32[]{:S(2)}) collective-permute-start(f32[1,128]{1,0:T(1,128)S(1)} %add.39), channel_id=1, source_target_pairs={{0,16},{8,24},{16,0},{24,8},{1,17},{9,25},{17,1},{25,9},{2,18},{10... | collective-permute-start | bytes 1544 | tf_op jit(solution)/shard_map/ppermute | solution.py:336
  12.5 2.7 %prep.1 = (f32[8,4480]{1,0:T(8,128)S(1)}, f32[8,4480]{1,0:T(8,128)S(1)}, f32[8,4480]{1,0:T(8,128)S(1)}, f32[8,4480]{1,0:T(8,128)S(1)}, f32[3,4,8,2368]{3,2,1,0:T(8,128)S(1)}, /*index=5*/s32[1,128]{1,0:T(1,128)S(1)}) custom-call(s32[1]{0:T(128)} %bitcast.me_ref, s32[2,32]{1,0:T(2,128)} %old_ref.1, s32[2,32]{1,0:T(2,128)} %new_ref.1, ...), custom_call_target="tpu_custom_call" | custom-call | tf_op jit(solution)/shard_map/prep/pallas_call | solution.py:145
  15.8 2.2 %collective-permute-start.7 = (f32[8,4480]{1,0:T(8,128)S(1)}, f32[8,4480]{1,0:T(8,128)S(1)}, u32[]{:S(2)}, u32[]{:S(2)}) collective-permute-start(f32[8,4480]{1,0:T(8,128)S(1)} %get-tuple-element.30), channel_id=1, source_target_pairs={{0,2},{1,3},{2,0},{3,1},{4,6},{5,7},{6,4},{7,5},{8,10},{9,11},{10,... | collective-permute-start | bytes 430088 | tf_op jit(solution)/shard_map/ppermute | solution.py:325
  18.0 2.0 %collective-permute-start.8 = (f32[8,4480]{1,0:T(8,128)S(1)}, f32[8,4480]{1,0:T(8,128)S(1)}, u32[]{:S(2)}, u32[]{:S(2)}) collective-permute-start(f32[8,4480]{1,0:T(8,128)S(1)} %get-tuple-element.31), channel_id=1, source_target_pairs={{0,4},{1,5},{2,6},{3,7},{4,0},{5,1},{6,2},{7,3},{8,12},{9,13},{10,... | collective-permute-start | bytes 430088 | tf_op jit(solution)/shard_map/ppermute | solution.py:325
  20.6 2.3 %collective-permute-start.16 = (f32[8,4736]{1,0:T(8,128)S(1)}, f32[8,4736]{1,0:T(8,128)S(1)}, u32[]{:S(2)}, u32[]{:S(2)}) collective-permute-start(f32[8,4736]{1,0:T(8,128)S(1)} %get-tuple-element.36), channel_id=1, source_target_pairs={{0,2},{1,3},{2,0},{3,1},{4,6},{5,7},{6,4},{7,5},{8,10},{9,11},{10,... | collective-permute-start | bytes 454664 | tf_op jit(solution)/shard_map/ppermute | solution.py:325
  24.1 5.5 %collective-permute-done.8.rest_2_ = f32[8,4480]{1,0:T(8,128)S(1)} collective-permute-done((f32[8,4480]{1,0:T(8,128)S(1)}, f32[8,4480]{1,0:T(8,128)S(1)}, u32[]{:S(2)}, u32[]{:S(2)}) %collective-permute-start.8) | collective-permute-done | bytes 143392 | tf_op jit(solution)/shard_map/ppermute | solution.py:325
  29.6 9.8 %collective-permute-done.9.rest_3_ = f32[8,4480]{1,0:T(8,128)S(1)} collective-permute-done((f32[8,4480]{1,0:T(8,128)S(1)}, f32[8,4480]{1,0:T(8,128)S(1)}, u32[]{:S(2)}, u32[]{:S(2)}) %collective-permute-start.9) | collective-permute-done | bytes 143392 | tf_op jit(solution)/shard_map/ppermute | solution.py:325
  40.1 2.0 %collective-permute-done.17.rest_2_ = f32[8,4736]{1,0:T(8,128)S(1)} collective-permute-done((f32[8,4736]{1,0:T(8,128)S(1)}, f32[8,4736]{1,0:T(8,128)S(1)}, u32[]{:S(2)}, u32[]{:S(2)}) %collective-permute-start.17) | collective-permute-done | bytes 151584 | tf_op jit(solution)/shard_map/ppermute | solution.py:325
  42.0 2.7 %collective-permute-done.18.rest_3_ = f32[8,4736]{1,0:T(8,128)S(1)} collective-permute-done((f32[8,4736]{1,0:T(8,128)S(1)}, f32[8,4736]{1,0:T(8,128)S(1)}, u32[]{:S(2)}, u32[]{:S(2)}) %collective-permute-start.18) | collective-permute-done | bytes 151584 | tf_op jit(solution)/shard_map/ppermute | solution.py:325
  45.3 2.1 %pick.2 = (f32[8,3968]{1,0:T(8,128)S(1)}, f32[8,3968]{1,0:T(8,128)}, f32[8,3968]{1,0:T(8,128)S(1)}, f32[8,3968]{1,0:T(8,128)S(1)}) custom-call(s32[1,128]{1,0:T(1,128)S(1)} %get-tuple-element.26.notes, f32[1,128]{1,0:T(1,128)S(1)} %get-tuple-element.28.clip, f32[8,4480]{1,0:T(8,128)S(1)} %get-tuple-element.29.rest_0_, ...), custom_call_target="tpu_custom_call" | custom-call | tf_op jit(solution)/shard_map/pick/pallas_call | solution.py:246
  47.4 3.5 %collective-permute-start.14 = (f32[8,3968]{1,0:T(8,128)S(1)}, f32[8,3968]{1,0:T(8,128)S(1)}, u32[]{:S(2)}, u32[]{:S(2)}) collective-permute-start(f32[8,3968]{1,0:T(8,128)S(1)} %get-tuple-element.33), channel_id=1, source_target_pairs={{0,4},{1,5},{2,6},{3,7},{4,0},{5,1},{6,2},{7,3},{8,12},{9,13},{10,... | collective-permute-start | bytes 380936 | tf_op jit(solution)/shard_map/ppermute | solution.py:325
  52.1 2.5 %collective-permute-start.23 = (f32[8,4736]{1,0:T(8,128)S(1)}, f32[8,4736]{1,0:T(8,128)S(1)}, u32[]{:S(2)}, u32[]{:S(2)}) collective-permute-start(f32[8,4736]{1,0:T(8,128)S(1)} %get-tuple-element.39), channel_id=1, source_target_pairs={{0,4},{1,5},{2,6},{3,7},{4,0},{5,1},{6,2},{7,3},{8,12},{9,13},{10,... | collective-permute-start | bytes 454664 | tf_op jit(solution)/shard_map/ppermute | solution.py:325
  55.2 1.4 %collective-permute-start.26 = (f32[8,4736]{1,0:T(8,128)S(1)}, f32[8,4736]{1,0:T(8,128)S(1)}, u32[]{:S(2)}, u32[]{:S(2)}) collective-permute-start(f32[8,4736]{1,0:T(8,128)S(1)} %get-tuple-element.44), channel_id=1, source_target_pairs={{0,2},{1,3},{2,0},{3,1},{4,6},{5,7},{6,4},{7,5},{8,10},{9,11},{10,... | collective-permute-start | bytes 454664 | tf_op jit(solution)/shard_map/ppermute | solution.py:325
  56.6 5.2 %multiply_subtract_fusion = (f32[2,4,16,2880]{3,2,1,0:T(8,128)}, f32[2,4,16,2880]{3,2,1,0:T(8,128)}, f32[2,4,16,2880]{3,2,1,0:T(8,128)}) fusion(f32[2,4,16,2880]{3,2,1,0:T(8,128)} %master.1, f32[]{:T(128)S(1)} %bitcast.3, bf16[2,4,16,2880]{3,2,1,0:T(8,128)(2,1)S(1)} %copy-done, f32[2,4,16,2880]{3,2,1,0:T(8,128)} %mone.1, f32[2,4,16,2880]{3,2,1,0:T(8,128)} %mtwo.1), kind=kLoop, calls=%fused_computation.2 | loop fusion | flops 6266880 | bytes 9584644 | tf_op jit(solution)/shard_map/sub | solution.py:51
  61.8 6.8 %collective-permute-done.26.rest_3_ = f32[8,4736]{1,0:T(8,128)S(1)} collective-permute-done((f32[8,4736]{1,0:T(8,128)S(1)}, f32[8,4736]{1,0:T(8,128)S(1)}, u32[]{:S(2)}, u32[]{:S(2)}) %collective-permute-start.26) | collective-permute-done | bytes 151584 | tf_op jit(solution)/shard_map/ppermute | solution.py:325
  68.6 1.2 %land.2 = (f32[2,4,16,2880]{3,2,1,0:T(8,128)}, f32[2,4,16,2880]{3,2,1,0:T(8,128)}, f32[2,4,16,2880]{3,2,1,0:T(8,128)}) custom-call(s32[1,128]{1,0:T(1,128)S(1)} %get-tuple-element.26.notes, f32[8,3968]{1,0:T(8,128)S(1)} %get-tuple-element.41.rest_0_, ...), custom_call_target="tpu_custom_call", output_to_operand_aliasing={{0}: (5, {}), {1}: (6, {}), {2}: (7, {})} | custom-call | tf_op jit(solution)/shard_map/land/pallas_call | solution.py:303
  69.9 2.6 %collective-permute-done.23.rest_2_ = f32[8,4736]{1,0:T(8,128)S(1)} collective-permute-done((f32[8,4736]{1,0:T(8,128)S(1)}, f32[8,4736]{1,0:T(8,128)S(1)}, u32[]{:S(2)}, u32[]{:S(2)}) %collective-permute-start.23) | collective-permute-done | bytes 151584 | tf_op jit(solution)/shard_map/ppermute | solution.py:325
  72.5 3.1 %collective-permute-done.24.rest_3_ = f32[8,4736]{1,0:T(8,128)S(1)} collective-permute-done((f32[8,4736]{1,0:T(8,128)S(1)}, f32[8,4736]{1,0:T(8,128)S(1)}, u32[]{:S(2)}, u32[]{:S(2)}) %collective-permute-start.24) | collective-permute-done | bytes 151584 | tf_op jit(solution)/shard_map/ppermute | solution.py:325
  75.6 1.2 %land.3 = (f32[2,4,16,2880]{3,2,1,0:T(8,128)}, f32[2,4,16,2880]{3,2,1,0:T(8,128)}, f32[2,4,16,2880]{3,2,1,0:T(8,128)}) custom-call(s32[1,128]{1,0:T(1,128)S(1)} %get-tuple-element.26.notes, f32[8,3968]{1,0:T(8,128)S(1)} %collective-permute-done.14.rest_0_, ...), custom_call_target="tpu_custom_call", output_to_operand_aliasing={{0}: (5, {}), {1}: (6, {}), {2}: (7, {})} | custom-call | tf_op jit(solution)/shard_map/land/pallas_call | solution.py:303
  (45 shorter events, 8.1 us)
Async XLA Ops:
  3.6 4.5 %collective-permute-start.1 = (f32[1,128]{1,0:T(1,128)S(1)}, f32[1,128]{1,0:T(1,128)S(1)}, u32[]{:S(2)}, u32[]{:S(2)}) collective-permute-start(f32[1,128]{1,0:T(1,128)S(1)} %squares.1), channel_id=1, source_target_pairs={{0,4},{1,5},{2,6},{3,7},{4,0},{5,1},{6,2},{7,3},{8,12},{9,13},{10,... | collective-permute-start | bytes 1544 | tf_op jit(solution)/shard_map/ppermute | solution.py:325
  9.6 10.4 %collective-permute-start.6 = (f32[1,128]{1,0:T(1,128)S(1)}, f32[1,128]{1,0:T(1,128)S(1)}, u32[]{:S(2)}, u32[]{:S(2)}) collective-permute-start(f32[1,128]{1,0:T(1,128)S(1)} %add.39), channel_id=1, source_target_pairs={{0,24},{8,16},{16,8},{24,0},{1,25},{9,17},{17,9},{25,1},{2,26},{10... | collective-permute-start | bytes 1544 | tf_op jit(solution)/shard_map/ppermute | solution.py:336
  11.0 9.0 %collective-permute-start.5 = (f32[1,128]{1,0:T(1,128)S(1)}, f32[1,128]{1,0:T(1,128)S(1)}, u32[]{:S(2)}, u32[]{:S(2)}) collective-permute-start(f32[1,128]{1,0:T(1,128)S(1)} %add.39), channel_id=1, source_target_pairs={{0,16},{8,24},{16,0},{24,8},{1,17},{9,25},{17,1},{25,9},{2,18},{10... | collective-permute-start | bytes 1544 | tf_op jit(solution)/shard_map/ppermute | solution.py:336
  15.2 4.9 %collective-permute-start.4 = (f32[1,128]{1,0:T(1,128)S(1)}, f32[1,128]{1,0:T(1,128)S(1)}, u32[]{:S(2)}, u32[]{:S(2)}) collective-permute-start(f32[1,128]{1,0:T(1,128)S(1)} %add.39), channel_id=1, source_target_pairs={{0,8},{8,0},{16,24},{24,16},{1,9},{9,1},{17,25},{25,17},{2,10},{10... | collective-permute-start | bytes 1544 | tf_op jit(solution)/shard_map/ppermute | solution.py:336
  15.8 7.2 %collective-permute-start.7 = (f32[8,4480]{1,0:T(8,128)S(1)}, f32[8,4480]{1,0:T(8,128)S(1)}, u32[]{:S(2)}, u32[]{:S(2)}) collective-permute-start(f32[8,4480]{1,0:T(8,128)S(1)} %get-tuple-element.30), channel_id=1, source_target_pairs={{0,2},{1,3},{2,0},{3,1},{4,6},{5,7},{6,4},{7,5},{8,10},{9,11},{10,... | collective-permute-start | bytes 430088 | tf_op jit(solution)/shard_map/ppermute | solution.py:325
  18.0 11.6 %collective-permute-start.8 = (f32[8,4480]{1,0:T(8,128)S(1)}, f32[8,4480]{1,0:T(8,128)S(1)}, u32[]{:S(2)}, u32[]{:S(2)}) collective-permute-start(f32[8,4480]{1,0:T(8,128)S(1)} %get-tuple-element.31), channel_id=1, source_target_pairs={{0,4},{1,5},{2,6},{3,7},{4,0},{5,1},{6,2},{7,3},{8,12},{9,13},{10,... | collective-permute-start | bytes 430088 | tf_op jit(solution)/shard_map/ppermute | solution.py:325
  20.0 19.5 %collective-permute-start.9 = (f32[8,4480]{1,0:T(8,128)S(1)}, f32[8,4480]{1,0:T(8,128)S(1)}, u32[]{:S(2)}, u32[]{:S(2)}) collective-permute-start(f32[8,4480]{1,0:T(8,128)S(1)} %get-tuple-element.32), channel_id=1, source_target_pairs={{0,6},{1,7},{2,4},{3,5},{4,2},{5,3},{6,0},{7,1},{8,14},{9,15},{10,... | collective-permute-start | bytes 430088 | tf_op jit(solution)/shard_map/ppermute | solution.py:325
  20.0 19.5 %collective-permute-start.10 = (f32[8,4480]{1,0:T(8,128)S(1)}, f32[8,4480]{1,0:T(8,128)S(1)}, u32[]{:S(2)}, u32[]{:S(2)}) collective-permute-start(f32[8,4480]{1,0:T(8,128)S(1)} %get-tuple-element.29.rest_0_), channel_id=1, source_target_pairs={{0,1},{1,0},{2,3},{3,2},{4,5},{5,4},{6,7},{7,6},{8,9},{9,8},{10,11... | collective-permute-start | bytes 430088 | tf_op jit(solution)/shard_map/ppermute | solution.py:342
  20.6 19.4 %collective-permute-start.16 = (f32[8,4736]{1,0:T(8,128)S(1)}, f32[8,4736]{1,0:T(8,128)S(1)}, u32[]{:S(2)}, u32[]{:S(2)}) collective-permute-start(f32[8,4736]{1,0:T(8,128)S(1)} %get-tuple-element.36), channel_id=1, source_target_pairs={{0,2},{1,3},{2,0},{3,1},{4,6},{5,7},{6,4},{7,5},{8,10},{9,11},{10,... | collective-permute-start | bytes 454664 | tf_op jit(solution)/shard_map/ppermute | solution.py:325
  23.0 19.0 %collective-permute-start.17 = (f32[8,4736]{1,0:T(8,128)S(1)}, f32[8,4736]{1,0:T(8,128)S(1)}, u32[]{:S(2)}, u32[]{:S(2)}) collective-permute-start(f32[8,4736]{1,0:T(8,128)S(1)} %get-tuple-element.37), channel_id=1, source_target_pairs={{0,4},{1,5},{2,6},{3,7},{4,0},{5,1},{6,2},{7,3},{8,12},{9,13},{10,... | collective-permute-start | bytes 454664 | tf_op jit(solution)/shard_map/ppermute | solution.py:325
  29.6 15.1 %collective-permute-start.18 = (f32[8,4736]{1,0:T(8,128)S(1)}, f32[8,4736]{1,0:T(8,128)S(1)}, u32[]{:S(2)}, u32[]{:S(2)}) collective-permute-start(f32[8,4736]{1,0:T(8,128)S(1)} %get-tuple-element.38), channel_id=1, source_target_pairs={{0,6},{1,7},{2,4},{3,5},{4,2},{5,3},{6,0},{7,1},{8,14},{9,15},{10,... | collective-permute-start | bytes 454664 | tf_op jit(solution)/shard_map/ppermute | solution.py:325
  39.5 5.3 %collective-permute-start.11 = (f32[8,4480]{1,0:T(8,128)S(1)}, f32[8,4480]{1,0:T(8,128)S(1)}, u32[]{:S(2)}, u32[]{:S(2)}) collective-permute-start(f32[8,4480]{1,0:T(8,128)S(1)} %collective-permute-done.7.rest_1_), channel_id=1, source_target_pairs={{0,1},{1,0},{2,3},{3,2},{4,5},{5,4},{6,7},{7,6},{8,9},{9,8},{10,11... | collective-permute-start | bytes 430088 | tf_op jit(solution)/shard_map/ppermute | solution.py:342
  39.5 5.8 %collective-permute-start.12 = (f32[8,4480]{1,0:T(8,128)S(1)}, f32[8,4480]{1,0:T(8,128)S(1)}, u32[]{:S(2)}, u32[]{:S(2)}) collective-permute-start(f32[8,4480]{1,0:T(8,128)S(1)} %collective-permute-done.8.rest_2_), channel_id=1, source_target_pairs={{0,1},{1,0},{2,3},{3,2},{4,5},{5,4},{6,7},{7,6},{8,9},{9,8},{10,11... | collective-permute-start | bytes 430088 | tf_op jit(solution)/shard_map/ppermute | solution.py:342
  40.0 5.4 %collective-permute-start.13 = (f32[8,4480]{1,0:T(8,128)S(1)}, f32[8,4480]{1,0:T(8,128)S(1)}, u32[]{:S(2)}, u32[]{:S(2)}) collective-permute-start(f32[8,4480]{1,0:T(8,128)S(1)} %collective-permute-done.9.rest_3_), channel_id=1, source_target_pairs={{0,1},{1,0},{2,3},{3,2},{4,5},{5,4},{6,7},{7,6},{8,9},{9,8},{10,11... | collective-permute-start | bytes 430088 | tf_op jit(solution)/shard_map/ppermute | solution.py:342
  42.0 5.4 %collective-permute-start.19 = (f32[8,4736]{1,0:T(8,128)S(1)}, f32[8,4736]{1,0:T(8,128)S(1)}, u32[]{:S(2)}, u32[]{:S(2)}) collective-permute-start(f32[8,4736]{1,0:T(8,128)S(1)} %get-tuple-element.35.rest_0_), channel_id=1, source_target_pairs={{0,1},{1,0},{2,3},{3,2},{4,5},{5,4},{6,7},{7,6},{8,9},{9,8},{10,11... | collective-permute-start | bytes 454664 | tf_op jit(solution)/shard_map/ppermute | solution.py:342
  44.8 6.1 %collective-permute-start.20 = (f32[8,4736]{1,0:T(8,128)S(1)}, f32[8,4736]{1,0:T(8,128)S(1)}, u32[]{:S(2)}, u32[]{:S(2)}) collective-permute-start(f32[8,4736]{1,0:T(8,128)S(1)} %collective-permute-done.16.rest_1_), channel_id=1, source_target_pairs={{0,1},{1,0},{2,3},{3,2},{4,5},{5,4},{6,7},{7,6},{8,9},{9,8},{10,11... | collective-permute-start | bytes 454664 | tf_op jit(solution)/shard_map/ppermute | solution.py:342
  44.8 6.1 %collective-permute-start.21 = (f32[8,4736]{1,0:T(8,128)S(1)}, f32[8,4736]{1,0:T(8,128)S(1)}, u32[]{:S(2)}, u32[]{:S(2)}) collective-permute-start(f32[8,4736]{1,0:T(8,128)S(1)} %collective-permute-done.17.rest_2_), channel_id=1, source_target_pairs={{0,1},{1,0},{2,3},{3,2},{4,5},{5,4},{6,7},{7,6},{8,9},{9,8},{10,11... | collective-permute-start | bytes 454664 | tf_op jit(solution)/shard_map/ppermute | solution.py:342
  45.3 5.6 %collective-permute-start.22 = (f32[8,4736]{1,0:T(8,128)S(1)}, f32[8,4736]{1,0:T(8,128)S(1)}, u32[]{:S(2)}, u32[]{:S(2)}) collective-permute-start(f32[8,4736]{1,0:T(8,128)S(1)} %collective-permute-done.18.rest_3_), channel_id=1, source_target_pairs={{0,1},{1,0},{2,3},{3,2},{4,5},{5,4},{6,7},{7,6},{8,9},{9,8},{10,11... | collective-permute-start | bytes 454664 | tf_op jit(solution)/shard_map/ppermute | solution.py:342
  47.4 7.8 %collective-permute-start.25 = (f32[8,3968]{1,0:T(8,128)}, f32[8,3968]{1,0:T(8,128)S(1)}, u32[]{:S(2)}, u32[]{:S(2)}) collective-permute-start(f32[8,3968]{1,0:T(8,128)} %get-tuple-element.42), channel_id=1, source_target_pairs={{0,2},{1,3},{2,0},{3,1},{4,6},{5,7},{6,4},{7,5},{8,10},{9,11},{10,... | collective-permute-start | bytes 380936 | tf_op jit(solution)/shard_map/ppermute | solution.py:325
  47.4 22.4 %collective-permute-start.14 = (f32[8,3968]{1,0:T(8,128)S(1)}, f32[8,3968]{1,0:T(8,128)S(1)}, u32[]{:S(2)}, u32[]{:S(2)}) collective-permute-start(f32[8,3968]{1,0:T(8,128)S(1)} %get-tuple-element.33), channel_id=1, source_target_pairs={{0,4},{1,5},{2,6},{3,7},{4,0},{5,1},{6,2},{7,3},{8,12},{9,13},{10,... | collective-permute-start | bytes 380936 | tf_op jit(solution)/shard_map/ppermute | solution.py:325
  50.9 19.0 %collective-permute-start.15 = (f32[8,3968]{1,0:T(8,128)S(1)}, f32[8,3968]{1,0:T(8,128)S(1)}, u32[]{:S(2)}, u32[]{:S(2)}) collective-permute-start(f32[8,3968]{1,0:T(8,128)S(1)} %get-tuple-element.34), channel_id=1, source_target_pairs={{0,6},{1,7},{2,4},{3,5},{4,2},{5,3},{6,0},{7,1},{8,14},{9,15},{10,... | collective-permute-start | bytes 380936 | tf_op jit(solution)/shard_map/ppermute | solution.py:325
  52.1 20.4 %collective-permute-start.23 = (f32[8,4736]{1,0:T(8,128)S(1)}, f32[8,4736]{1,0:T(8,128)S(1)}, u32[]{:S(2)}, u32[]{:S(2)}) collective-permute-start(f32[8,4736]{1,0:T(8,128)S(1)} %get-tuple-element.39), channel_id=1, source_target_pairs={{0,4},{1,5},{2,6},{3,7},{4,0},{5,1},{6,2},{7,3},{8,12},{9,13},{10,... | collective-permute-start | bytes 454664 | tf_op jit(solution)/shard_map/ppermute | solution.py:325
  54.6 21.0 %collective-permute-start.24 = (f32[8,4736]{1,0:T(8,128)S(1)}, f32[8,4736]{1,0:T(8,128)S(1)}, u32[]{:S(2)}, u32[]{:S(2)}) collective-permute-start(f32[8,4736]{1,0:T(8,128)S(1)} %get-tuple-element.40), channel_id=1, source_target_pairs={{0,6},{1,7},{2,4},{3,5},{4,2},{5,3},{6,0},{7,1},{8,14},{9,15},{10,... | collective-permute-start | bytes 454664 | tf_op jit(solution)/shard_map/ppermute | solution.py:325
  55.2 13.4 %collective-permute-start.26 = (f32[8,4736]{1,0:T(8,128)S(1)}, f32[8,4736]{1,0:T(8,128)S(1)}, u32[]{:S(2)}, u32[]{:S(2)}) collective-permute-start(f32[8,4736]{1,0:T(8,128)S(1)} %get-tuple-element.44), channel_id=1, source_target_pairs={{0,2},{1,3},{2,0},{3,1},{4,6},{5,7},{6,4},{7,5},{8,10},{9,11},{10,... | collective-permute-start | bytes 454664 | tf_op jit(solution)/shard_map/ppermute | solution.py:325
  (5 other events, 54.0 us)

commit v5 on v4

--- a/solution.py
+++ b/solution.py
@@ -90,7 +90,9 @@
 def prep_kernel(sz, me_ref, old_ref, new_ref, master, mone, mtwo, grad, *rest):
     c = sz.chips
     pieces = rest[:c]
-    late_raw, notes, plan, mv, m1v, m2v, gv, st, sem = rest[c:]
+    late_raw, total, notes, plan, mv, m1v, m2v, gv, st, sem_g, sem = rest[c:]
+    for i in range(sz.layers):
+        pltpu.make_async_copy(grad.at[i], gv.at[i], sem_g.at[i]).start()
     me = me_ref[0]
     chip = lax.div(me, CORES)
     n_slots = sz.layers * sz.group
@@ -106,12 +108,19 @@
 
         lax.fori_loop(0, old_ref.shape[1], note, 0, unroll=8)
         slot = plan[1, i * sz.group + me]
-        for a, (src, dst) in enumerate(((master, mv), (mone, m1v), (mtwo, m2v), (grad, gv))):
+        for a, (src, dst) in enumerate(((master, mv), (mone, m1v), (mtwo, m2v))):
             pltpu.make_async_copy(src.at[i, slot], dst.at[i], sem.at[i, a]).start()
-    for i in range(sz.layers):
-        for a, (src, dst) in enumerate(((master, mv), (mone, m1v), (mtwo, m2v), (grad, gv))):
+    acc = jnp.zeros((sz.rows, sz.cols), jnp.float32)
+    for i in range(sz.layers):
+        pltpu.make_async_copy(grad.at[i], gv.at[i], sem_g.at[i]).wait()
+        for s in range(sz.slots):
+            x = gv[i, s].astype(jnp.float32)
+            acc = acc + x * x
+    total[...] = jnp.broadcast_to(jnp.sum(acc), total.shape)
+    for i in range(sz.layers):
+        for a, (src, dst) in enumerate(((master, mv), (mone, m1v), (mtwo, m2v))):
             pltpu.make_async_copy(src.at[i, 0], dst.at[i], sem.at[i, a]).wait()
-        g = gv[i].astype(jnp.float32)
+        g = gv[i, plan[1, i * sz.group + me]].astype(jnp.float32)
         for q in range(sz.per_layer):
             k = i * sz.per_layer + q
             r = slice(q * sz.piece, (q + 1) * sz.piece)
@@ -140,51 +149,26 @@
     slot = (sz.layers, sz.rows, sz.cols)
     outs = [out(sz.piece, width(sz.groups[0], 3))] * sz.chips + [
         out(3, sz.chips, sz.piece, sz.late),
+        out(1, LANES),
         out(1, up(sz.layers * (sz.group + 1) + 1), dtype=jnp.int32),
     ]
     return pl.pallas_call(
         functools.partial(prep_kernel, sz),
         in_specs=[SMEM, SMEM, SMEM, ANY, ANY, ANY, ANY],
-        out_specs=[VMEM] * (sz.chips + 2),
+        out_specs=[VMEM] * (sz.chips + 3),
         out_shape=outs,
         scratch_shapes=[
             pltpu.SMEM((2, sz.layers * sz.group + 1), jnp.int32),
             pltpu.VMEM(slot, f32),
             pltpu.VMEM(slot, f32),
             pltpu.VMEM(slot, f32),
-            pltpu.VMEM(slot, grad.dtype),
+            pltpu.VMEM(grad.shape, grad.dtype),
             pltpu.VMEM((4, sz.chips, sz.piece, sz.cols), f32),
-            pltpu.SemaphoreType.DMA((sz.layers, 4)),
+            pltpu.SemaphoreType.DMA((sz.layers,)),
+            pltpu.SemaphoreType.DMA((sz.layers, 3)),
         ],
         name="prep",
     )(me, old_slot, new_slot, master, mone, mtwo, grad)
-
-
-def square_kernel(sz, grad, total, gv, sem):
-    copies = [pltpu.make_async_copy(grad.at[i], gv.at[i], sem.at[i]) for i in range(sz.layers)]
-    for cp in copies:
-        cp.start()
-    acc = jnp.zeros((sz.rows, sz.cols), jnp.float32)
-    for i in range(sz.layers):
-        copies[i].wait()
-        for s in range(sz.slots):
-            x = gv[i, s].astype(jnp.float32)
-            acc = acc + x * x
-    total[...] = jnp.broadcast_to(jnp.sum(acc), total.shape)
-
-
-def squares(sz, grad):
-    return pl.pallas_call(
-        functools.partial(square_kernel, sz),
-        in_specs=[ANY],
-        out_specs=VMEM,
-        out_shape=out(1, LANES),
-        scratch_shapes=[
-            pltpu.VMEM(grad.shape, grad.dtype),
-            pltpu.SemaphoreType.DMA((sz.layers,)),
-        ],
-        name="squares",
-    )(grad)
 
 
 def scale_kernel(sz, total, raw, clip, clip_copy, *late):
@@ -327,7 +311,7 @@
 
 
 def spread(sz, arrays):
-    return near(shifts(sz, arrays))
+    return near(shifts(sz, near(arrays)))
 
 
 def from_others(value, axis):
@@ -346,11 +330,10 @@
     sz = Sizes(master.shape, lax.axis_size("expert"), lax.axis_size("dp"))
     me = lax.axis_index("expert").reshape(1)
     c = sz.chips
-    total = squares(sz, gradient)
+    got = prep(sz, me, old_slot, new_slot, master, moment_one, moment_two, gradient)
+    pieces, raw, total = list(got[:c]), got[c], got[c + 1]
+    (notes,) = near([got[c + 2]])
     totals = shifts(sz, [total] * c)
-    got = prep(sz, me, old_slot, new_slot, master, moment_one, moment_two, gradient)
-    pieces, raw = list(got[:c]), got[c]
-    (notes,) = near([got[c + 1]])
     held = spread(sz, pieces)
     total = sum(totals)
     total = total + swap(sz, [total])[0]

time: 77.4 us -> 76 us (0.982)
  Pallas kernels: 10.3 us -> 8.94 us
    pallas_call x1 -> x0, Pallas kernels: 1.32 us -> none  [squares(): pl.pallas_call(functools.partial(square_kernel, sz), in_specs=[ANY], out_...]
  transfers between devices with their start and end apart: 27 -> 27, of which waited for: 11 -> 11; matrix products, arithmetic and copies ran while one was open for 7% -> 7% of each run, Pallas kernels for 10% -> 7%
where the time goes in v5:
time: 76 us; the launch traced here: 75.4 us
  waiting for transfers between devices  35.9 us (47%)
  starting transfers between devices  24.4 us (32%)
  Pallas kernels  8.94 us (12%)
  other arithmetic  5.46 us (7%)
    ppermute x15, waiting for transfers between devices, shifts(): got[x] = lax.ppermute(arrays[x], 'expert', pairs)  34.7 us
    ppermute x15, starting transfers between devices, shifts(): got[x] = lax.ppermute(arrays[x], 'expert', pairs)  19.7 us
    sub x1, other arithmetic, new_weights(): return master - LEARN_RATE * (step_dir + DECAY_RATE * master)  5.44 us
    ppermute x3, starting transfers between devices, from_others(): lax.ppermute(value, axis, [(i, peer(i, x, n)) for i in range(n)])  3.49 us
    pallas_call x2, Pallas kernels, pick(): pl.pallas_call(functools.partial(pick_kernel, sz, group), in_specs=[VMEM]...  3.25 us
    pallas_call x1, Pallas kernels, prep(): pl.pallas_call(functools.partial(prep_kernel, sz), in_specs=[SMEM, SMEM,...  2.66 us
    pallas_call x2, Pallas kernels, land(): pl.pallas_call(functools.partial(land_kernel, sz, which), in_specs=[VMEM]...  2.5 us
  transfers between devices with their start and end apart: 27, of which 11 were waited for; matrix products, arithmetic and copies ran while one was open for 7% of the time, Pallas kernels for 7%

profile of v5, /device:TPU:12, one launch (start us, length us, event | category | flops | bytes accessed | tf_op | source)
XLA Modules:
  0.0 75.4 jit_solution(11068253401359163765)
XLA Ops:
  0.6 2.7 %prep.1 = (f32[8,4480]{1,0:T(8,128)S(1)}, f32[8,4480]{1,0:T(8,128)S(1)}, f32[8,4480]{1,0:T(8,128)S(1)}, f32[8,4480]{1,0:T(8,128)S(1)}, f32[3,4,8,2368]{3,2,1,0:T...) custom-call(s32[1]{0:T(128)} %bitcast.me_ref, s32[2,32]{1,0:T(2,128)} %old_ref.1, s32[2,32]{1,0:T(2,128)} %new_ref.1, ...), custom_call_target="tpu_custom_call" | custom-call | tf_op jit(solution)/shard_map/prep/pallas_call | solution.py:155
  3.3 1.6 %collective-permute-start.2 = (f32[1,128]{1,0:T(1,128)S(1)}, f32[1,128]{1,0:T(1,128)S(1)}, u32[]{:S(2)}, u32[]{:S(2)}) collective-permute-start(f32[1,128]{1,0:T(1,128)S(1)} %get-tuple-element.28), channel_id=1, source_target_pairs={{0,6},{1,7},{2,4},{3,5},{4,2},{5,3},{6,0},{7,1},{8,14},{9,15},{10,... | collective-permute-start | bytes 1544 | tf_op jit(solution)/shard_map/ppermute | solution.py:309
  4.9 1.2 %collective-permute-start.1 = (f32[1,128]{1,0:T(1,128)S(1)}, f32[1,128]{1,0:T(1,128)S(1)}, u32[]{:S(2)}, u32[]{:S(2)}) collective-permute-start(f32[1,128]{1,0:T(1,128)S(1)} %get-tuple-element.28), channel_id=1, source_target_pairs={{0,4},{1,5},{2,6},{3,7},{4,0},{5,1},{6,2},{7,3},{8,12},{9,13},{10,... | collective-permute-start | bytes 1544 | tf_op jit(solution)/shard_map/ppermute | solution.py:309
  6.2 1.2 %collective-permute-start = (f32[1,128]{1,0:T(1,128)S(1)}, f32[1,128]{1,0:T(1,128)S(1)}, u32[]{:S(2)}, u32[]{:S(2)}) collective-permute-start(f32[1,128]{1,0:T(1,128)S(1)} %get-tuple-element.28), channel_id=1, source_target_pairs={{0,2},{1,3},{2,0},{3,1},{4,6},{5,7},{6,4},{7,5},{8,10},{9,11},{10,... | collective-permute-start | bytes 1544 | tf_op jit(solution)/shard_map/ppermute | solution.py:309
  7.4 2.0 %collective-permute-done.1 = f32[1,128]{1,0:T(1,128)S(1)} collective-permute-done((f32[1,128]{1,0:T(1,128)S(1)}, f32[1,128]{1,0:T(1,128)S(1)}, u32[]{:S(2)}, u32[]{:S(2)}) %collective-permute-start.1) | collective-permute-done | bytes 544 | tf_op jit(solution)/shard_map/ppermute | solution.py:309
  10.9 1.4 %collective-permute-start.6 = (f32[1,128]{1,0:T(1,128)S(1)}, f32[1,128]{1,0:T(1,128)S(1)}, u32[]{:S(2)}, u32[]{:S(2)}) collective-permute-start(f32[1,128]{1,0:T(1,128)S(1)} %add.39), channel_id=1, source_target_pairs={{0,24},{8,16},{16,8},{24,0},{1,25},{9,17},{17,9},{25,1},{2,26},{10... | collective-permute-start | bytes 1544 | tf_op jit(solution)/shard_map/ppermute | solution.py:320
  12.4 1.5 %collective-permute-start.5 = (f32[1,128]{1,0:T(1,128)S(1)}, f32[1,128]{1,0:T(1,128)S(1)}, u32[]{:S(2)}, u32[]{:S(2)}) collective-permute-start(f32[1,128]{1,0:T(1,128)S(1)} %add.39), channel_id=1, source_target_pairs={{0,16},{8,24},{16,0},{24,8},{1,17},{9,25},{17,1},{25,9},{2,18},{10... | collective-permute-start | bytes 1544 | tf_op jit(solution)/shard_map/ppermute | solution.py:320
  14.4 2.2 %collective-permute-start.7 = (f32[8,4480]{1,0:T(8,128)S(1)}, f32[8,4480]{1,0:T(8,128)S(1)}, u32[]{:S(2)}, u32[]{:S(2)}) collective-permute-start(f32[8,4480]{1,0:T(8,128)S(1)} %get-tuple-element.32), channel_id=1, source_target_pairs={{0,2},{1,3},{2,0},{3,1},{4,6},{5,7},{6,4},{7,5},{8,10},{9,11},{10,... | collective-permute-start | bytes 430088 | tf_op jit(solution)/shard_map/ppermute | solution.py:309
  16.6 2.0 %collective-permute-start.8 = (f32[8,4480]{1,0:T(8,128)S(1)}, f32[8,4480]{1,0:T(8,128)S(1)}, u32[]{:S(2)}, u32[]{:S(2)}) collective-permute-start(f32[8,4480]{1,0:T(8,128)S(1)} %get-tuple-element.33), channel_id=1, source_target_pairs={{0,4},{1,5},{2,6},{3,7},{4,0},{5,1},{6,2},{7,3},{8,12},{9,13},{10,... | collective-permute-start | bytes 430088 | tf_op jit(solution)/shard_map/ppermute | solution.py:309
  19.2 2.3 %collective-permute-start.16 = (f32[8,4736]{1,0:T(8,128)S(1)}, f32[8,4736]{1,0:T(8,128)S(1)}, u32[]{:S(2)}, u32[]{:S(2)}) collective-permute-start(f32[8,4736]{1,0:T(8,128)S(1)} %get-tuple-element.38), channel_id=1, source_target_pairs={{0,2},{1,3},{2,0},{3,1},{4,6},{5,7},{6,4},{7,5},{8,10},{9,11},{10,... | collective-permute-start | bytes 454664 | tf_op jit(solution)/shard_map/ppermute | solution.py:309
  22.7 5.5 %collective-permute-done.8.rest_2_ = f32[8,4480]{1,0:T(8,128)S(1)} collective-permute-done((f32[8,4480]{1,0:T(8,128)S(1)}, f32[8,4480]{1,0:T(8,128)S(1)}, u32[]{:S(2)}, u32[]{:S(2)}) %collective-permute-start.8) | collective-permute-done | bytes 143392 | tf_op jit(solution)/shard_map/ppermute | solution.py:309
  28.2 9.8 %collective-permute-done.9.rest_3_ = f32[8,4480]{1,0:T(8,128)S(1)} collective-permute-done((f32[8,4480]{1,0:T(8,128)S(1)}, f32[8,4480]{1,0:T(8,128)S(1)}, u32[]{:S(2)}, u32[]{:S(2)}) %collective-permute-start.9) | collective-permute-done | bytes 143392 | tf_op jit(solution)/shard_map/ppermute | solution.py:309
  38.7 2.0 %collective-permute-done.17.rest_2_ = f32[8,4736]{1,0:T(8,128)S(1)} collective-permute-done((f32[8,4736]{1,0:T(8,128)S(1)}, f32[8,4736]{1,0:T(8,128)S(1)}, u32[]{:S(2)}, u32[]{:S(2)}) %collective-permute-start.17) | collective-permute-done | bytes 151584 | tf_op jit(solution)/shard_map/ppermute | solution.py:309
  40.7 2.7 %collective-permute-done.18.rest_3_ = f32[8,4736]{1,0:T(8,128)S(1)} collective-permute-done((f32[8,4736]{1,0:T(8,128)S(1)}, f32[8,4736]{1,0:T(8,128)S(1)}, u32[]{:S(2)}, u32[]{:S(2)}) %collective-permute-start.18) | collective-permute-done | bytes 151584 | tf_op jit(solution)/shard_map/ppermute | solution.py:309
  44.0 2.1 %pick.2 = (f32[8,3968]{1,0:T(8,128)S(1)}, f32[8,3968]{1,0:T(8,128)}, f32[8,3968]{1,0:T(8,128)S(1)}, f32[8,3968]{1,0:T(8,128)S(1)}) custom-call(s32[1,128]{1,0:T(1,128)S(1)} %get-tuple-element.27.notes, f32[1,128]{1,0:T(1,128)S(1)} %get-tuple-element.30.clip, f32[8,4480]{1,0:T(8,128)S(1)} %get-tuple-element.31.rest_0_, ...), custom_call_target="tpu_custom_call" | custom-call | tf_op jit(solution)/shard_map/pick/pallas_call | solution.py:230
  46.0 3.5 %collective-permute-start.14 = (f32[8,3968]{1,0:T(8,128)S(1)}, f32[8,3968]{1,0:T(8,128)S(1)}, u32[]{:S(2)}, u32[]{:S(2)}) collective-permute-start(f32[8,3968]{1,0:T(8,128)S(1)} %get-tuple-element.35), channel_id=1, source_target_pairs={{0,4},{1,5},{2,6},{3,7},{4,0},{5,1},{6,2},{7,3},{8,12},{9,13},{10,... | collective-permute-start | bytes 380936 | tf_op jit(solution)/shard_map/ppermute | solution.py:309
  50.7 2.4 %collective-permute-start.23 = (f32[8,4736]{1,0:T(8,128)S(1)}, f32[8,4736]{1,0:T(8,128)S(1)}, u32[]{:S(2)}, u32[]{:S(2)}) collective-permute-start(f32[8,4736]{1,0:T(8,128)S(1)} %get-tuple-element.41), channel_id=1, source_target_pairs={{0,4},{1,5},{2,6},{3,7},{4,0},{5,1},{6,2},{7,3},{8,12},{9,13},{10,... | collective-permute-start | bytes 454664 | tf_op jit(solution)/shard_map/ppermute | solution.py:309
  53.8 1.4 %collective-permute-start.26 = (f32[8,4736]{1,0:T(8,128)S(1)}, f32[8,4736]{1,0:T(8,128)S(1)}, u32[]{:S(2)}, u32[]{:S(2)}) collective-permute-start(f32[8,4736]{1,0:T(8,128)S(1)} %get-tuple-element.46), channel_id=1, source_target_pairs={{0,2},{1,3},{2,0},{3,1},{4,6},{5,7},{6,4},{7,5},{8,10},{9,11},{10,... | collective-permute-start | bytes 454664 | tf_op jit(solution)/shard_map/ppermute | solution.py:309
  55.2 5.4 %multiply_subtract_fusion = (f32[2,4,16,2880]{3,2,1,0:T(8,128)}, f32[2,4,16,2880]{3,2,1,0:T(8,128)}, f32[2,4,16,2880]{3,2,1,0:T(8,128)}) fusion(f32[2,4,16,2880]{3,2,1,0:T(8,128)} %master.1, f32[]{:T(128)S(1)} %bitcast.3, bf16[2,4,16,2880]{3,2,1,0:T(8,128)(2,1)} %grad.1, f32[2,4,16,2880]{3,2,1,0:T(8,128)} %mone.1, f32[2,4,16,2880]{3,2,1,0:T(8,128)} %mtwo.1), kind=kLoop, calls=%fused_computation.2 | loop fusion | flops 6266880 | bytes 9584644 | tf_op jit(solution)/shard_map/sub | solution.py:51
  60.6 6.6 %collective-permute-done.26.rest_3_ = f32[8,4736]{1,0:T(8,128)S(1)} collective-permute-done((f32[8,4736]{1,0:T(8,128)S(1)}, f32[8,4736]{1,0:T(8,128)S(1)}, u32[]{:S(2)}, u32[]{:S(2)}) %collective-permute-start.26) | collective-permute-done | bytes 151584 | tf_op jit(solution)/shard_map/ppermute | solution.py:309
  67.2 1.2 %land.2 = (f32[2,4,16,2880]{3,2,1,0:T(8,128)}, f32[2,4,16,2880]{3,2,1,0:T(8,128)}, f32[2,4,16,2880]{3,2,1,0:T(8,128)}) custom-call(s32[1,128]{1,0:T(1,128)S(1)} %get-tuple-element.27.notes, f32[8,3968]{1,0:T(8,128)S(1)} %get-tuple-element.43.rest_0_, ...), custom_call_target="tpu_custom_call", output_to_operand_aliasing={{0}: (5, {}), {1}: (6, {}), {2}: (7, {})} | custom-call | tf_op jit(solution)/shard_map/land/pallas_call | solution.py:287
  68.5 2.6 %collective-permute-done.23.rest_2_ = f32[8,4736]{1,0:T(8,128)S(1)} collective-permute-done((f32[8,4736]{1,0:T(8,128)S(1)}, f32[8,4736]{1,0:T(8,128)S(1)}, u32[]{:S(2)}, u32[]{:S(2)}) %collective-permute-start.23) | collective-permute-done | bytes 151584 | tf_op jit(solution)/shard_map/ppermute | solution.py:309
  71.1 3.1 %collective-permute-done.24.rest_3_ = f32[8,4736]{1,0:T(8,128)S(1)} collective-permute-done((f32[8,4736]{1,0:T(8,128)S(1)}, f32[8,4736]{1,0:T(8,128)S(1)}, u32[]{:S(2)}, u32[]{:S(2)}) %collective-permute-start.24) | collective-permute-done | bytes 151584 | tf_op jit(solution)/shard_map/ppermute | solution.py:309
  74.2 1.2 %land.3 = (f32[2,4,16,2880]{3,2,1,0:T(8,128)}, f32[2,4,16,2880]{3,2,1,0:T(8,128)}, f32[2,4,16,2880]{3,2,1,0:T(8,128)}) custom-call(s32[1,128]{1,0:T(1,128)S(1)} %get-tuple-element.27.notes, f32[8,3968]{1,0:T(8,128)S(1)} %collective-permute-done.14.rest_0_, ...), custom_call_target="tpu_custom_call", output_to_operand_aliasing={{0}: (5, {}), {1}: (6, {}), {2}: (7, {})} | custom-call | tf_op jit(solution)/shard_map/land/pallas_call | solution.py:287
  (42 shorter events, 6.9 us)
Async XLA Ops:
  4.9 4.5 %collective-permute-start.1 = (f32[1,128]{1,0:T(1,128)S(1)}, f32[1,128]{1,0:T(1,128)S(1)}, u32[]{:S(2)}, u32[]{:S(2)}) collective-permute-start(f32[1,128]{1,0:T(1,128)S(1)} %get-tuple-element.28), channel_id=1, source_target_pairs={{0,4},{1,5},{2,6},{3,7},{4,0},{5,1},{6,2},{7,3},{8,12},{9,13},{10,... | collective-permute-start | bytes 1544 | tf_op jit(solution)/shard_map/ppermute | solution.py:309
  10.9 7.7 %collective-permute-start.6 = (f32[1,128]{1,0:T(1,128)S(1)}, f32[1,128]{1,0:T(1,128)S(1)}, u32[]{:S(2)}, u32[]{:S(2)}) collective-permute-start(f32[1,128]{1,0:T(1,128)S(1)} %add.39), channel_id=1, source_target_pairs={{0,24},{8,16},{16,8},{24,0},{1,25},{9,17},{17,9},{25,1},{2,26},{10... | collective-permute-start | bytes 1544 | tf_op jit(solution)/shard_map/ppermute | solution.py:320
  12.4 6.2 %collective-permute-start.5 = (f32[1,128]{1,0:T(1,128)S(1)}, f32[1,128]{1,0:T(1,128)S(1)}, u32[]{:S(2)}, u32[]{:S(2)}) collective-permute-start(f32[1,128]{1,0:T(1,128)S(1)} %add.39), channel_id=1, source_target_pairs={{0,16},{8,24},{16,0},{24,8},{1,17},{9,25},{17,1},{25,9},{2,18},{10... | collective-permute-start | bytes 1544 | tf_op jit(solution)/shard_map/ppermute | solution.py:320
  13.9 4.8 %collective-permute-start.4 = (f32[1,128]{1,0:T(1,128)S(1)}, f32[1,128]{1,0:T(1,128)S(1)}, u32[]{:S(2)}, u32[]{:S(2)}) collective-permute-start(f32[1,128]{1,0:T(1,128)S(1)} %add.39), channel_id=1, source_target_pairs={{0,8},{8,0},{16,24},{24,16},{1,9},{9,1},{17,25},{25,17},{2,10},{10... | collective-permute-start | bytes 1544 | tf_op jit(solution)/shard_map/ppermute | solution.py:320
  14.4 7.2 %collective-permute-start.7 = (f32[8,4480]{1,0:T(8,128)S(1)}, f32[8,4480]{1,0:T(8,128)S(1)}, u32[]{:S(2)}, u32[]{:S(2)}) collective-permute-start(f32[8,4480]{1,0:T(8,128)S(1)} %get-tuple-element.32), channel_id=1, source_target_pairs={{0,2},{1,3},{2,0},{3,1},{4,6},{5,7},{6,4},{7,5},{8,10},{9,11},{10,... | collective-permute-start | bytes 430088 | tf_op jit(solution)/shard_map/ppermute | solution.py:309
  16.6 11.6 %collective-permute-start.8 = (f32[8,4480]{1,0:T(8,128)S(1)}, f32[8,4480]{1,0:T(8,128)S(1)}, u32[]{:S(2)}, u32[]{:S(2)}) collective-permute-start(f32[8,4480]{1,0:T(8,128)S(1)} %get-tuple-element.33), channel_id=1, source_target_pairs={{0,4},{1,5},{2,6},{3,7},{4,0},{5,1},{6,2},{7,3},{8,12},{9,13},{10,... | collective-permute-start | bytes 430088 | tf_op jit(solution)/shard_map/ppermute | solution.py:309
  18.6 19.5 %collective-permute-start.9 = (f32[8,4480]{1,0:T(8,128)S(1)}, f32[8,4480]{1,0:T(8,128)S(1)}, u32[]{:S(2)}, u32[]{:S(2)}) collective-permute-start(f32[8,4480]{1,0:T(8,128)S(1)} %get-tuple-element.34), channel_id=1, source_target_pairs={{0,6},{1,7},{2,4},{3,5},{4,2},{5,3},{6,0},{7,1},{8,14},{9,15},{10,... | collective-permute-start | bytes 430088 | tf_op jit(solution)/shard_map/ppermute | solution.py:309
  18.6 19.5 %collective-permute-start.10 = (f32[8,4480]{1,0:T(8,128)S(1)}, f32[8,4480]{1,0:T(8,128)S(1)}, u32[]{:S(2)}, u32[]{:S(2)}) collective-permute-start(f32[8,4480]{1,0:T(8,128)S(1)} %get-tuple-element.31.rest_0_), channel_id=1, source_target_pairs={{0,1},{1,0},{2,3},{3,2},{4,5},{5,4},{6,7},{7,6},{8,9},{9,8},{10,11... | collective-permute-start | bytes 430088 | tf_op jit(solution)/shard_map/ppermute | solution.py:326
  19.2 19.4 %collective-permute-start.16 = (f32[8,4736]{1,0:T(8,128)S(1)}, f32[8,4736]{1,0:T(8,128)S(1)}, u32[]{:S(2)}, u32[]{:S(2)}) collective-permute-start(f32[8,4736]{1,0:T(8,128)S(1)} %get-tuple-element.38), channel_id=1, source_target_pairs={{0,2},{1,3},{2,0},{3,1},{4,6},{5,7},{6,4},{7,5},{8,10},{9,11},{10,... | collective-permute-start | bytes 454664 | tf_op jit(solution)/shard_map/ppermute | solution.py:309
  21.6 19.0 %collective-permute-start.17 = (f32[8,4736]{1,0:T(8,128)S(1)}, f32[8,4736]{1,0:T(8,128)S(1)}, u32[]{:S(2)}, u32[]{:S(2)}) collective-permute-start(f32[8,4736]{1,0:T(8,128)S(1)} %get-tuple-element.39), channel_id=1, source_target_pairs={{0,4},{1,5},{2,6},{3,7},{4,0},{5,1},{6,2},{7,3},{8,12},{9,13},{10,... | collective-permute-start | bytes 454664 | tf_op jit(solution)/shard_map/ppermute | solution.py:309
  28.2 15.1 %collective-permute-start.18 = (f32[8,4736]{1,0:T(8,128)S(1)}, f32[8,4736]{1,0:T(8,128)S(1)}, u32[]{:S(2)}, u32[]{:S(2)}) collective-permute-start(f32[8,4736]{1,0:T(8,128)S(1)} %get-tuple-element.40), channel_id=1, source_target_pairs={{0,6},{1,7},{2,4},{3,5},{4,2},{5,3},{6,0},{7,1},{8,14},{9,15},{10,... | collective-permute-start | bytes 454664 | tf_op jit(solution)/shard_map/ppermute | solution.py:309
  38.1 5.3 %collective-permute-start.11 = (f32[8,4480]{1,0:T(8,128)S(1)}, f32[8,4480]{1,0:T(8,128)S(1)}, u32[]{:S(2)}, u32[]{:S(2)}) collective-permute-start(f32[8,4480]{1,0:T(8,128)S(1)} %collective-permute-done.7.rest_1_), channel_id=1, source_target_pairs={{0,1},{1,0},{2,3},{3,2},{4,5},{5,4},{6,7},{7,6},{8,9},{9,8},{10,11... | collective-permute-start | bytes 430088 | tf_op jit(solution)/shard_map/ppermute | solution.py:326
  38.1 5.8 %collective-permute-start.12 = (f32[8,4480]{1,0:T(8,128)S(1)}, f32[8,4480]{1,0:T(8,128)S(1)}, u32[]{:S(2)}, u32[]{:S(2)}) collective-permute-start(f32[8,4480]{1,0:T(8,128)S(1)} %collective-permute-done.8.rest_2_), channel_id=1, source_target_pairs={{0,1},{1,0},{2,3},{3,2},{4,5},{5,4},{6,7},{7,6},{8,9},{9,8},{10,11... | collective-permute-start | bytes 430088 | tf_op jit(solution)/shard_map/ppermute | solution.py:326
  38.6 5.4 %collective-permute-start.13 = (f32[8,4480]{1,0:T(8,128)S(1)}, f32[8,4480]{1,0:T(8,128)S(1)}, u32[]{:S(2)}, u32[]{:S(2)}) collective-permute-start(f32[8,4480]{1,0:T(8,128)S(1)} %collective-permute-done.9.rest_3_), channel_id=1, source_target_pairs={{0,1},{1,0},{2,3},{3,2},{4,5},{5,4},{6,7},{7,6},{8,9},{9,8},{10,11... | collective-permute-start | bytes 430088 | tf_op jit(solution)/shard_map/ppermute | solution.py:326
  40.7 5.4 %collective-permute-start.19 = (f32[8,4736]{1,0:T(8,128)S(1)}, f32[8,4736]{1,0:T(8,128)S(1)}, u32[]{:S(2)}, u32[]{:S(2)}) collective-permute-start(f32[8,4736]{1,0:T(8,128)S(1)} %get-tuple-element.37.rest_0_), channel_id=1, source_target_pairs={{0,1},{1,0},{2,3},{3,2},{4,5},{5,4},{6,7},{7,6},{8,9},{9,8},{10,11... | collective-permute-start | bytes 454664 | tf_op jit(solution)/shard_map/ppermute | solution.py:326
  43.4 6.1 %collective-permute-start.20 = (f32[8,4736]{1,0:T(8,128)S(1)}, f32[8,4736]{1,0:T(8,128)S(1)}, u32[]{:S(2)}, u32[]{:S(2)}) collective-permute-start(f32[8,4736]{1,0:T(8,128)S(1)} %collective-permute-done.16.rest_1_), channel_id=1, source_target_pairs={{0,1},{1,0},{2,3},{3,2},{4,5},{5,4},{6,7},{7,6},{8,9},{9,8},{10,11... | collective-permute-start | bytes 454664 | tf_op jit(solution)/shard_map/ppermute | solution.py:326
  43.4 6.1 %collective-permute-start.21 = (f32[8,4736]{1,0:T(8,128)S(1)}, f32[8,4736]{1,0:T(8,128)S(1)}, u32[]{:S(2)}, u32[]{:S(2)}) collective-permute-start(f32[8,4736]{1,0:T(8,128)S(1)} %collective-permute-done.17.rest_2_), channel_id=1, source_target_pairs={{0,1},{1,0},{2,3},{3,2},{4,5},{5,4},{6,7},{7,6},{8,9},{9,8},{10,11... | collective-permute-start | bytes 454664 | tf_op jit(solution)/shard_map/ppermute | solution.py:326
  43.9 5.6 %collective-permute-start.22 = (f32[8,4736]{1,0:T(8,128)S(1)}, f32[8,4736]{1,0:T(8,128)S(1)}, u32[]{:S(2)}, u32[]{:S(2)}) collective-permute-start(f32[8,4736]{1,0:T(8,128)S(1)} %collective-permute-done.18.rest_3_), channel_id=1, source_target_pairs={{0,1},{1,0},{2,3},{3,2},{4,5},{5,4},{6,7},{7,6},{8,9},{9,8},{10,11... | collective-permute-start | bytes 454664 | tf_op jit(solution)/shard_map/ppermute | solution.py:326
  46.0 7.8 %collective-permute-start.25 = (f32[8,3968]{1,0:T(8,128)}, f32[8,3968]{1,0:T(8,128)S(1)}, u32[]{:S(2)}, u32[]{:S(2)}) collective-permute-start(f32[8,3968]{1,0:T(8,128)} %get-tuple-element.44), channel_id=1, source_target_pairs={{0,2},{1,3},{2,0},{3,1},{4,6},{5,7},{6,4},{7,5},{8,10},{9,11},{10,... | collective-permute-start | bytes 380936 | tf_op jit(solution)/shard_map/ppermute | solution.py:309
  46.0 22.4 %collective-permute-start.14 = (f32[8,3968]{1,0:T(8,128)S(1)}, f32[8,3968]{1,0:T(8,128)S(1)}, u32[]{:S(2)}, u32[]{:S(2)}) collective-permute-start(f32[8,3968]{1,0:T(8,128)S(1)} %get-tuple-element.35), channel_id=1, source_target_pairs={{0,4},{1,5},{2,6},{3,7},{4,0},{5,1},{6,2},{7,3},{8,12},{9,13},{10,... | collective-permute-start | bytes 380936 | tf_op jit(solution)/shard_map/ppermute | solution.py:309
  49.5 19.0 %collective-permute-start.15 = (f32[8,3968]{1,0:T(8,128)S(1)}, f32[8,3968]{1,0:T(8,128)S(1)}, u32[]{:S(2)}, u32[]{:S(2)}) collective-permute-start(f32[8,3968]{1,0:T(8,128)S(1)} %get-tuple-element.36), channel_id=1, source_target_pairs={{0,6},{1,7},{2,4},{3,5},{4,2},{5,3},{6,0},{7,1},{8,14},{9,15},{10,... | collective-permute-start | bytes 380936 | tf_op jit(solution)/shard_map/ppermute | solution.py:309
  50.7 20.4 %collective-permute-start.23 = (f32[8,4736]{1,0:T(8,128)S(1)}, f32[8,4736]{1,0:T(8,128)S(1)}, u32[]{:S(2)}, u32[]{:S(2)}) collective-permute-start(f32[8,4736]{1,0:T(8,128)S(1)} %get-tuple-element.41), channel_id=1, source_target_pairs={{0,4},{1,5},{2,6},{3,7},{4,0},{5,1},{6,2},{7,3},{8,12},{9,13},{10,... | collective-permute-start | bytes 454664 | tf_op jit(solution)/shard_map/ppermute | solution.py:309
  53.1 21.0 %collective-permute-start.24 = (f32[8,4736]{1,0:T(8,128)S(1)}, f32[8,4736]{1,0:T(8,128)S(1)}, u32[]{:S(2)}, u32[]{:S(2)}) collective-permute-start(f32[8,4736]{1,0:T(8,128)S(1)} %get-tuple-element.42), channel_id=1, source_target_pairs={{0,6},{1,7},{2,4},{3,5},{4,2},{5,3},{6,0},{7,1},{8,14},{9,15},{10,... | collective-permute-start | bytes 454664 | tf_op jit(solution)/shard_map/ppermute | solution.py:309
  53.8 13.4 %collective-permute-start.26 = (f32[8,4736]{1,0:T(8,128)S(1)}, f32[8,4736]{1,0:T(8,128)S(1)}, u32[]{:S(2)}, u32[]{:S(2)}) collective-permute-start(f32[8,4736]{1,0:T(8,128)S(1)} %get-tuple-element.46), channel_id=1, source_target_pairs={{0,2},{1,3},{2,0},{3,1},{4,6},{5,7},{6,4},{7,5},{8,10},{9,11},{10,... | collective-permute-start | bytes 454664 | tf_op jit(solution)/shard_map/ppermute | solution.py:309
  (4 other events, 44.8 us)

commit v6 on v5

--- a/solution.py
+++ b/solution.py
@@ -87,13 +87,13 @@
     return i ^ x if n & (n - 1) == 0 else lax.rem(i + x, n)
 
 
-def prep_kernel(sz, me_ref, old_ref, new_ref, master, mone, mtwo, grad, *rest):
+def prep_kernel(sz, old_ref, new_ref, master, mone, mtwo, grad, *rest):
     c = sz.chips
     pieces = rest[:c]
     late_raw, total, notes, plan, mv, m1v, m2v, gv, st, sem_g, sem = rest[c:]
     for i in range(sz.layers):
         pltpu.make_async_copy(grad.at[i], gv.at[i], sem_g.at[i]).start()
-    me = me_ref[0]
+    me = lax.axis_index("expert")
     chip = lax.div(me, CORES)
     n_slots = sz.layers * sz.group
 
@@ -144,7 +144,7 @@
             late_raw[a, x] = st[a + 1, k, :, sz.early :]
 
 
-def prep(sz, me, old_slot, new_slot, master, mone, mtwo, grad):
+def prep(sz, old_slot, new_slot, master, mone, mtwo, grad):
     f32 = jnp.float32
     slot = (sz.layers, sz.rows, sz.cols)
     outs = [out(sz.piece, width(sz.groups[0], 3))] * sz.chips + [
@@ -154,7 +154,7 @@
     ]
     return pl.pallas_call(
         functools.partial(prep_kernel, sz),
-        in_specs=[SMEM, SMEM, SMEM, ANY, ANY, ANY, ANY],
+        in_specs=[SMEM, SMEM, ANY, ANY, ANY, ANY],
         out_specs=[VMEM] * (sz.chips + 3),
         out_shape=outs,
         scratch_shapes=[
@@ -168,7 +168,7 @@
             pltpu.SemaphoreType.DMA((sz.layers, 3)),
         ],
         name="prep",
-    )(me, old_slot, new_slot, master, mone, mtwo, grad)
+    )(old_slot, new_slot, master, mone, mtwo, grad)
 
 
 def scale_kernel(sz, total, raw, clip, clip_copy, *late):
@@ -201,7 +201,7 @@
     outs = rest[2 * c : 3 * c]
     head, _, size, stride = group
     at = [head + a * stride for a in range(3)]
-    me = read(notes, sz.layers * (sz.group + 1))
+    me = lax.axis_index("expert")
     chip = lax.div(me, CORES)
     core = lax.rem(me, CORES)
     layer = lax.div(chip, sz.per_layer)
@@ -242,29 +242,34 @@
     outs = rest[2 * n + 3 : 2 * n + 6]
     st, full, sem = rest[2 * n + 6 :]
     n_slots = sz.layers * sz.group
-    chip = lax.div(read(notes, n_slots + sz.layers), CORES)
+    chip = lax.div(lax.axis_index("expert"), CORES)
     e, f = sz.early, sz.full
     copies = []
     for j, x in enumerate(which):
         k = dyn_peer(chip, x, c) if c & (c - 1) == 0 else lax.rem(chip - x + c, c)
         a, b = early[j], late[j]
         spot = j if sz.by_piece else k
-        first, second = a[:, f : f + e], a[:, f + e : f + 2 * e]
-        st[0, spot, :, :e] = new_weights(a[:, :e], first, second)
-        st[1, spot, :, :e] = first
-        st[2, spot, :, :e] = second
+        first_e, second_e = a[:, f : f + e], a[:, f + e : f + 2 * e]
         first, second = b[:, : sz.late], b[:, sz.lat : sz.lat + sz.late]
-        st[0, spot, :, e:] = new_weights(a[:, e : sz.cols], first, second)
-        st[1, spot, :, e:] = first
-        st[2, spot, :, e:] = second
-        if sz.by_piece:
-            layer = lax.div(k, sz.per_layer)
-            row = pl.multiple_of(lax.rem(k, sz.per_layer) * sz.piece, sz.piece)
-            slot = read(notes, n_slots + layer)
-            for i in range(3):
+        layer = lax.div(k, sz.per_layer)
+        row = pl.multiple_of(lax.rem(k, sz.per_layer) * sz.piece, sz.piece)
+        slot = read(notes, n_slots + layer)
+
+        def send(i):
+            if sz.by_piece:
                 there = outs[i].at[layer, slot, pl.ds(row, sz.piece)]
                 copies.append(pltpu.make_async_copy(st.at[i, j], there, sem.at[i, j]))
                 copies[-1].start()
+
+        st[1, spot, :, :e] = first_e
+        st[1, spot, :, e:] = first
+        send(1)
+        st[2, spot, :, :e] = second_e
+        st[2, spot, :, e:] = second
+        send(2)
+        st[0, spot, :, :e] = new_weights(a[:, :e], first_e, second_e)
+        st[0, spot, :, e:] = new_weights(a[:, e : sz.cols], first, second)
+        send(0)
     if not sz.by_piece:
         for i in range(sz.layers):
             slot = read(notes, n_slots + i)
@@ -328,9 +333,8 @@
 
 def shards(master, moment_one, moment_two, gradient, old_slot, new_slot):
     sz = Sizes(master.shape, lax.axis_size("expert"), lax.axis_size("dp"))
-    me = lax.axis_index("expert").reshape(1)
-    c = sz.chips
-    got = prep(sz, me, old_slot, new_slot, master, moment_one, moment_two, gradient)
+    c = sz.chips
+    got = prep(sz, old_slot, new_slot, master, moment_one, moment_two, gradient)
     pieces, raw, total = list(got[:c]), got[c], got[c + 1]
     (notes,) = near([got[c + 2]])
     totals = shifts(sz, [total] * c)

time: 76 us -> 75.6 us (level)
  transfers between devices with their start and end apart: 27 -> 27, of which waited for: 11 -> 12; matrix products, arithmetic and copies ran while one was open for 7% -> 7% of each run, Pallas kernels for 7% -> 6%
where the time goes in v6:
time: 75.6 us; the launch traced here: 75.1 us
  waiting for transfers between devices  36.3 us (48%)
  starting transfers between devices  24.4 us (32%)
  Pallas kernels  8.19 us (11%)
  other arithmetic  5.46 us (7%)
    ppermute x15, waiting for transfers between devices, shifts(): got[x] = lax.ppermute(arrays[x], 'expert', pairs)  35.1 us
    ppermute x15, starting transfers between devices, shifts(): got[x] = lax.ppermute(arrays[x], 'expert', pairs)  19.7 us
    sub x1, other arithmetic, new_weights(): return master - LEARN_RATE * (step_dir + DECAY_RATE * master)  5.44 us
    ppermute x3, starting transfers between devices, from_others(): lax.ppermute(value, axis, [(i, peer(i, x, n)) for i in range(n)])  3.49 us
    pallas_call x2, Pallas kernels, pick(): pl.pallas_call(functools.partial(pick_kernel, sz, group), in_specs=[VMEM]...  2.85 us
    pallas_call x1, Pallas kernels, prep(): pl.pallas_call(functools.partial(prep_kernel, sz), in_specs=[SMEM, SMEM,...  2.67 us
    pallas_call x2, Pallas kernels, land(): pl.pallas_call(functools.partial(land_kernel, sz, which), in_specs=[VMEM]...  2.14 us
  transfers between devices with their start and end apart: 27, of which 12 were waited for; matrix products, arithmetic and copies ran while one was open for 7% of the time, Pallas kernels for 6%

profile of v6, /device:TPU:12, one launch (start us, length us, event | category | flops | bytes accessed | tf_op | source)
XLA Modules:
  0.0 75.1 jit_solution(18249632515148482804)
XLA Ops:
  0.6 2.7 %prep.1 = (f32[8,4480]{1,0:T(8,128)S(1)}, f32[8,4480]{1,0:T(8,128)S(1)}, f32[8,4480]{1,0:T(8,128)S(1)}, f32[8,4480]{1,0:T(8,128)S(1)}, f32[3,4,8,2368]{3,2,1,0:T...) custom-call(s32[2,32]{1,0:T(2,128)} %old_ref.1, s32[2,32]{1,0:T(2,128)} %new_ref.1, f32[2,4,16,2880]{3,2,1,0:T(8,128)} %master.1, ...), custom_call_target="tpu_custom_call" | custom-call | tf_op jit(solution)/shard_map/prep/pallas_call | solution.py:155
  3.3 1.6 %collective-permute-start.2 = (f32[1,128]{1,0:T(1,128)S(1)}, f32[1,128]{1,0:T(1,128)S(1)}, u32[]{:S(2)}, u32[]{:S(2)}) collective-permute-start(f32[1,128]{1,0:T(1,128)S(1)} %get-tuple-element.28), channel_id=1, source_target_pairs={{0,6},{1,7},{2,4},{3,5},{4,2},{5,3},{6,0},{7,1},{8,14},{9,15},{10,... | collective-permute-start | bytes 1544 | tf_op jit(solution)/shard_map/ppermute | solution.py:314
  5.0 1.2 %collective-permute-start.1 = (f32[1,128]{1,0:T(1,128)S(1)}, f32[1,128]{1,0:T(1,128)S(1)}, u32[]{:S(2)}, u32[]{:S(2)}) collective-permute-start(f32[1,128]{1,0:T(1,128)S(1)} %get-tuple-element.28), channel_id=1, source_target_pairs={{0,4},{1,5},{2,6},{3,7},{4,0},{5,1},{6,2},{7,3},{8,12},{9,13},{10,... | collective-permute-start | bytes 1544 | tf_op jit(solution)/shard_map/ppermute | solution.py:314
  6.2 1.2 %collective-permute-start = (f32[1,128]{1,0:T(1,128)S(1)}, f32[1,128]{1,0:T(1,128)S(1)}, u32[]{:S(2)}, u32[]{:S(2)}) collective-permute-start(f32[1,128]{1,0:T(1,128)S(1)} %get-tuple-element.28), channel_id=1, source_target_pairs={{0,2},{1,3},{2,0},{3,1},{4,6},{5,7},{6,4},{7,5},{8,10},{9,11},{10,... | collective-permute-start | bytes 1544 | tf_op jit(solution)/shard_map/ppermute | solution.py:314
  7.4 2.0 %collective-permute-done.1 = f32[1,128]{1,0:T(1,128)S(1)} collective-permute-done((f32[1,128]{1,0:T(1,128)S(1)}, f32[1,128]{1,0:T(1,128)S(1)}, u32[]{:S(2)}, u32[]{:S(2)}) %collective-permute-start.1) | collective-permute-done | bytes 544 | tf_op jit(solution)/shard_map/ppermute | solution.py:314
  9.8 1.2 %collective-permute-done.3 = f32[1,128]{1,0:T(1,128)S(1)} collective-permute-done((f32[1,128]{1,0:T(1,128)S(1)}, f32[1,128]{1,0:T(1,128)S(1)}, u32[]{:S(2)}, u32[]{:S(2)}) %collective-permute-start.3) | collective-permute-done | bytes 544 | tf_op jit(solution)/shard_map/ppermute | solution.py:331
  10.9 1.4 %collective-permute-start.6 = (f32[1,128]{1,0:T(1,128)S(1)}, f32[1,128]{1,0:T(1,128)S(1)}, u32[]{:S(2)}, u32[]{:S(2)}) collective-permute-start(f32[1,128]{1,0:T(1,128)S(1)} %add.39), channel_id=1, source_target_pairs={{0,24},{8,16},{16,8},{24,0},{1,25},{9,17},{17,9},{25,1},{2,26},{10... | collective-permute-start | bytes 1544 | tf_op jit(solution)/shard_map/ppermute | solution.py:325
  12.4 1.5 %collective-permute-start.5 = (f32[1,128]{1,0:T(1,128)S(1)}, f32[1,128]{1,0:T(1,128)S(1)}, u32[]{:S(2)}, u32[]{:S(2)}) collective-permute-start(f32[1,128]{1,0:T(1,128)S(1)} %add.39), channel_id=1, source_target_pairs={{0,16},{8,24},{16,0},{24,8},{1,17},{9,25},{17,1},{25,9},{2,18},{10... | collective-permute-start | bytes 1544 | tf_op jit(solution)/shard_map/ppermute | solution.py:325
  14.4 2.2 %collective-permute-start.7 = (f32[8,4480]{1,0:T(8,128)S(1)}, f32[8,4480]{1,0:T(8,128)S(1)}, u32[]{:S(2)}, u32[]{:S(2)}) collective-permute-start(f32[8,4480]{1,0:T(8,128)S(1)} %get-tuple-element.32), channel_id=1, source_target_pairs={{0,2},{1,3},{2,0},{3,1},{4,6},{5,7},{6,4},{7,5},{8,10},{9,11},{10,... | collective-permute-start | bytes 430088 | tf_op jit(solution)/shard_map/ppermute | solution.py:314
  16.6 2.0 %collective-permute-start.8 = (f32[8,4480]{1,0:T(8,128)S(1)}, f32[8,4480]{1,0:T(8,128)S(1)}, u32[]{:S(2)}, u32[]{:S(2)}) collective-permute-start(f32[8,4480]{1,0:T(8,128)S(1)} %get-tuple-element.33), channel_id=1, source_target_pairs={{0,4},{1,5},{2,6},{3,7},{4,0},{5,1},{6,2},{7,3},{8,12},{9,13},{10,... | collective-permute-start | bytes 430088 | tf_op jit(solution)/shard_map/ppermute | solution.py:314
  19.2 2.3 %collective-permute-start.16 = (f32[8,4736]{1,0:T(8,128)S(1)}, f32[8,4736]{1,0:T(8,128)S(1)}, u32[]{:S(2)}, u32[]{:S(2)}) collective-permute-start(f32[8,4736]{1,0:T(8,128)S(1)} %get-tuple-element.38), channel_id=1, source_target_pairs={{0,2},{1,3},{2,0},{3,1},{4,6},{5,7},{6,4},{7,5},{8,10},{9,11},{10,... | collective-permute-start | bytes 454664 | tf_op jit(solution)/shard_map/ppermute | solution.py:314
  21.6 1.1 %collective-permute-start.17 = (f32[8,4736]{1,0:T(8,128)S(1)}, f32[8,4736]{1,0:T(8,128)S(1)}, u32[]{:S(2)}, u32[]{:S(2)}) collective-permute-start(f32[8,4736]{1,0:T(8,128)S(1)} %get-tuple-element.39), channel_id=1, source_target_pairs={{0,4},{1,5},{2,6},{3,7},{4,0},{5,1},{6,2},{7,3},{8,12},{9,13},{10,... | collective-permute-start | bytes 454664 | tf_op jit(solution)/shard_map/ppermute | solution.py:314
  22.7 5.5 %collective-permute-done.8.rest_2_ = f32[8,4480]{1,0:T(8,128)S(1)} collective-permute-done((f32[8,4480]{1,0:T(8,128)S(1)}, f32[8,4480]{1,0:T(8,128)S(1)}, u32[]{:S(2)}, u32[]{:S(2)}) %collective-permute-start.8) | collective-permute-done | bytes 143392 | tf_op jit(solution)/shard_map/ppermute | solution.py:314
  28.3 9.8 %collective-permute-done.9.rest_3_ = f32[8,4480]{1,0:T(8,128)S(1)} collective-permute-done((f32[8,4480]{1,0:T(8,128)S(1)}, f32[8,4480]{1,0:T(8,128)S(1)}, u32[]{:S(2)}, u32[]{:S(2)}) %collective-permute-start.9) | collective-permute-done | bytes 143392 | tf_op jit(solution)/shard_map/ppermute | solution.py:314
  38.7 2.0 %collective-permute-done.17.rest_2_ = f32[8,4736]{1,0:T(8,128)S(1)} collective-permute-done((f32[8,4736]{1,0:T(8,128)S(1)}, f32[8,4736]{1,0:T(8,128)S(1)}, u32[]{:S(2)}, u32[]{:S(2)}) %collective-permute-start.17) | collective-permute-done | bytes 151584 | tf_op jit(solution)/shard_map/ppermute | solution.py:314
  40.7 2.7 %collective-permute-done.18.rest_3_ = f32[8,4736]{1,0:T(8,128)S(1)} collective-permute-done((f32[8,4736]{1,0:T(8,128)S(1)}, f32[8,4736]{1,0:T(8,128)S(1)}, u32[]{:S(2)}, u32[]{:S(2)}) %collective-permute-start.18) | collective-permute-done | bytes 151584 | tf_op jit(solution)/shard_map/ppermute | solution.py:314
  44.0 1.8 %pick.2 = (f32[8,3968]{1,0:T(8,128)S(1)}, f32[8,3968]{1,0:T(8,128)}, f32[8,3968]{1,0:T(8,128)S(1)}, f32[8,3968]{1,0:T(8,128)S(1)}) custom-call(s32[1,128]{1,0:T(1,128)S(1)} %get-tuple-element.27.notes, f32[1,128]{1,0:T(1,128)S(1)} %get-tuple-element.30.clip, f32[8,4480]{1,0:T(8,128)S(1)} %get-tuple-element.31.rest_0_, ...), custom_call_target="tpu_custom_call" | custom-call | tf_op jit(solution)/shard_map/pick/pallas_call | solution.py:230
  45.8 3.5 %collective-permute-start.14 = (f32[8,3968]{1,0:T(8,128)S(1)}, f32[8,3968]{1,0:T(8,128)S(1)}, u32[]{:S(2)}, u32[]{:S(2)}) collective-permute-start(f32[8,3968]{1,0:T(8,128)S(1)} %get-tuple-element.35), channel_id=1, source_target_pairs={{0,4},{1,5},{2,6},{3,7},{4,0},{5,1},{6,2},{7,3},{8,12},{9,13},{10,... | collective-permute-start | bytes 380936 | tf_op jit(solution)/shard_map/ppermute | solution.py:314
  50.3 2.4 %collective-permute-start.23 = (f32[8,4736]{1,0:T(8,128)S(1)}, f32[8,4736]{1,0:T(8,128)S(1)}, u32[]{:S(2)}, u32[]{:S(2)}) collective-permute-start(f32[8,4736]{1,0:T(8,128)S(1)} %get-tuple-element.41), channel_id=1, source_target_pairs={{0,4},{1,5},{2,6},{3,7},{4,0},{5,1},{6,2},{7,3},{8,12},{9,13},{10,... | collective-permute-start | bytes 454664 | tf_op jit(solution)/shard_map/ppermute | solution.py:314
  53.4 1.4 %collective-permute-start.26 = (f32[8,4736]{1,0:T(8,128)S(1)}, f32[8,4736]{1,0:T(8,128)S(1)}, u32[]{:S(2)}, u32[]{:S(2)}) collective-permute-start(f32[8,4736]{1,0:T(8,128)S(1)} %get-tuple-element.46), channel_id=1, source_target_pairs={{0,2},{1,3},{2,0},{3,1},{4,6},{5,7},{6,4},{7,5},{8,10},{9,11},{10,... | collective-permute-start | bytes 454664 | tf_op jit(solution)/shard_map/ppermute | solution.py:314
  54.8 5.4 %multiply_subtract_fusion = (f32[2,4,16,2880]{3,2,1,0:T(8,128)}, f32[2,4,16,2880]{3,2,1,0:T(8,128)}, f32[2,4,16,2880]{3,2,1,0:T(8,128)}) fusion(f32[2,4,16,2880]{3,2,1,0:T(8,128)} %master.1, f32[]{:T(128)S(1)} %bitcast.2, bf16[2,4,16,2880]{3,2,1,0:T(8,128)(2,1)} %grad.1, f32[2,4,16,2880]{3,2,1,0:T(8,128)} %mone.1, f32[2,4,16,2880]{3,2,1,0:T(8,128)} %mtwo.1), kind=kLoop, calls=%fused_computation.2 | loop fusion | flops 6266880 | bytes 9584644 | tf_op jit(solution)/shard_map/sub | solution.py:51
  60.2 6.8 %collective-permute-done.26.rest_3_ = f32[8,4736]{1,0:T(8,128)S(1)} collective-permute-done((f32[8,4736]{1,0:T(8,128)S(1)}, f32[8,4736]{1,0:T(8,128)S(1)}, u32[]{:S(2)}, u32[]{:S(2)}) %collective-permute-start.26) | collective-permute-done | bytes 151584 | tf_op jit(solution)/shard_map/ppermute | solution.py:314
  68.3 2.6 %collective-permute-done.23.rest_2_ = f32[8,4736]{1,0:T(8,128)S(1)} collective-permute-done((f32[8,4736]{1,0:T(8,128)S(1)}, f32[8,4736]{1,0:T(8,128)S(1)}, u32[]{:S(2)}, u32[]{:S(2)}) %collective-permute-start.23) | collective-permute-done | bytes 151584 | tf_op jit(solution)/shard_map/ppermute | solution.py:314
  70.9 3.1 %collective-permute-done.24.rest_3_ = f32[8,4736]{1,0:T(8,128)S(1)} collective-permute-done((f32[8,4736]{1,0:T(8,128)S(1)}, f32[8,4736]{1,0:T(8,128)S(1)}, u32[]{:S(2)}, u32[]{:S(2)}) %collective-permute-start.24) | collective-permute-done | bytes 151584 | tf_op jit(solution)/shard_map/ppermute | solution.py:314
  (42 shorter events, 6.8 us)
Async XLA Ops:
  5.0 4.5 %collective-permute-start.1 = (f32[1,128]{1,0:T(1,128)S(1)}, f32[1,128]{1,0:T(1,128)S(1)}, u32[]{:S(2)}, u32[]{:S(2)}) collective-permute-start(f32[1,128]{1,0:T(1,128)S(1)} %get-tuple-element.28), channel_id=1, source_target_pairs={{0,4},{1,5},{2,6},{3,7},{4,0},{5,1},{6,2},{7,3},{8,12},{9,13},{10,... | collective-permute-start | bytes 1544 | tf_op jit(solution)/shard_map/ppermute | solution.py:314
  10.9 7.7 %collective-permute-start.6 = (f32[1,128]{1,0:T(1,128)S(1)}, f32[1,128]{1,0:T(1,128)S(1)}, u32[]{:S(2)}, u32[]{:S(2)}) collective-permute-start(f32[1,128]{1,0:T(1,128)S(1)} %add.39), channel_id=1, source_target_pairs={{0,24},{8,16},{16,8},{24,0},{1,25},{9,17},{17,9},{25,1},{2,26},{10... | collective-permute-start | bytes 1544 | tf_op jit(solution)/shard_map/ppermute | solution.py:325
  12.4 6.2 %collective-permute-start.5 = (f32[1,128]{1,0:T(1,128)S(1)}, f32[1,128]{1,0:T(1,128)S(1)}, u32[]{:S(2)}, u32[]{:S(2)}) collective-permute-start(f32[1,128]{1,0:T(1,128)S(1)} %add.39), channel_id=1, source_target_pairs={{0,16},{8,24},{16,0},{24,8},{1,17},{9,25},{17,1},{25,9},{2,18},{10... | collective-permute-start | bytes 1544 | tf_op jit(solution)/shard_map/ppermute | solution.py:325
  13.9 4.8 %collective-permute-start.4 = (f32[1,128]{1,0:T(1,128)S(1)}, f32[1,128]{1,0:T(1,128)S(1)}, u32[]{:S(2)}, u32[]{:S(2)}) collective-permute-start(f32[1,128]{1,0:T(1,128)S(1)} %add.39), channel_id=1, source_target_pairs={{0,8},{8,0},{16,24},{24,16},{1,9},{9,1},{17,25},{25,17},{2,10},{10... | collective-permute-start | bytes 1544 | tf_op jit(solution)/shard_map/ppermute | solution.py:325
  14.4 7.2 %collective-permute-start.7 = (f32[8,4480]{1,0:T(8,128)S(1)}, f32[8,4480]{1,0:T(8,128)S(1)}, u32[]{:S(2)}, u32[]{:S(2)}) collective-permute-start(f32[8,4480]{1,0:T(8,128)S(1)} %get-tuple-element.32), channel_id=1, source_target_pairs={{0,2},{1,3},{2,0},{3,1},{4,6},{5,7},{6,4},{7,5},{8,10},{9,11},{10,... | collective-permute-start | bytes 430088 | tf_op jit(solution)/shard_map/ppermute | solution.py:314
  16.6 11.6 %collective-permute-start.8 = (f32[8,4480]{1,0:T(8,128)S(1)}, f32[8,4480]{1,0:T(8,128)S(1)}, u32[]{:S(2)}, u32[]{:S(2)}) collective-permute-start(f32[8,4480]{1,0:T(8,128)S(1)} %get-tuple-element.33), channel_id=1, source_target_pairs={{0,4},{1,5},{2,6},{3,7},{4,0},{5,1},{6,2},{7,3},{8,12},{9,13},{10,... | collective-permute-start | bytes 430088 | tf_op jit(solution)/shard_map/ppermute | solution.py:314
  18.6 19.5 %collective-permute-start.9 = (f32[8,4480]{1,0:T(8,128)S(1)}, f32[8,4480]{1,0:T(8,128)S(1)}, u32[]{:S(2)}, u32[]{:S(2)}) collective-permute-start(f32[8,4480]{1,0:T(8,128)S(1)} %get-tuple-element.34), channel_id=1, source_target_pairs={{0,6},{1,7},{2,4},{3,5},{4,2},{5,3},{6,0},{7,1},{8,14},{9,15},{10,... | collective-permute-start | bytes 430088 | tf_op jit(solution)/shard_map/ppermute | solution.py:314
  18.6 19.5 %collective-permute-start.10 = (f32[8,4480]{1,0:T(8,128)S(1)}, f32[8,4480]{1,0:T(8,128)S(1)}, u32[]{:S(2)}, u32[]{:S(2)}) collective-permute-start(f32[8,4480]{1,0:T(8,128)S(1)} %get-tuple-element.31.rest_0_), channel_id=1, source_target_pairs={{0,1},{1,0},{2,3},{3,2},{4,5},{5,4},{6,7},{7,6},{8,9},{9,8},{10,11... | collective-permute-start | bytes 430088 | tf_op jit(solution)/shard_map/ppermute | solution.py:331
  19.2 19.4 %collective-permute-start.16 = (f32[8,4736]{1,0:T(8,128)S(1)}, f32[8,4736]{1,0:T(8,128)S(1)}, u32[]{:S(2)}, u32[]{:S(2)}) collective-permute-start(f32[8,4736]{1,0:T(8,128)S(1)} %get-tuple-element.38), channel_id=1, source_target_pairs={{0,2},{1,3},{2,0},{3,1},{4,6},{5,7},{6,4},{7,5},{8,10},{9,11},{10,... | collective-permute-start | bytes 454664 | tf_op jit(solution)/shard_map/ppermute | solution.py:314
  21.6 19.0 %collective-permute-start.17 = (f32[8,4736]{1,0:T(8,128)S(1)}, f32[8,4736]{1,0:T(8,128)S(1)}, u32[]{:S(2)}, u32[]{:S(2)}) collective-permute-start(f32[8,4736]{1,0:T(8,128)S(1)} %get-tuple-element.39), channel_id=1, source_target_pairs={{0,4},{1,5},{2,6},{3,7},{4,0},{5,1},{6,2},{7,3},{8,12},{9,13},{10,... | collective-permute-start | bytes 454664 | tf_op jit(solution)/shard_map/ppermute | solution.py:314
  28.2 15.1 %collective-permute-start.18 = (f32[8,4736]{1,0:T(8,128)S(1)}, f32[8,4736]{1,0:T(8,128)S(1)}, u32[]{:S(2)}, u32[]{:S(2)}) collective-permute-start(f32[8,4736]{1,0:T(8,128)S(1)} %get-tuple-element.40), channel_id=1, source_target_pairs={{0,6},{1,7},{2,4},{3,5},{4,2},{5,3},{6,0},{7,1},{8,14},{9,15},{10,... | collective-permute-start | bytes 454664 | tf_op jit(solution)/shard_map/ppermute | solution.py:314
  38.1 5.3 %collective-permute-start.11 = (f32[8,4480]{1,0:T(8,128)S(1)}, f32[8,4480]{1,0:T(8,128)S(1)}, u32[]{:S(2)}, u32[]{:S(2)}) collective-permute-start(f32[8,4480]{1,0:T(8,128)S(1)} %collective-permute-done.7.rest_1_), channel_id=1, source_target_pairs={{0,1},{1,0},{2,3},{3,2},{4,5},{5,4},{6,7},{7,6},{8,9},{9,8},{10,11... | collective-permute-start | bytes 430088 | tf_op jit(solution)/shard_map/ppermute | solution.py:331
  38.1 5.8 %collective-permute-start.12 = (f32[8,4480]{1,0:T(8,128)S(1)}, f32[8,4480]{1,0:T(8,128)S(1)}, u32[]{:S(2)}, u32[]{:S(2)}) collective-permute-start(f32[8,4480]{1,0:T(8,128)S(1)} %collective-permute-done.8.rest_2_), channel_id=1, source_target_pairs={{0,1},{1,0},{2,3},{3,2},{4,5},{5,4},{6,7},{7,6},{8,9},{9,8},{10,11... | collective-permute-start | bytes 430088 | tf_op jit(solution)/shard_map/ppermute | solution.py:331
  38.6 5.4 %collective-permute-start.13 = (f32[8,4480]{1,0:T(8,128)S(1)}, f32[8,4480]{1,0:T(8,128)S(1)}, u32[]{:S(2)}, u32[]{:S(2)}) collective-permute-start(f32[8,4480]{1,0:T(8,128)S(1)} %collective-permute-done.9.rest_3_), channel_id=1, source_target_pairs={{0,1},{1,0},{2,3},{3,2},{4,5},{5,4},{6,7},{7,6},{8,9},{9,8},{10,11... | collective-permute-start | bytes 430088 | tf_op jit(solution)/shard_map/ppermute | solution.py:331
  40.7 5.2 %collective-permute-start.19 = (f32[8,4736]{1,0:T(8,128)S(1)}, f32[8,4736]{1,0:T(8,128)S(1)}, u32[]{:S(2)}, u32[]{:S(2)}) collective-permute-start(f32[8,4736]{1,0:T(8,128)S(1)} %get-tuple-element.37.rest_0_), channel_id=1, source_target_pairs={{0,1},{1,0},{2,3},{3,2},{4,5},{5,4},{6,7},{7,6},{8,9},{9,8},{10,11... | collective-permute-start | bytes 454664 | tf_op jit(solution)/shard_map/ppermute | solution.py:331
  43.4 5.9 %collective-permute-start.20 = (f32[8,4736]{1,0:T(8,128)S(1)}, f32[8,4736]{1,0:T(8,128)S(1)}, u32[]{:S(2)}, u32[]{:S(2)}) collective-permute-start(f32[8,4736]{1,0:T(8,128)S(1)} %collective-permute-done.16.rest_1_), channel_id=1, source_target_pairs={{0,1},{1,0},{2,3},{3,2},{4,5},{5,4},{6,7},{7,6},{8,9},{9,8},{10,11... | collective-permute-start | bytes 454664 | tf_op jit(solution)/shard_map/ppermute | solution.py:331
  43.4 5.9 %collective-permute-start.21 = (f32[8,4736]{1,0:T(8,128)S(1)}, f32[8,4736]{1,0:T(8,128)S(1)}, u32[]{:S(2)}, u32[]{:S(2)}) collective-permute-start(f32[8,4736]{1,0:T(8,128)S(1)} %collective-permute-done.17.rest_2_), channel_id=1, source_target_pairs={{0,1},{1,0},{2,3},{3,2},{4,5},{5,4},{6,7},{7,6},{8,9},{9,8},{10,11... | collective-permute-start | bytes 454664 | tf_op jit(solution)/shard_map/ppermute | solution.py:331
  43.9 5.4 %collective-permute-start.22 = (f32[8,4736]{1,0:T(8,128)S(1)}, f32[8,4736]{1,0:T(8,128)S(1)}, u32[]{:S(2)}, u32[]{:S(2)}) collective-permute-start(f32[8,4736]{1,0:T(8,128)S(1)} %collective-permute-done.18.rest_3_), channel_id=1, source_target_pairs={{0,1},{1,0},{2,3},{3,2},{4,5},{5,4},{6,7},{7,6},{8,9},{9,8},{10,11... | collective-permute-start | bytes 454664 | tf_op jit(solution)/shard_map/ppermute | solution.py:331
  45.8 7.6 %collective-permute-start.25 = (f32[8,3968]{1,0:T(8,128)}, f32[8,3968]{1,0:T(8,128)S(1)}, u32[]{:S(2)}, u32[]{:S(2)}) collective-permute-start(f32[8,3968]{1,0:T(8,128)} %get-tuple-element.44), channel_id=1, source_target_pairs={{0,2},{1,3},{2,0},{3,1},{4,6},{5,7},{6,4},{7,5},{8,10},{9,11},{10,... | collective-permute-start | bytes 380936 | tf_op jit(solution)/shard_map/ppermute | solution.py:314
  45.8 22.3 %collective-permute-start.14 = (f32[8,3968]{1,0:T(8,128)S(1)}, f32[8,3968]{1,0:T(8,128)S(1)}, u32[]{:S(2)}, u32[]{:S(2)}) collective-permute-start(f32[8,3968]{1,0:T(8,128)S(1)} %get-tuple-element.35), channel_id=1, source_target_pairs={{0,4},{1,5},{2,6},{3,7},{4,0},{5,1},{6,2},{7,3},{8,12},{9,13},{10,... | collective-permute-start | bytes 380936 | tf_op jit(solution)/shard_map/ppermute | solution.py:314
  49.3 19.0 %collective-permute-start.15 = (f32[8,3968]{1,0:T(8,128)S(1)}, f32[8,3968]{1,0:T(8,128)S(1)}, u32[]{:S(2)}, u32[]{:S(2)}) collective-permute-start(f32[8,3968]{1,0:T(8,128)S(1)} %get-tuple-element.36), channel_id=1, source_target_pairs={{0,6},{1,7},{2,4},{3,5},{4,2},{5,3},{6,0},{7,1},{8,14},{9,15},{10,... | collective-permute-start | bytes 380936 | tf_op jit(solution)/shard_map/ppermute | solution.py:314
  50.3 20.6 %collective-permute-start.23 = (f32[8,4736]{1,0:T(8,128)S(1)}, f32[8,4736]{1,0:T(8,128)S(1)}, u32[]{:S(2)}, u32[]{:S(2)}) collective-permute-start(f32[8,4736]{1,0:T(8,128)S(1)} %get-tuple-element.41), channel_id=1, source_target_pairs={{0,4},{1,5},{2,6},{3,7},{4,0},{5,1},{6,2},{7,3},{8,12},{9,13},{10,... | collective-permute-start | bytes 454664 | tf_op jit(solution)/shard_map/ppermute | solution.py:314
  52.7 21.2 %collective-permute-start.24 = (f32[8,4736]{1,0:T(8,128)S(1)}, f32[8,4736]{1,0:T(8,128)S(1)}, u32[]{:S(2)}, u32[]{:S(2)}) collective-permute-start(f32[8,4736]{1,0:T(8,128)S(1)} %get-tuple-element.42), channel_id=1, source_target_pairs={{0,6},{1,7},{2,4},{3,5},{4,2},{5,3},{6,0},{7,1},{8,14},{9,15},{10,... | collective-permute-start | bytes 454664 | tf_op jit(solution)/shard_map/ppermute | solution.py:314
  53.4 13.6 %collective-permute-start.26 = (f32[8,4736]{1,0:T(8,128)S(1)}, f32[8,4736]{1,0:T(8,128)S(1)}, u32[]{:S(2)}, u32[]{:S(2)}) collective-permute-start(f32[8,4736]{1,0:T(8,128)S(1)} %get-tuple-element.46), channel_id=1, source_target_pairs={{0,2},{1,3},{2,0},{3,1},{4,6},{5,7},{6,4},{7,5},{8,10},{9,11},{10,... | collective-permute-start | bytes 454664 | tf_op jit(solution)/shard_map/ppermute | solution.py:314
  (4 other events, 44.4 us)
